TPU v7x, 128 devices: a whole 4x4x4 slice. The times are simulated.
128 devices in a mesh: prow: 8 (over z, y_lo), pcol: 16 (over x, y_hi, core).
Axes of the slice: x: 4, y: 4 (y_hi: 2, y_lo: 2; y = y_hi * 2 + y_lo), z: 4, core: 2. Of those that a mesh axis runs over, the one named last changes fastest.
Arguments:
- ainv_in: float32 [18, 8, 9, 16, 128, 128], P(None, 'prow', None, 'pcol'), as said below
- ufactor: bfloat16 [18, 8, 6, 128, 128], P(None, 'prow'), may hold values from -0.08984375 to 0.08984375
- dinv: float32 [6, 128, 128], replicated, may hold values from -6 to 6
- pattern: int32 [144, 144], replicated, may hold values from 0 to 1, as said below
Outputs:
- ainv_out: float32 [18, 8, 9, 16, 128, 128], P(None, 'prow', None, 'pcol')
Inputs may be any that keep to these rules, and one draw needn't show every extreme that they name: For a column j below 6, pattern[i, j] is 0 for i <= j, 1 at the parent row (the nearest row below j that has a 1, at most 3 below j), and the other 1s of column j lie in rows where the parent's column has a 1; for j at least 6, pattern[i, j] is 1 exactly where i > j. `ainv_in`: a symmetric matrix.
All inputs are finite; a program needn't handle non-finite values.
Results may differ from a plain program's by a relative error of at most 0.0003.
Values may be sent and summed in bfloat16 or wider, within the bound.
No kernel may reach another device: no remote copies, remote signals or barrier semaphores. Data moves between devices by JAX's collectives and lax.ppermute only.
A program may use at most 128 MiB of HBM per device.

v0:
```python
import jax
import jax.numpy as jnp
from jax import lax
from jax.experimental import pallas as pl
from jax.experimental.pallas import tpu as pltpu
from jax.sharding import PartitionSpec as P


F32, BF16 = jnp.float32, jnp.bfloat16
PARTS = ((0, 8), (8, 10))
VMEM = pl.BlockSpec(memory_space=pltpu.VMEM)
SMEM = pl.BlockSpec(memory_space=pltpu.SMEM)
ANY = pl.BlockSpec(memory_space=pl.ANY)


def halves(value):
    high = value.astype(BF16)
    return high, (value - high.astype(F32)).astype(BF16)


def stacked(core, own, other):
    return jnp.concatenate([jnp.where(core > 0, other, own), jnp.where(core > 0, own, other)], axis=0)


def dot(left, right):
    return jnp.dot(left, right, preferred_element_type=F32)


def product_kernel(live, x_ref, u_ref, *refs):
    copy_ref, out_ref = refs[-2:]
    step = pl.program_id(0)
    rows, cols, _, _ = x_ref.shape
    steps = u_ref.shape[1]
    left, high, low = [], [], []
    for r in range(rows):
        wide = []
        for k in range(steps):
            block = u_ref[r, k]
            wide.append(jnp.where(live[step * rows + r, k] > 0, block, jnp.zeros_like(block)))
        left.append(jnp.concatenate(wide, axis=1))
        value = jnp.concatenate([x_ref[r, c] for c in range(cols)], axis=1)
        for c in range(cols):
            copy_ref[r, c] = x_ref[r, c]
        a, b = halves(value)
        high.append(a)
        low.append(b)
    left = jnp.concatenate(left, axis=0).T
    both = jnp.concatenate([left, left], axis=1)
    term = dot(both, jnp.concatenate(high + low, axis=0))
    term = term.reshape(out_ref.shape)

    @pl.when(step == 0)
    def _():
        out_ref[...] = term

    @pl.when(step > 0)
    def _():
        out_ref[...] += term


def products(blocks, lower, live, whole, first, count, rows=2):
    _, cols, width, _ = blocks.shape
    steps = lower.shape[1]
    start = first // rows
    known = [] if whole is None else [whole]
    return pl.pallas_call(
        product_kernel,
        grid_spec=pltpu.PrefetchScalarGridSpec(
            num_scalar_prefetch=1,
            grid=(count // rows,),
            in_specs=[
                pl.BlockSpec((rows, cols, width, width), lambda i, _: (start + i, 0, 0, 0)),
                pl.BlockSpec((rows, steps, width, width), lambda i, _: (start + i, 0, 0, 0)),
            ]
            + [ANY] * len(known),
            out_specs=[
                pl.BlockSpec((rows, cols, width, width), lambda i, _: (start + i, 0, 0, 0)),
                pl.BlockSpec((steps, width, cols * width), lambda i, _: (0, 0, 0)),
            ],
        ),
        out_shape=[
            jax.ShapeDtypeStruct(blocks.shape, F32),
            jax.ShapeDtypeStruct((steps, width, cols * width), F32),
        ],
        input_output_aliases={3: 0} if known else {},
        cost_estimate=pl.CostEstimate(
            flops=4 * count * cols * steps * width**3, bytes_accessed=8 * count * cols * width**2, transcendentals=0
        ),
        name="products",
    )(live[first : first + count], blocks, lower, *known)


def eliminate_kernel(take, live, *refs):
    *part_refs, u_ref, v_ref, up_ref, down_ref, up2_ref, down2_ref, own_ref, w_ref = refs
    steps = w_ref.shape[0]
    high, low = [], []
    for k in reversed(range(steps)):
        total = part_refs[0][k]
        for ref in part_refs[1:]:
            total = total + ref[k]
        if high:
            blocks = []
            for j in range(k + 1, steps):
                block = stacked(take[8], u_ref[j, k], v_ref[j, k])
                blocks.append(jnp.where(live[j, k] > 0, block, jnp.zeros_like(block)).T)
            left = jnp.concatenate(blocks + blocks, axis=1)
            total = total + dot(left, jnp.concatenate(high[::-1] + low[::-1], axis=0))
        total = -total
        w_ref[k] = total
        a, b = halves(total)
        high.append(a)
        low.append(b)
    places = [up_ref.at[0], up_ref.at[1], down_ref.at[0], down_ref.at[1], up2_ref, down2_ref, own_ref.at[0], own_ref.at[1]]
    for n, place in enumerate(places):
        place[...] = w_ref[take[n]]


def eliminate(parts, corner, live, take):
    _, width, wide = parts[0].shape
    one = jax.ShapeDtypeStruct((width, wide), F32)
    two = jax.ShapeDtypeStruct((2, width, wide), F32)
    return pl.pallas_call(
        eliminate_kernel,
        in_specs=[SMEM, SMEM] + [VMEM] * (len(parts) + 2),
        out_specs=[VMEM] * 5,
        out_shape=[two, two, one, one, two],
        scratch_shapes=[pltpu.VMEM(parts[0].shape, F32)],
        cost_estimate=pl.CostEstimate(flops=1000 * parts[0].size, bytes_accessed=20 * parts[0].size, transcendentals=0),
        name="eliminate",
    )(take, live, *parts, *corner)


def column_kernel(info, live, row_ref, near_ref, far_ref, out_ref):
    cols, steps, width, _ = near_ref.shape
    total = None
    for c in range(0, cols, 2):
        count = min(2, cols - c)
        left = jnp.concatenate(halves(row_ref[:, pl.ds(c * width, count * width)]), axis=0)
        right = []
        for r in range(c, c + count):
            wide = []
            for k in range(steps):
                block = jnp.where(info[0] > 0, near_ref[r, k], far_ref[r, k])
                wide.append(jnp.where(live[r, k] > 0, block, jnp.zeros_like(block)))
            right.append(jnp.concatenate(wide, axis=1))
        term = dot(left, jnp.concatenate(right, axis=0))
        total = term if total is None else total + term
    out_ref[...] = total[:width] + total[width:]


def column_products(info, live, row, near, far):
    cols, steps, width, _ = near.shape
    return pl.pallas_call(
        column_kernel,
        in_specs=[SMEM, SMEM, VMEM, VMEM, VMEM],
        out_specs=VMEM,
        out_shape=jax.ShapeDtypeStruct((width, steps * width), F32),
        cost_estimate=pl.CostEstimate(flops=4 * cols * steps * width**3, bytes_accessed=6 * 10**6, transcendentals=0),
        name="column",
    )(info, live, row, near, far)


def corner_kernel(info, live, g_ref, h_ref, u_ref, v_ref, dinv_ref, out_ref, x_ref):
    steps, width, _ = dinv_ref.shape
    for k in reversed(range(steps)):
        here = pl.ds(k * width, width)
        later = steps - 1 - k
        if later:
            right = []
            for j in range(k + 1, steps):
                block = stacked(info[2], u_ref[j, k], v_ref[j, k])
                right.append(jnp.where(live[j, k] > 0, block, jnp.zeros_like(block)))
            right = jnp.concatenate(right, axis=0)
            both = jnp.concatenate([right, right], axis=0)
            rest = pl.ds((k + 1) * width, later * width)
            known = jnp.concatenate(halves(x_ref[rest, rest]), axis=1)
            value = dot(known, both)
            turned = []
            for i in range(k + 1, steps):
                at = (i - k - 1) * width
                block = -(value[at : at + width] + stacked(info[2], g_ref[i, :, here], h_ref[i, :, here]))
                block = jnp.where(live[i, k] > 0, block, jnp.zeros_like(block))
                x_ref[pl.ds(i * width, width), here] = block
                turned.append(block.T)
            turned = jnp.concatenate(turned, axis=1)
            x_ref[here, rest] = turned
            tail = dot(jnp.concatenate(halves(turned), axis=1), both)
            x_ref[here, here] = dinv_ref[k].T - stacked(info[2], g_ref[k, :, here], h_ref[k, :, here]) - tail
        else:
            x_ref[here, here] = dinv_ref[k].T - stacked(info[2], g_ref[k, :, here], h_ref[k, :, here])
    for k in range(steps):
        for j in range(steps):

            @pl.when((info[0] == k) & (info[1] == j))
            def _():
                out_ref[...] = x_ref[pl.ds(k * width, width), pl.ds(j * width, width)]


def corner_blocks(info, live, sums, corner, dinv):
    steps, width, _ = dinv.shape
    return pl.pallas_call(
        corner_kernel,
        in_specs=[SMEM, SMEM] + [VMEM] * 5,
        out_specs=VMEM,
        out_shape=jax.ShapeDtypeStruct((width, width), F32),
        scratch_shapes=[pltpu.VMEM((steps * width, steps * width), F32)],
        cost_estimate=pl.CostEstimate(flops=10**9, bytes_accessed=10**6, transcendentals=0),
        name="corner",
    )(info, live, *sums, *corner, dinv)


def patch_kernel(info, *refs):
    *value_refs, _, out_ref, turned_ref, sem_ref = refs
    row_blocks, cols, width, _ = out_ref.shape
    has_row, has_col, row_first, col_first = info[0], info[1], info[2], info[3]
    rows, columns = [], []
    for row_ref, even_ref, odd_ref in zip(value_refs[::3], value_refs[1::3], value_refs[2::3]):
        for c in range(row_ref.shape[1] // width):
            rows.append((row_ref, pl.ds(c * width, width)))
            columns.append((even_ref, pl.ds(c * width, width)))
            columns.append((odd_ref, pl.ds(c * width, width)))

    def row_copy(c):
        return pltpu.make_async_copy(rows[c][0].at[:, rows[c][1]], out_ref.at[0, c], sem_ref.at[c])

    def col_copy(a):
        return pltpu.make_async_copy(turned_ref.at[a], out_ref.at[a, 0], sem_ref.at[cols + a])

    @pl.when(has_row > 0)
    def _():
        for c in range(1, cols):
            row_copy(c).start()

    @pl.when(row_first > 0)
    def _():
        row_copy(0).start()

    @pl.when(has_col > 0)
    def _():
        for a in range(row_blocks):
            turned_ref[a] = columns[a][0][:, columns[a][1]].T
        for a in range(1, row_blocks):
            col_copy(a).start()
        for a in range(1, row_blocks):
            col_copy(a).wait()

    @pl.when(col_first > 0)
    def _():
        col_copy(0).start()
        col_copy(0).wait()

    @pl.when(has_row > 0)
    def _():
        for c in range(1, cols):
            row_copy(c).wait()

    @pl.when(row_first > 0)
    def _():
        row_copy(0).wait()


def patch(info, values, whole):
    row_blocks, cols, width, _ = whole.shape
    return pl.pallas_call(
        patch_kernel,
        in_specs=[SMEM] + [VMEM] * len(values) + [ANY],
        out_specs=ANY,
        out_shape=jax.ShapeDtypeStruct(whole.shape, F32),
        scratch_shapes=[pltpu.VMEM((row_blocks, width, width), F32), pltpu.SemaphoreType.DMA((row_blocks + cols,))],
        input_output_aliases={1 + len(values): 0},
        cost_estimate=pl.CostEstimate(flops=10**8, bytes_accessed=4 * 10**6, transcendentals=0),
        name="patch",
    )(info, *values, whole)


def first_kernel(info, block_ref, _, out_ref, sem_ref):
    @pl.when(info[0] > 0)
    def _():
        copy = pltpu.make_async_copy(block_ref, out_ref.at[0, 0], sem_ref)
        copy.start()
        copy.wait()


def patch_first(info, block, whole):
    return pl.pallas_call(
        first_kernel,
        in_specs=[SMEM, VMEM, ANY],
        out_specs=ANY,
        out_shape=jax.ShapeDtypeStruct(whole.shape, F32),
        scratch_shapes=[pltpu.SemaphoreType.DMA],
        input_output_aliases={2: 0},
        name="patch_first",
    )(info, block, whole)


def per_device(ainv_in, ufactor, dinv, pattern):
    row_blocks, _, cols, _, width, _ = ainv_in.shape
    steps = dinv.shape[0]
    n_row, n_col = lax.axis_size("prow"), lax.axis_size("pcol")
    blocks = ainv_in.reshape(row_blocks, cols, width, width)
    lower = ufactor.reshape(row_blocks, steps, width, width)
    p, q = lax.axis_index("prow"), lax.axis_index("pcol")
    z, y, core = p // 2, p % 2, q % 2
    n_z = n_row // 2
    row_ids = jnp.arange(row_blocks, dtype=jnp.int32) * n_row + p
    col_ids = jnp.arange(cols, dtype=jnp.int32) * n_col + q

    flags = pattern[:, :steps]
    mine = lax.dynamic_index_in_dim(flags.reshape(row_blocks, n_row, steps), p, 1, keepdims=False)
    live = ((mine > 0) & (row_ids >= steps)[:, None]).astype(jnp.int32)
    live_corner = flags[:steps]
    mine = lax.dynamic_index_in_dim(flags.reshape(cols, n_col, steps), q, 1, keepdims=False)
    live_cols = ((mine > 0) & (col_ids >= steps)[:, None]).astype(jnp.int32)
    row_live = lax.dynamic_index_in_dim(live_cols, jnp.minimum(p, steps - 1), 1, keepdims=False) > 0

    def at(zz, yy):
        return zz % n_z * 2 + yy

    flip_y = [(d, d ^ 1) for d in range(n_row)]
    flip_z = [(d, d ^ 2) for d in range(n_row)]
    mirror = [(d, at(n_z - 1 - d // 2, d % 2)) for d in range(n_row)]
    flip_core = [(d, d ^ 1) for d in range(n_col)]

    half = width // 2
    mine = lax.dynamic_slice_in_dim(lower[0], core * half, half, axis=1)

    def join(bit, own, other):
        return jnp.where(bit == 0, jnp.concatenate([own, other]), jnp.concatenate([other, own]))

    def ring(shift):
        return [(at(zz, yy), at(zz + shift, yy)) for zz in range(n_z) for yy in range(2)]

    pair = join(y, mine[None], lax.ppermute(mine[None], "prow", flip_y))
    moved = [pair] + [lax.ppermute(pair, "prow", ring(shift)) for shift in (1, 2, 3)]
    corner = []
    for t in range(steps // 2):
        away = (z - t) % n_z
        corner.append(jnp.where(away == 0, moved[0], jnp.where(away == 1, moved[1], jnp.where(away == 2, moved[2], moved[3]))))
    corner = jnp.concatenate(corner)
    corner = corner, lax.ppermute(corner, "pcol", flip_core)

    n_dest = steps // 2

    both, grid = ("prow", "pcol"), [(x, h, c) for x in range(n_col // 4) for h in range(2) for c in range(2)]

    def device(x, h, c, zz, yy):
        return at(zz, yy) * n_col + x * 4 + h * 2 + c

    def source(x, h):
        return x % 2 * 2 + h

    mine = lower.reshape(cols, 2, steps, width, width)
    mine = lax.dynamic_index_in_dim(mine, q // n_row, 1, keepdims=False)
    ahead = [(device(x, h, c, source(x, h), c), device(x, h, c, source(x, h) + 1, c)) for x, h, c in grid]
    behind = [(device(x, h, 1 - c, source(x, h), c), device(x, h, c, source(x, h) + 3, c)) for x, h, c in grid]
    from_behind = lax.ppermute(mine, both, ahead)
    from_ahead = lax.ppermute(mine, both, behind)
    cut = (cols + 1) // 2
    ahead = [(device(x, h, c, source(x, h) + 1, c), device(x, h, c, source(x, h) + 2, c)) for x, h, c in grid]
    behind = [(device(x, h, c, source(x, h) + 3, c), device(x, h, c, source(x, h) + 2, c)) for x, h, c in grid]
    opposite = jnp.concatenate(
        [lax.ppermute(from_behind[:cut], both, ahead), lax.ppermute(from_ahead[cut:], both, behind)]
    )
    apart = (z - (q // 4 % 2 * 2 + q // 2 % 2)) % n_z
    near_u = jnp.where(
        apart == 0, mine, jnp.where(apart == 1, from_behind, jnp.where(apart == 3, from_ahead, opposite))
    )
    across = [
        (device(x, h, c, zz, c), device(x, h, c, zz, 1 - c)) for x, h, c in grid for zz in range(n_dest)
    ]
    far_u = lax.ppermute(near_u, both, across)

    whole, parts = None, []
    for first, count in PARTS:
        whole, part = products(blocks, lower, live, whole, first, count)
        parts.append(part)

    def near(shift):
        return [(s, d) for s, d in ring(shift) if d < steps]

    def slot(zz, par):
        return jnp.minimum(zz % n_z, n_dest - 1) * 2 + par

    take = [slot(z + 2, 0), slot(z + 1, 1), slot(z + 2, 1), slot(z - 1, 0)]
    take += [slot(z + 1, 0), slot(z - 1, 1), slot(z, 0), slot(z, 1), core]
    up, down, up2, down2, own = eliminate(parts, corner, live_corner, jnp.stack(take).astype(jnp.int32))
    up = lax.ppermute(up, "prow", ring(1))
    down = lax.ppermute(down, "prow", ring(-1))
    up2 = lax.ppermute(up2 + up[0], "prow", near(1))
    down2 = lax.ppermute(down2 + down[0], "prow", near(-1))
    even, odd = own[0] + down[1] + up2, own[1] + up[1] + down2
    keep, give = jnp.where(y == 0, even, odd), jnp.where(y == 0, odd, even)
    full = keep + lax.ppermute(give, "prow", [(d, d ^ 1) for d in range(steps)])
    mask = jnp.broadcast_to(row_live[:, None], (cols, width)).reshape(1, cols * width)
    row = jnp.where(mask, full, jnp.zeros_like(full))

    def route(group):
        return [(k * n_col + d + group * n_row, d * n_col + k) for k in range(steps) for d in range(n_row)]

    values = [row, lax.ppermute(row, both, route(0)), lax.ppermute(row, both, route(1))]

    sums = column_products((y == core).astype(jnp.int32).reshape(1), live_cols, row, near_u, far_u)
    parts = sums.reshape(2, half, steps * width)
    keep = lax.dynamic_index_in_dim(parts, core, 0, keepdims=False)
    give = lax.dynamic_index_in_dim(parts, 1 - core, 0, keepdims=False)
    got = keep + lax.ppermute(give, "pcol", flip_core)
    got = got + lax.ppermute(got, "pcol", [(d, d ^ 2) for d in range(n_col)])
    got = got + lax.ppermute(got, "pcol", [(d, d ^ 4) for d in range(n_col)])
    got = got + lax.ppermute(got, "pcol", [(d, (n_col // 4 - 1 - d // 4) * 4 + d % 4) for d in range(n_col)])

    def here(perm):
        return [(s * n_col + d, t * n_col + d) for s, t in perm for d in range(steps)]

    got = got[None]
    got = join(y, got, lax.ppermute(got, both, here(flip_y)))
    got = join(z % 2, got, lax.ppermute(got, both, here(flip_z)))
    last = steps - 4
    rise = lax.ppermute(got, both, here([(s, t) for s, t in mirror if s < 4]))
    fall = lax.ppermute(got[:last], both, here([(s, t) for s, t in mirror if s >= 4]))
    upper = z // 2 == 1
    got = jnp.concatenate([jnp.where(upper, rise, got), jnp.where(upper, got[:last], fall)])
    other = lax.ppermute(got, "pcol", [(d, d ^ 1) for d in range(steps)])
    sums = got, other

    has_row, has_col = p < steps, q < steps
    info = jnp.stack([has_row, has_col, has_row & ~has_col, has_col & ~has_row]).astype(jnp.int32)
    whole = patch(info, values, whole)
    info = jnp.stack([p, q, core]).astype(jnp.int32)
    block = corner_blocks(info, live_corner, sums, corner, dinv)
    info = jnp.stack([has_row & has_col]).astype(jnp.int32)
    whole = patch_first(info, block, whole)
    return whole.reshape(ainv_in.shape)


def solution(mesh):
    placed = (
        P(None, "prow", None, "pcol", None, None),
        P(None, "prow", None, None, None),
        P(),
        P(),
    )
    return jax.shard_map(
        per_device,
        mesh=mesh,
        in_specs=placed,
        out_specs=P(None, "prow", None, "pcol", None, None),
        check_vma=False,
    )
```

profile of v0, /device:TPU:33, one launch (start us, length us, event | category | flops | bytes accessed | tf_op | source)
XLA Modules:
  0.0 293.8 jit_solution(5986655728596673521)
XLA Ops:
  0.0 2.9 dynamic-slice_bitcast_fusion
  3.7 2.0 collective-permute-start.11
  6.7 1.9 collective-permute-start
  9.1 1.7 collective-permute-done
  11.9 6.6 %collective-permute-start.2 = (bf16[2,6,64,128]{3,2,1,0:T(8,128)(2,1)S(1)}, bf16[2,6,64,128]{3,2,1,0:T(8,128)(2,1)S(1)}, u32[]{:S(2)}, u32[]{:S(2)}) collective-permute-start(bf16[2,6,64,128]{3,2,1,0:T(8,128)(2,1)S(1)} %maximum_select_fusion.3), channel_id=1, source_target_pairs={{0,64},{16,80},{32,96},{48,112},{64,0},{80,16},{96,32},{112,48},{1... | collective-permute-start | bytes 589832 | tf_op jit(solution)/shard_map/ppermute | solution.py:334
  19.2 3.0 %collective-permute-done.1 = bf16[2,6,64,128]{3,2,1,0:T(8,128)(2,1)S(1)} collective-permute-done((bf16[2,6,64,128]{3,2,1,0:T(8,128)(2,1)S(1)}, bf16[2,6,64,128]{3,2,1,0:T(8,128)(2,1)S(1)}, u32[]{:S(2)}, u32[]{:S(2)}) %collective-permute-start.1) | collective-permute-done | bytes 196640 | tf_op jit(solution)/shard_map/ppermute | solution.py:334
  23.2 4.9 %collective-permute-done.3 = bf16[2,6,64,128]{3,2,1,0:T(8,128)(2,1)S(1)} collective-permute-done((bf16[2,6,64,128]{3,2,1,0:T(8,128)(2,1)S(1)}, bf16[2,6,64,128]{3,2,1,0:T(8,128)(2,1)S(1)}, u32[]{:S(2)}, u32[]{:S(2)}) %collective-permute-start.3) | collective-permute-done | bytes 196640 | tf_op jit(solution)/shard_map/ppermute | solution.py:334
  28.3 6.5 %collective-permute-start.4 = (bf16[6,6,64,128]{3,2,1,0:T(8,128)(2,1)S(1)}, bf16[6,6,64,128]{3,2,1,0:T(8,128)(2,1)S(1)}, u32[]{:S(2)}, u32[]{:S(2)}) collective-permute-start(bf16[6,6,64,128]{3,2,1,0:T(8,128)(2,1)S(1)} %pad_maximum_fusion.1.refs_2_.u_ref), channel_id=1, source_target_pairs={{0,1},{1,0},{2,3},{3,2},{4,5},{5,4},{6,7},{7,6},{8,9},{9,8},{10,11... | collective-permute-start | bytes 1769480 | tf_op jit(solution)/shard_map/ppermute | solution.py:340
  34.8 11.0 %products.2 = (f32[18,9,128,128]{3,2,1,0:T(8,128)}, f32[6,128,1152]{2,1,0:T(8,128)}) custom-call(s32[8,6]{1,0:T(8,128)} %slice.59.live, f32[18,9,128,128]{3,2,1,0:T(8,128)} %bitcast.76, bf16[18,6,128,128]{3,2,1,0:T(8,128)(2,1)} %bitcast.79), custom_call_target="tpu_custom_call" | custom-call | flops 3623878656 | bytes 9437184 | tf_op jit(solution)/shard_map/products/pallas_call | solution.py:66
  47.6 12.7 %products.3 = (f32[18,9,128,128]{3,2,1,0:T(8,128)}, f32[6,128,1152]{2,1,0:T(8,128)}) custom-call(s32[10,6]{1,0:T(8,128)} %slice.60.live, f32[18,9,128,128]{3,2,1,0:T(8,128)} %bitcast.77, bf16[18,6,128,128]{3,2,1,0:T(8,128)(2,1)} %bitcast.80, f32[18,9,128,128]{3,2,1,0:T(8,128)} %get-tuple-element.15.refs_0_), custom_call_target="tpu_custom_call", output_to_operand_aliasing={{0}: (3, {})} | custom-call | flops 4529848320 | bytes 11796480 | tf_op jit(solution)/shard_map/products/pallas_call | solution.py:66
  61.1 7.4 %eliminate.1 = (f32[2,128,1152]{2,1,0:T(8,128)}, f32[2,128,1152]{2,1,0:T(8,128)}, f32[128,1152]{1,0:T(8,128)}, f32[128,1152]{1,0:T(8,128)}, f32[2,128,1152]{2,1,0:T(8,128)}) custom-call(s32[9]{0:T(128)} %stack.68.take, s32[6,6]{1,0:T(8,128)} %slice.45.live, f32[6,128,1152]{2,1,0:T(8,128)} %get-tuple-element.14.refs_0_, ...), custom_call_target="tpu_custom_call" | custom-call | flops 884736000 | bytes 17694720 | tf_op jit(solution)/shard_map/eliminate/pallas_call | solution.py:122
  68.5 3.3 %collective-permute-start.6 = (f32[2,128,1152]{2,1,0:T(8,128)}, f32[2,128,1152]{2,1,0:T(8,128)S(1)}, u32[]{:S(2)}, u32[]{:S(2)}) collective-permute-start(f32[2,128,1152]{2,1,0:T(8,128)} %get-tuple-element.20), channel_id=1, source_target_pairs={{0,32},{16,48},{32,64},{48,80},{64,96},{80,112},{96,0},{112,16},{1... | collective-permute-start | bytes 3538952 | tf_op jit(solution)/shard_map/ppermute | solution.py:387
  71.9 2.2 slice.66
  74.1 1.7 collective-permute-start.13
  75.8 1.1 slice.65
  76.9 1.6 collective-permute-start.12
  78.6 19.4 %collective-permute-done.6 = f32[2,128,1152]{2,1,0:T(8,128)S(1)} collective-permute-done((f32[2,128,1152]{2,1,0:T(8,128)}, f32[2,128,1152]{2,1,0:T(8,128)S(1)}, u32[]{:S(2)}, u32[]{:S(2)}) %collective-permute-start.6) | collective-permute-done | bytes 1179680 | tf_op jit(solution)/shard_map/ppermute | solution.py:387
  98.8 3.8 %collective-permute-start.7 = (f32[128,1152]{1,0:T(8,128)}, f32[128,1152]{1,0:T(8,128)}, u32[]{:S(2)}, u32[]{:S(2)}) collective-permute-start(f32[128,1152]{1,0:T(8,128)} %fusion.5), channel_id=1, source_target_pairs={{0,32},{16,48},{32,64},{48,80},{96,0},{112,16},{1,33},{17,49},{33,... | collective-permute-start | bytes 1769480 | tf_op jit(solution)/shard_map/ppermute | solution.py:389
  104.6 3.4 %collective-permute-start.8 = (f32[128,1152]{1,0:T(8,128)}, f32[128,1152]{1,0:T(8,128)}, u32[]{:S(2)}, u32[]{:S(2)}) collective-permute-start(f32[128,1152]{1,0:T(8,128)} %fusion.2), channel_id=1, source_target_pairs={{32,0},{48,16},{64,32},{80,48},{96,64},{112,80},{33,1},{49,17},{65... | collective-permute-start | bytes 1769480 | tf_op jit(solution)/shard_map/ppermute | solution.py:390
  108.7 3.7 %fusion.1.near_ref = bf16[9,6,128,128]{3,2,1,0:T(8,128)(2,1)} fusion(bf16[9,6,128,128]{3,2,1,0:T(8,128)(2,1)} %copy-done.6, bf16[9,6,128,128]{3,2,1,0:T(8,128)(2,1)} %collective-permute-done.11, bf16[4,6,128,128]{3,2,1,0:T(8,128)(2,1)} %collective-permute-done.13, bf16[5,6,128,128]{3,2,1,0:T(8,128)(2,1)} %collective-permute-done.12, pred[]{:T(512)S(6)} %eq.84, ...), kind=kLoop, calls=%fused_computation.2 | loop fusion | flops 3538944 | bytes 8847367 | tf_op jit(solution)/shard_map/jit(_where)/select_n | solution.py:365
  112.4 1.3 collective-permute-start.14
  113.7 3.4 %collective-permute-done.7 = f32[128,1152]{1,0:T(8,128)} collective-permute-done((f32[128,1152]{1,0:T(8,128)}, f32[128,1152]{1,0:T(8,128)}, u32[]{:S(2)}, u32[]{:S(2)}) %collective-permute-start.7) | collective-permute-done | bytes 589856 | tf_op jit(solution)/shard_map/ppermute | solution.py:389
  117.1 2.9 %collective-permute-done.8 = f32[128,1152]{1,0:T(8,128)} collective-permute-done((f32[128,1152]{1,0:T(8,128)}, f32[128,1152]{1,0:T(8,128)}, u32[]{:S(2)}, u32[]{:S(2)}) %collective-permute-start.8) | collective-permute-done | bytes 589856 | tf_op jit(solution)/shard_map/ppermute | solution.py:390
  120.1 2.5 broadcast_select_fusion.1
  122.6 4.7 %collective-permute-start.9 = (f32[128,1152]{1,0:T(8,128)}, f32[128,1152]{1,0:T(8,128)}, u32[]{:S(2)}, u32[]{:S(2)}) collective-permute-start(f32[128,1152]{1,0:T(8,128)} %broadcast_select_fusion.1), channel_id=1, source_target_pairs={{0,16},{16,0},{32,48},{48,32},{64,80},{80,64},{1,17},{17,1},{33,49... | collective-permute-start | bytes 1769480 | tf_op jit(solution)/shard_map/ppermute | solution.py:393
  128.0 20.9 %collective-permute-done.9 = f32[128,1152]{1,0:T(8,128)} collective-permute-done((f32[128,1152]{1,0:T(8,128)}, f32[128,1152]{1,0:T(8,128)}, u32[]{:S(2)}, u32[]{:S(2)}) %collective-permute-start.9) | collective-permute-done | bytes 589856 | tf_op jit(solution)/shard_map/ppermute | solution.py:393
  149.0 2.4 add_select_fusion.row_ref.refs_0_
  151.4 3.7 %column.1 = f32[128,768]{1,0:T(8,128)} custom-call(s32[1]{0:T(128)} %bitcast.4.info, s32[9,6]{1,0:T(8,128)} %copy-done.20, f32[128,1152]{1,0:T(8,128)} %add_select_fusion.row_ref.refs_0_, bf16[9,6,128,128]{3,2,1,0:T(8,128)(2,1)} %fusion.1.near_ref, bf16[9,6,128,128]{3,2,1,0:T(8,128)(2,1)} %collective-permute-done.14.far_ref), custom_call_target="tpu_custom_call" | custom-call | flops 452984832 | bytes 6000000 | tf_op jit(solution)/shard_map/column/pallas_call | solution.py:153
  156.1 2.8 collective-permute-start.15
  161.1 7.6 %collective-permute-done.16 = f32[64,768]{1,0:T(8,128)S(1)} collective-permute-done((f32[64,768]{1,0:T(8,128)S(1)}, f32[64,768]{1,0:T(8,128)S(1)}, u32[]{:S(2)}, u32[]{:S(2)}) %collective-permute-start.16) | collective-permute-done | bytes 196640 | tf_op jit(solution)/shard_map/ppermute | solution.py:407
  169.4 4.7 %collective-permute-done.17 = f32[64,768]{1,0:T(8,128)S(1)} collective-permute-done((f32[64,768]{1,0:T(8,128)S(1)}, f32[64,768]{1,0:T(8,128)S(1)}, u32[]{:S(2)}, u32[]{:S(2)}) %collective-permute-start.17) | collective-permute-done | bytes 196640 | tf_op jit(solution)/shard_map/ppermute | solution.py:408
  174.1 1.9 collective-permute-start.18
  176.0 3.9 %collective-permute-done.18 = f32[64,768]{1,0:T(8,128)S(1)} collective-permute-done((f32[64,768]{1,0:T(8,128)S(1)}, f32[64,768]{1,0:T(8,128)S(1)}, u32[]{:S(2)}, u32[]{:S(2)}) %collective-permute-start.18) | collective-permute-done | bytes 196640 | tf_op jit(solution)/shard_map/ppermute | solution.py:409
  179.9 4.1 %collective-permute-start.19 = (f32[1,64,768]{2,1,0:T(8,128)S(1)}, f32[1,64,768]{2,1,0:T(8,128)S(1)}, u32[]{:S(2)}, u32[]{:S(2)}) collective-permute-start(f32[1,64,768]{2,1,0:T(8,128)S(1)} %add_bitcast_fusion), channel_id=1, source_target_pairs={{0,16},{1,17},{2,18},{3,19},{4,20},{5,21},{16,0},{17,1},{18,2},{19... | collective-permute-start | bytes 589832 | tf_op jit(solution)/shard_map/ppermute | solution.py:415
  184.0 3.0 %collective-permute-done.19 = f32[1,64,768]{2,1,0:T(8,128)S(1)} collective-permute-done((f32[1,64,768]{2,1,0:T(8,128)S(1)}, f32[1,64,768]{2,1,0:T(8,128)S(1)}, u32[]{:S(2)}, u32[]{:S(2)}) %collective-permute-start.19) | collective-permute-done | bytes 196640 | tf_op jit(solution)/shard_map/ppermute | solution.py:415
  187.1 5.8 %collective-permute-start.20 = (f32[2,64,768]{2,1,0:T(8,128)S(1)}, f32[2,64,768]{2,1,0:T(8,128)S(1)}, u32[]{:S(2)}, u32[]{:S(2)}) collective-permute-start(f32[2,64,768]{2,1,0:T(8,128)S(1)} %maximum_select_fusion.2), channel_id=1, source_target_pairs={{0,32},{1,33},{2,34},{3,35},{4,36},{5,37},{16,48},{17,49},{18,50},... | collective-permute-start | bytes 1179656 | tf_op jit(solution)/shard_map/ppermute | solution.py:416
  192.9 5.6 %collective-permute-done.20 = f32[2,64,768]{2,1,0:T(8,128)S(1)} collective-permute-done((f32[2,64,768]{2,1,0:T(8,128)S(1)}, f32[2,64,768]{2,1,0:T(8,128)S(1)}, u32[]{:S(2)}, u32[]{:S(2)}) %collective-permute-start.20) | collective-permute-done | bytes 393248 | tf_op jit(solution)/shard_map/ppermute | solution.py:416
  198.6 1.3 collective-permute-start.21
  200.0 1.3 collective-permute-start.22
  201.3 7.2 %collective-permute-done.22 = f32[2,64,768]{2,1,0:T(8,128)S(1)} collective-permute-done((f32[2,64,768]{2,1,0:T(8,128)S(1)}, f32[2,64,768]{2,1,0:T(8,128)S(1)}, u32[]{:S(2)}, u32[]{:S(2)}) %collective-permute-start.22) | collective-permute-done | bytes 393248 | tf_op jit(solution)/shard_map/ppermute | solution.py:419
  208.6 3.6 %collective-permute-done.21 = f32[4,64,768]{2,1,0:T(8,128)S(1)} collective-permute-done((f32[4,64,768]{2,1,0:T(8,128)S(1)}, f32[4,64,768]{2,1,0:T(8,128)S(1)}, u32[]{:S(2)}, u32[]{:S(2)}) %collective-permute-start.21) | collective-permute-done | bytes 786464 | tf_op jit(solution)/shard_map/ppermute | solution.py:418
  212.4 7.5 %collective-permute-start.23 = (f32[6,64,768]{2,1,0:T(8,128)S(1)}, f32[6,64,768]{2,1,0:T(8,128)S(1)}, u32[]{:S(2)}, u32[]{:S(2)}) collective-permute-start(f32[6,64,768]{2,1,0:T(8,128)S(1)} %pad_maximum_fusion.g_ref), channel_id=1, source_target_pairs={{0,1},{1,0},{2,3},{3,2},{4,5},{5,4},{16,17},{17,16},{18,19},{19,18... | collective-permute-start | bytes 3538952 | tf_op jit(solution)/shard_map/ppermute | solution.py:422
  219.9 4.8 %collective-permute-start.24 = (f32[128,1152]{1,0:T(8,128)S(1)}, f32[128,1152]{1,0:T(8,128)S(1)}, u32[]{:S(2)}, u32[]{:S(2)}) collective-permute-start(f32[128,1152]{1,0:T(8,128)S(1)} %copy-done.1), channel_id=1, source_target_pairs={{0,0},{1,16},{2,32},{3,48},{4,64},{5,80},{6,96},{7,112},{16,1},{17... | collective-permute-start | bytes 1769480 | tf_op jit(solution)/shard_map/ppermute | solution.py:400
  224.8 1.3 collective-permute-start.25
  227.3 53.9 %collective-permute-done.24.refs_1_ = f32[128,1152]{1,0:T(8,128)S(1)} collective-permute-done((f32[128,1152]{1,0:T(8,128)S(1)}, f32[128,1152]{1,0:T(8,128)S(1)}, u32[]{:S(2)}, u32[]{:S(2)}) %collective-permute-start.24) | collective-permute-done | bytes 589856 | tf_op jit(solution)/shard_map/ppermute | solution.py:400
  282.1 3.0 %patch.1._ = f32[18,9,128,128]{3,2,1,0:T(8,128)} custom-call(s32[4]{0:T(128)} %add_convert_fusion.info, f32[128,1152]{1,0:T(8,128)} %add_select_fusion.row_ref.refs_0_, f32[128,1152]{1,0:T(8,128)} %copy-done.15, f32[128,1152]{1,0:T(8,128)} %collective-permute-done.25.refs_2_, ...), custom_call_target="tpu_custom_call", output_to_operand_aliasing={{}: (4, {})} | custom-call | flops 100000000 | bytes 4000000 | tf_op jit(solution)/shard_map/patch/pallas_call | solution.py:264
  286.2 6.0 %corner.1.block_ref = f32[128,128]{1,0:T(8,128)} custom-call(s32[3]{0:T(128)} %pad_add_fusion.info, s32[6,6]{1,0:T(8,128)} %slice.45.live, f32[6,64,768]{2,1,0:T(8,128)} %copy-done.3, f32[6,64,768]{2,1,0:T(8,128)} %copy-done.14, bf16[6,6,64,128]{3,2,1,0:T(8,128)(2,1)} %copy-done.2, bf16[6,6,64,128]{3,2,1,0:T(8,128)(2,1)} %copy-done.13, f32[6,128,128]{2,1,0:T(8,128)} %dinv_ref.1), custom_call_target="tpu_custom_call" | custom-call | flops 1000000000 | bytes 1000000 | tf_op jit(solution)/shard_map/corner/pallas_call | solution.py:201
  292.2 1.5 patch_first.1
  (98 shorter events, 19.6 us)
Async XLA Ops:
  0.0 8.5 %slice-start = ((s32[144,144]{1,0:T(8,128)}), s32[144,6]{1,0:T(8,128)S(1)}, s32[]{:S(2)}) async-start(s32[144,144]{1,0:T(8,128)} %param.7), calls=%async_computation | async-start | bytes 147456 | tf_op jit(solution)/shard_map/slice | solution.py:308
  2.9 72.9 %collective-permute-start.10 = (bf16[9,6,128,128]{3,2,1,0:T(8,128)(2,1)}, bf16[9,6,128,128]{3,2,1,0:T(8,128)(2,1)S(1)}, u32[]{:S(2)}, u32[]{:S(2)}) collective-permute-start(bf16[9,6,128,128]{3,2,1,0:T(8,128)(2,1)} %dynamic-slice_bitcast_fusion), channel_id=1, source_target_pairs={{0,32},{17,49},{34,66},{51,83},{68,100},{85,117},{102,6},{119,23},... | collective-permute-start | bytes 5308424 | tf_op jit(solution)/shard_map/ppermute | solution.py:356
  3.7 68.2 %collective-permute-start.11 = (bf16[9,6,128,128]{3,2,1,0:T(8,128)(2,1)}, bf16[9,6,128,128]{3,2,1,0:T(8,128)(2,1)}, u32[]{:S(2)}, u32[]{:S(2)}) collective-permute-start(bf16[9,6,128,128]{3,2,1,0:T(8,128)(2,1)} %dynamic-slice_bitcast_fusion), channel_id=1, source_target_pairs={{1,96},{16,113},{35,2},{50,19},{69,36},{84,53},{103,70},{118,87},{... | collective-permute-start | bytes 5308424 | tf_op jit(solution)/shard_map/ppermute | solution.py:357
  6.7 4.2 %collective-permute-start = (bf16[1,6,64,128]{3,2,1,0:T(8,128)(2,1)S(1)}, bf16[1,6,64,128]{3,2,1,0:T(8,128)(2,1)S(1)}, u32[]{:S(2)}, u32[]{:S(2)}) collective-permute-start(bf16[1,6,64,128]{3,2,1,0:T(8,128)(2,1)S(1)} %dynamic-slice_bitcast_fusion.2), channel_id=1, source_target_pairs={{0,16},{16,0},{32,48},{48,32},{64,80},{80,64},{96,112},{112,96},{1... | collective-permute-start | bytes 294920 | tf_op jit(solution)/shard_map/ppermute | solution.py:333
  10.9 11.3 %collective-permute-start.1 = (bf16[2,6,64,128]{3,2,1,0:T(8,128)(2,1)S(1)}, bf16[2,6,64,128]{3,2,1,0:T(8,128)(2,1)S(1)}, u32[]{:S(2)}, u32[]{:S(2)}) collective-permute-start(bf16[2,6,64,128]{3,2,1,0:T(8,128)(2,1)S(1)} %maximum_select_fusion.3), channel_id=1, source_target_pairs={{0,32},{16,48},{32,64},{48,80},{64,96},{80,112},{96,0},{112,16},{1... | collective-permute-start | bytes 589832 | tf_op jit(solution)/shard_map/ppermute | solution.py:334
  11.9 11.2 %collective-permute-start.2 = (bf16[2,6,64,128]{3,2,1,0:T(8,128)(2,1)S(1)}, bf16[2,6,64,128]{3,2,1,0:T(8,128)(2,1)S(1)}, u32[]{:S(2)}, u32[]{:S(2)}) collective-permute-start(bf16[2,6,64,128]{3,2,1,0:T(8,128)(2,1)S(1)} %maximum_select_fusion.3), channel_id=1, source_target_pairs={{0,64},{16,80},{32,96},{48,112},{64,0},{80,16},{96,32},{112,48},{1... | collective-permute-start | bytes 589832 | tf_op jit(solution)/shard_map/ppermute | solution.py:334
  18.5 9.6 %collective-permute-start.3 = (bf16[2,6,64,128]{3,2,1,0:T(8,128)(2,1)S(1)}, bf16[2,6,64,128]{3,2,1,0:T(8,128)(2,1)S(1)}, u32[]{:S(2)}, u32[]{:S(2)}) collective-permute-start(bf16[2,6,64,128]{3,2,1,0:T(8,128)(2,1)S(1)} %maximum_select_fusion.3), channel_id=1, source_target_pairs={{0,96},{16,112},{32,0},{48,16},{64,32},{80,48},{96,64},{112,80},{1... | collective-permute-start | bytes 589832 | tf_op jit(solution)/shard_map/ppermute | solution.py:334
  28.3 17.5 %copy-start.2 = (bf16[6,6,64,128]{3,2,1,0:T(8,128)(2,1)}, bf16[6,6,64,128]{3,2,1,0:T(8,128)(2,1)S(1)}, u32[]{:S(2)}) copy-start(bf16[6,6,64,128]{3,2,1,0:T(8,128)(2,1)S(1)} %pad_maximum_fusion.1.refs_2_.u_ref) | copy-start | bytes 1769476
  28.3 32.0 %collective-permute-start.4 = (bf16[6,6,64,128]{3,2,1,0:T(8,128)(2,1)S(1)}, bf16[6,6,64,128]{3,2,1,0:T(8,128)(2,1)S(1)}, u32[]{:S(2)}, u32[]{:S(2)}) collective-permute-start(bf16[6,6,64,128]{3,2,1,0:T(8,128)(2,1)S(1)} %pad_maximum_fusion.1.refs_2_.u_ref), channel_id=1, source_target_pairs={{0,1},{1,0},{2,3},{3,2},{4,5},{5,4},{6,7},{7,6},{8,9},{9,8},{10,11... | collective-permute-start | bytes 1769480 | tf_op jit(solution)/shard_map/ppermute | solution.py:340
  34.8 11.0 %copy-start.18 = (s32[144,144]{1,0:T(8,128)S(1)}, s32[144,144]{1,0:T(8,128)}, u32[]{:S(2)}) copy-start(s32[144,144]{1,0:T(8,128)} %param.7) | copy-start | bytes 248836
  60.3 0.8 copy-start.13
  68.5 29.4 %collective-permute-start.6 = (f32[2,128,1152]{2,1,0:T(8,128)}, f32[2,128,1152]{2,1,0:T(8,128)S(1)}, u32[]{:S(2)}, u32[]{:S(2)}) collective-permute-start(f32[2,128,1152]{2,1,0:T(8,128)} %get-tuple-element.20), channel_id=1, source_target_pairs={{0,32},{16,48},{32,64},{48,80},{64,96},{80,112},{96,0},{112,16},{1... | collective-permute-start | bytes 3538952 | tf_op jit(solution)/shard_map/ppermute | solution.py:387
  71.8 26.1 %copy-start.17 = (f32[128,1152]{1,0:T(8,128)S(1)}, f32[128,1152]{1,0:T(8,128)}, u32[]{:S(2)}) copy-start(f32[128,1152]{1,0:T(8,128)} %get-tuple-element.19) | copy-start | bytes 1769476
  71.8 30.8 %collective-permute-start.5 = (f32[2,128,1152]{2,1,0:T(8,128)}, f32[2,128,1152]{2,1,0:T(8,128)S(1)}, u32[]{:S(2)}, u32[]{:S(2)}) collective-permute-start(f32[2,128,1152]{2,1,0:T(8,128)} %get-tuple-element.18), channel_id=1, source_target_pairs={{0,96},{16,112},{32,0},{48,16},{64,32},{80,48},{96,64},{112,80},{1... | collective-permute-start | bytes 3538952 | tf_op jit(solution)/shard_map/ppermute | solution.py:388
  74.1 29.6 %copy-start.16 = (f32[128,1152]{1,0:T(8,128)S(1)}, f32[128,1152]{1,0:T(8,128)}, u32[]{:S(2)}) copy-start(f32[128,1152]{1,0:T(8,128)} %get-tuple-element.21) | copy-start | bytes 1769476
  74.1 34.6 %collective-permute-start.13 = (bf16[4,6,128,128]{3,2,1,0:T(8,128)(2,1)}, bf16[4,6,128,128]{3,2,1,0:T(8,128)(2,1)}, u32[]{:S(2)}, u32[]{:S(2)}) collective-permute-start(bf16[4,6,128,128]{3,2,1,0:T(8,128)(2,1)} %slice.66), channel_id=1, source_target_pairs={{96,64},{113,81},{2,98},{19,115},{36,4},{53,21},{70,38},{87,55},{1... | collective-permute-start | bytes 2359304 | tf_op jit(solution)/shard_map/ppermute | solution.py:362
  75.8 22.1 %copy-start.6 = (bf16[9,6,128,128]{3,2,1,0:T(8,128)(2,1)}, bf16[9,6,128,128]{3,2,1,0:T(8,128)(2,1)S(1)}, u32[]{:S(2)}) copy-start(bf16[9,6,128,128]{3,2,1,0:T(8,128)(2,1)S(1)} %collective-permute-done.10) | copy-start | bytes 5308420
  76.9 31.8 %collective-permute-start.12 = (bf16[5,6,128,128]{3,2,1,0:T(8,128)(2,1)}, bf16[5,6,128,128]{3,2,1,0:T(8,128)(2,1)}, u32[]{:S(2)}, u32[]{:S(2)}) collective-permute-start(bf16[5,6,128,128]{3,2,1,0:T(8,128)(2,1)} %slice.65), channel_id=1, source_target_pairs={{32,64},{49,81},{66,98},{83,115},{100,4},{117,21},{6,38},{23,55},{... | collective-permute-start | bytes 2949128 | tf_op jit(solution)/shard_map/ppermute | solution.py:362
  97.9 6.6 %copy-start.7 = (f32[2,128,1152]{2,1,0:T(8,128)}, f32[2,128,1152]{2,1,0:T(8,128)S(1)}, u32[]{:S(2)}) copy-start(f32[2,128,1152]{2,1,0:T(8,128)S(1)} %collective-permute-done.6) | copy-start | bytes 3538948
  97.9 10.8 %copy-start = (bf16[18,1,6,128,128]{4,3,2,1,0:T(8,128)(2,1)S(1)}, bf16[18,1,6,128,128]{4,3,2,1,0:T(8,128)(2,1)}, u32[]{:S(2)}) copy-start(bf16[18,1,6,128,128]{4,3,2,1,0:T(8,128)(2,1)} %param.5) | copy-start | bytes 10616836
  98.8 18.3 %collective-permute-start.7 = (f32[128,1152]{1,0:T(8,128)}, f32[128,1152]{1,0:T(8,128)}, u32[]{:S(2)}, u32[]{:S(2)}) collective-permute-start(f32[128,1152]{1,0:T(8,128)} %fusion.5), channel_id=1, source_target_pairs={{0,32},{16,48},{32,64},{48,80},{96,0},{112,16},{1,33},{17,49},{33,... | collective-permute-start | bytes 1769480 | tf_op jit(solution)/shard_map/ppermute | solution.py:389
  102.7 1.0 copy-start.10
  104.6 15.5 %collective-permute-start.8 = (f32[128,1152]{1,0:T(8,128)}, f32[128,1152]{1,0:T(8,128)}, u32[]{:S(2)}, u32[]{:S(2)}) collective-permute-start(f32[128,1152]{1,0:T(8,128)} %fusion.2), channel_id=1, source_target_pairs={{32,0},{48,16},{64,32},{80,48},{96,64},{112,80},{33,1},{49,17},{65... | collective-permute-start | bytes 1769480 | tf_op jit(solution)/shard_map/ppermute | solution.py:390
  108.7 11.4 %copy-start.4 = (f32[2,128,1152]{2,1,0:T(8,128)S(1)}, f32[2,128,1152]{2,1,0:T(8,128)}, u32[]{:S(2)}) copy-start(f32[2,128,1152]{2,1,0:T(8,128)} %get-tuple-element.17) | copy-start | bytes 3538948
  108.7 11.4 %copy-start.8 = (f32[2,128,1152]{2,1,0:T(8,128)S(1)}, f32[2,128,1152]{2,1,0:T(8,128)}, u32[]{:S(2)}) copy-start(f32[2,128,1152]{2,1,0:T(8,128)} %copy-done.7) | copy-start | bytes 3538948
  108.7 11.4 %copy-start.11 = (f32[2,128,1152]{2,1,0:T(8,128)S(1)}, f32[2,128,1152]{2,1,0:T(8,128)}, u32[]{:S(2)}) copy-start(f32[2,128,1152]{2,1,0:T(8,128)} %copy-done.10) | copy-start | bytes 3538948
  112.4 39.0 %collective-permute-start.14 = (bf16[9,6,128,128]{3,2,1,0:T(8,128)(2,1)}, bf16[9,6,128,128]{3,2,1,0:T(8,128)(2,1)}, u32[]{:S(2)}, u32[]{:S(2)}) collective-permute-start(bf16[9,6,128,128]{3,2,1,0:T(8,128)(2,1)} %fusion.1.near_ref), channel_id=1, source_target_pairs={{0,16},{32,48},{64,80},{17,1},{49,33},{81,65},{2,18},{34,50},{66,8... | collective-permute-start | bytes 5308424 | tf_op jit(solution)/shard_map/ppermute | solution.py:371
  120.1 7.3 %copy-start.19 = (s32[9,16,6]{1,0,2:T(8,128)S(1)}, s32[9,16,6]{1,0,2:T(8,128)}, u32[]{:S(2)}) copy-start(s32[9,16,6]{1,0,2:T(8,128)} %reshape.51) | copy-start | bytes 10372
  120.1 28.9 %copy-start.5 = (f32[2,128,1152]{2,1,0:T(8,128)S(1)}, f32[2,128,1152]{2,1,0:T(8,128)}, u32[]{:S(2)}) copy-start(f32[2,128,1152]{2,1,0:T(8,128)} %get-tuple-element.17) | copy-start | bytes 3538948
  120.1 28.9 %copy-start.9 = (f32[2,128,1152]{2,1,0:T(8,128)S(1)}, f32[2,128,1152]{2,1,0:T(8,128)}, u32[]{:S(2)}) copy-start(f32[2,128,1152]{2,1,0:T(8,128)} %copy-done.7) | copy-start | bytes 3538948
  120.1 28.9 %copy-start.12 = (f32[2,128,1152]{2,1,0:T(8,128)S(1)}, f32[2,128,1152]{2,1,0:T(8,128)}, u32[]{:S(2)}) copy-start(f32[2,128,1152]{2,1,0:T(8,128)} %copy-done.10) | copy-start | bytes 3538948
  122.6 26.3 %collective-permute-start.9 = (f32[128,1152]{1,0:T(8,128)}, f32[128,1152]{1,0:T(8,128)}, u32[]{:S(2)}, u32[]{:S(2)}) collective-permute-start(f32[128,1152]{1,0:T(8,128)} %broadcast_select_fusion.1), channel_id=1, source_target_pairs={{0,16},{16,0},{32,48},{48,32},{64,80},{80,64},{1,17},{17,1},{33,49... | collective-permute-start | bytes 1769480 | tf_op jit(solution)/shard_map/ppermute | solution.py:393
  127.8 23.6 %copy-start.20 = (s32[9,6]{1,0:T(8,128)}, s32[9,6]{1,0:T(8,128)S(1)}, u32[]{:S(2)}) copy-start(s32[9,6]{1,0:T(8,128)S(1)} %fusion.10.live) | copy-start | bytes 652
  156.1 3.8 %collective-permute-start.15 = (f32[64,768]{1,0:T(8,128)S(1)}, f32[64,768]{1,0:T(8,128)S(1)}, u32[]{:S(2)}, u32[]{:S(2)}) collective-permute-start(f32[64,768]{1,0:T(8,128)S(1)} %dynamic-slice_bitcast_fusion.1), channel_id=1, source_target_pairs={{0,1},{1,0},{2,3},{3,2},{4,5},{5,4},{6,7},{7,6},{8,9},{9,8},{10,11... | collective-permute-start | bytes 589832 | tf_op jit(solution)/shard_map/ppermute | solution.py:406
  160.9 7.9 %collective-permute-start.16 = (f32[64,768]{1,0:T(8,128)S(1)}, f32[64,768]{1,0:T(8,128)S(1)}, u32[]{:S(2)}, u32[]{:S(2)}) collective-permute-start(f32[64,768]{1,0:T(8,128)S(1)} %bitcast_add_fusion), channel_id=1, source_target_pairs={{0,2},{1,3},{2,0},{3,1},{4,6},{5,7},{6,4},{7,5},{8,10},{9,11},{10,... | collective-permute-start | bytes 589832 | tf_op jit(solution)/shard_map/ppermute | solution.py:407
  168.7 5.3 %collective-permute-start.17 = (f32[64,768]{1,0:T(8,128)S(1)}, f32[64,768]{1,0:T(8,128)S(1)}, u32[]{:S(2)}, u32[]{:S(2)}) collective-permute-start(f32[64,768]{1,0:T(8,128)S(1)} %add.195), channel_id=1, source_target_pairs={{0,4},{1,5},{2,6},{3,7},{4,0},{5,1},{6,2},{7,3},{8,12},{9,13},{10,... | collective-permute-start | bytes 589832 | tf_op jit(solution)/shard_map/ppermute | solution.py:408
  174.1 5.8 %collective-permute-start.18 = (f32[64,768]{1,0:T(8,128)S(1)}, f32[64,768]{1,0:T(8,128)S(1)}, u32[]{:S(2)}, u32[]{:S(2)}) collective-permute-start(f32[64,768]{1,0:T(8,128)S(1)} %add.196), channel_id=1, source_target_pairs={{0,12},{1,13},{2,14},{3,15},{4,8},{5,9},{6,10},{7,11},{8,4},{9,5},... | collective-permute-start | bytes 589832 | tf_op jit(solution)/shard_map/ppermute | solution.py:409
  179.9 7.2 %collective-permute-start.19 = (f32[1,64,768]{2,1,0:T(8,128)S(1)}, f32[1,64,768]{2,1,0:T(8,128)S(1)}, u32[]{:S(2)}, u32[]{:S(2)}) collective-permute-start(f32[1,64,768]{2,1,0:T(8,128)S(1)} %add_bitcast_fusion), channel_id=1, source_target_pairs={{0,16},{1,17},{2,18},{3,19},{4,20},{5,21},{16,0},{17,1},{18,2},{19... | collective-permute-start | bytes 589832 | tf_op jit(solution)/shard_map/ppermute | solution.py:415
  187.1 11.4 %collective-permute-start.20 = (f32[2,64,768]{2,1,0:T(8,128)S(1)}, f32[2,64,768]{2,1,0:T(8,128)S(1)}, u32[]{:S(2)}, u32[]{:S(2)}) collective-permute-start(f32[2,64,768]{2,1,0:T(8,128)S(1)} %maximum_select_fusion.2), channel_id=1, source_target_pairs={{0,32},{1,33},{2,34},{3,35},{4,36},{5,37},{16,48},{17,49},{18,50},... | collective-permute-start | bytes 1179656 | tf_op jit(solution)/shard_map/ppermute | solution.py:416
  198.6 13.5 %collective-permute-start.21 = (f32[4,64,768]{2,1,0:T(8,128)S(1)}, f32[4,64,768]{2,1,0:T(8,128)S(1)}, u32[]{:S(2)}, u32[]{:S(2)}) collective-permute-start(f32[4,64,768]{2,1,0:T(8,128)S(1)} %maximum_select_fusion.1), channel_id=1, source_target_pairs={{0,96},{1,97},{2,98},{3,99},{4,100},{5,101},{16,112},{17,113},{18,... | collective-permute-start | bytes 2359304 | tf_op jit(solution)/shard_map/ppermute | solution.py:418
  200.0 8.5 %collective-permute-start.22 = (f32[2,64,768]{2,1,0:T(8,128)S(1)}, f32[2,64,768]{2,1,0:T(8,128)S(1)}, u32[]{:S(2)}, u32[]{:S(2)}) collective-permute-start(f32[2,64,768]{2,1,0:T(8,128)S(1)} %slice.67), channel_id=1, source_target_pairs={{64,32},{65,33},{66,34},{67,35},{68,36},{69,37},{80,48},{81,49},{8... | collective-permute-start | bytes 1179656 | tf_op jit(solution)/shard_map/ppermute | solution.py:419
  212.2 7.7 %copy-start.1 = (f32[128,1152]{1,0:T(8,128)S(1)}, f32[128,1152]{1,0:T(8,128)}, u32[]{:S(2)}) copy-start(f32[128,1152]{1,0:T(8,128)} %add_select_fusion.row_ref.refs_0_) | copy-start | bytes 1769476
  212.3 72.8 %copy-start.3 = (f32[6,64,768]{2,1,0:T(8,128)}, f32[6,64,768]{2,1,0:T(8,128)S(1)}, u32[]{:S(2)}) copy-start(f32[6,64,768]{2,1,0:T(8,128)S(1)} %pad_maximum_fusion.g_ref) | copy-start | bytes 3538948
  212.4 72.8 %collective-permute-start.23 = (f32[6,64,768]{2,1,0:T(8,128)S(1)}, f32[6,64,768]{2,1,0:T(8,128)S(1)}, u32[]{:S(2)}, u32[]{:S(2)}) collective-permute-start(f32[6,64,768]{2,1,0:T(8,128)S(1)} %pad_maximum_fusion.g_ref), channel_id=1, source_target_pairs={{0,1},{1,0},{2,3},{3,2},{4,5},{5,4},{16,17},{17,16},{18,19},{19,18... | collective-permute-start | bytes 3538952 | tf_op jit(solution)/shard_map/ppermute | solution.py:422
  219.9 61.3 %collective-permute-start.24 = (f32[128,1152]{1,0:T(8,128)S(1)}, f32[128,1152]{1,0:T(8,128)S(1)}, u32[]{:S(2)}, u32[]{:S(2)}) collective-permute-start(f32[128,1152]{1,0:T(8,128)S(1)} %copy-done.1), channel_id=1, source_target_pairs={{0,0},{1,16},{2,32},{3,48},{4,64},{5,80},{6,96},{7,112},{16,1},{17... | collective-permute-start | bytes 1769480 | tf_op jit(solution)/shard_map/ppermute | solution.py:400
  224.8 56.5 %collective-permute-start.25 = (f32[128,1152]{1,0:T(8,128)S(1)}, f32[128,1152]{1,0:T(8,128)}, u32[]{:S(2)}, u32[]{:S(2)}) collective-permute-start(f32[128,1152]{1,0:T(8,128)S(1)} %copy-done.1), channel_id=1, source_target_pairs={{8,0},{9,16},{10,32},{11,48},{12,64},{13,80},{14,96},{15,112},{24,... | collective-permute-start | bytes 1769480 | tf_op jit(solution)/shard_map/ppermute | solution.py:400
  281.3 0.8 copy-start.15
  285.2 1.0 copy-start.14
where the time goes:
time: 295 us; the launch traced here: 294 us
  waiting for transfers between devices  148 us (50%)
  starting transfers between devices  70.5 us (24%)
  Pallas kernels  45.2 us (15%)
  local copies, waits for them, and re-layouts  15.8 us (5%)
  other arithmetic  13.7 us (5%)
    ppermute x1, waiting for transfers between devices, per_device(): lax.ppermute(row, both, route(0))  53.9 us
    pallas_call x2, Pallas kernels, products(): pl.pallas_call(product_kernel, grid_spec=pltpu.PrefetchScalarGridSpec(num...  23.6 us
    ppermute x1, waiting for transfers between devices, per_device(): full = keep + lax.ppermute(give, 'prow', [(d, d ^ 1) for d in range(steps)])  20.9 us
    ppermute x1, waiting for transfers between devices, per_device(): up = lax.ppermute(up, 'prow', ring(1))  19.4 us
    ppermute x3, waiting for transfers between devices, per_device(): lax.ppermute(pair, 'prow', ring(shift))  8.9 us
    ppermute x3, starting transfers between devices, per_device(): lax.ppermute(pair, 'prow', ring(shift))  7.65 us
    ppermute x1, waiting for transfers between devices, per_device(): got = got + lax.ppermute(got, 'pcol', [(d, d ^ 2) for d in range(n_col)])  7.58 us
    ppermute x1, starting transfers between devices, per_device(): other = lax.ppermute(got, 'pcol', [(d, d ^ 1) for d in range(steps)])  7.54 us
  transfers between devices with their start and end apart: 26, of which 17 were waited for; matrix products, arithmetic and copies ran while one was open for 7% of the time, Pallas kernels for 12%

commit v1 on v0

--- a/solution.py
+++ b/solution.py
@@ -130,38 +130,46 @@
     )(take, live, *parts, *corner)
 
 
-def column_kernel(info, live, row_ref, near_ref, far_ref, out_ref):
-    cols, steps, width, _ = near_ref.shape
-    total = None
-    for c in range(0, cols, 2):
-        count = min(2, cols - c)
-        left = jnp.concatenate(halves(row_ref[:, pl.ds(c * width, count * width)]), axis=0)
-        right = []
-        for r in range(c, c + count):
-            wide = []
-            for k in range(steps):
-                block = jnp.where(info[0] > 0, near_ref[r, k], far_ref[r, k])
-                wide.append(jnp.where(live[r, k] > 0, block, jnp.zeros_like(block)))
-            right.append(jnp.concatenate(wide, axis=1))
-        term = dot(left, jnp.concatenate(right, axis=0))
-        total = term if total is None else total + term
-    out_ref[...] = total[:width] + total[width:]
-
-
-def column_products(info, live, row, near, far):
-    cols, steps, width, _ = near.shape
+def column_kernel(live, *refs):
+    *value_refs, u_ref, out_ref = refs
+    _, steps, width, _ = u_ref.shape
+    total, a = None, 0
+    for even_ref, odd_ref in zip(value_refs[::2], value_refs[1::2]):
+        for c in range(even_ref.shape[1] // width):
+            part = pl.ds(c * width, width)
+            value = jnp.concatenate([even_ref[:, part], odd_ref[:, part]], axis=1)
+            left = jnp.concatenate(halves(value), axis=0)
+            right = []
+            for r in (a, a + 1):
+                wide = []
+                for k in range(steps):
+                    block = u_ref[r, k]
+                    wide.append(jnp.where(live[r, k] > 0, block, jnp.zeros_like(block)))
+                right.append(jnp.concatenate(wide, axis=1))
+            term = dot(left, jnp.concatenate(right, axis=0))
+            total = term if total is None else total + term
+            a += 2
+    total = total[:width] + total[width:]
+    out_ref[...] = total
+
+
+def column_products(values, lower, live):
+    row_blocks, steps, width, _ = lower.shape
     return pl.pallas_call(
         column_kernel,
-        in_specs=[SMEM, SMEM, VMEM, VMEM, VMEM],
+        in_specs=[SMEM] + [VMEM] * (len(values) + 1),
         out_specs=VMEM,
         out_shape=jax.ShapeDtypeStruct((width, steps * width), F32),
-        cost_estimate=pl.CostEstimate(flops=4 * cols * steps * width**3, bytes_accessed=6 * 10**6, transcendentals=0),
+        cost_estimate=pl.CostEstimate(flops=4 * row_blocks * steps * width**3, bytes_accessed=6 * 10**6, transcendentals=0),
         name="column",
-    )(info, live, row, near, far)
-
-
-def corner_kernel(info, live, g_ref, h_ref, u_ref, v_ref, dinv_ref, out_ref, x_ref):
+    )(live, *values, lower)
+
+
+def corner_kernel(info, live, *refs):
+    *sum_refs, u_ref, v_ref, dinv_ref, out_ref, x_ref, h_ref = refs
     steps, width, _ = dinv_ref.shape
+    for n, ref in enumerate(sum_refs):
+        h_ref[info[3 + n]] = ref[...]
     for k in reversed(range(steps)):
         here = pl.ds(k * width, width)
         later = steps - 1 - k
@@ -178,16 +186,16 @@
             turned = []
             for i in range(k + 1, steps):
                 at = (i - k - 1) * width
-                block = -(value[at : at + width] + stacked(info[2], g_ref[i, :, here], h_ref[i, :, here]))
+                block = -(value[at : at + width] + h_ref[i, :, here])
                 block = jnp.where(live[i, k] > 0, block, jnp.zeros_like(block))
                 x_ref[pl.ds(i * width, width), here] = block
                 turned.append(block.T)
             turned = jnp.concatenate(turned, axis=1)
             x_ref[here, rest] = turned
             tail = dot(jnp.concatenate(halves(turned), axis=1), both)
-            x_ref[here, here] = dinv_ref[k].T - stacked(info[2], g_ref[k, :, here], h_ref[k, :, here]) - tail
+            x_ref[here, here] = dinv_ref[k].T - h_ref[k, :, here] - tail
         else:
-            x_ref[here, here] = dinv_ref[k].T - stacked(info[2], g_ref[k, :, here], h_ref[k, :, here])
+            x_ref[here, here] = dinv_ref[k].T - h_ref[k, :, here]
     for k in range(steps):
         for j in range(steps):
 
@@ -200,10 +208,13 @@
     steps, width, _ = dinv.shape
     return pl.pallas_call(
         corner_kernel,
-        in_specs=[SMEM, SMEM] + [VMEM] * 5,
+        in_specs=[SMEM, SMEM] + [VMEM] * (len(sums) + 3),
         out_specs=VMEM,
         out_shape=jax.ShapeDtypeStruct((width, width), F32),
-        scratch_shapes=[pltpu.VMEM((steps * width, steps * width), F32)],
+        scratch_shapes=[
+            pltpu.VMEM((steps * width, steps * width), F32),
+            pltpu.VMEM((steps, width, steps * width), F32),
+        ],
         cost_estimate=pl.CostEstimate(flops=10**9, bytes_accessed=10**6, transcendentals=0),
         name="corner",
     )(info, live, *sums, *corner, dinv)
@@ -345,30 +356,6 @@
 
     def device(x, h, c, zz, yy):
         return at(zz, yy) * n_col + x * 4 + h * 2 + c
-
-    def source(x, h):
-        return x % 2 * 2 + h
-
-    mine = lower.reshape(cols, 2, steps, width, width)
-    mine = lax.dynamic_index_in_dim(mine, q // n_row, 1, keepdims=False)
-    ahead = [(device(x, h, c, source(x, h), c), device(x, h, c, source(x, h) + 1, c)) for x, h, c in grid]
-    behind = [(device(x, h, 1 - c, source(x, h), c), device(x, h, c, source(x, h) + 3, c)) for x, h, c in grid]
-    from_behind = lax.ppermute(mine, both, ahead)
-    from_ahead = lax.ppermute(mine, both, behind)
-    cut = (cols + 1) // 2
-    ahead = [(device(x, h, c, source(x, h) + 1, c), device(x, h, c, source(x, h) + 2, c)) for x, h, c in grid]
-    behind = [(device(x, h, c, source(x, h) + 3, c), device(x, h, c, source(x, h) + 2, c)) for x, h, c in grid]
-    opposite = jnp.concatenate(
-        [lax.ppermute(from_behind[:cut], both, ahead), lax.ppermute(from_ahead[cut:], both, behind)]
-    )
-    apart = (z - (q // 4 % 2 * 2 + q // 2 % 2)) % n_z
-    near_u = jnp.where(
-        apart == 0, mine, jnp.where(apart == 1, from_behind, jnp.where(apart == 3, from_ahead, opposite))
-    )
-    across = [
-        (device(x, h, c, zz, c), device(x, h, c, zz, 1 - c)) for x, h, c in grid for zz in range(n_dest)
-    ]
-    far_u = lax.ppermute(near_u, both, across)
 
     whole, parts = None, []
     for first, count in PARTS:
@@ -394,38 +381,43 @@
     mask = jnp.broadcast_to(row_live[:, None], (cols, width)).reshape(1, cols * width)
     row = jnp.where(mask, full, jnp.zeros_like(full))
 
-    def route(group):
-        return [(k * n_col + d + group * n_row, d * n_col + k) for k in range(steps) for d in range(n_row)]
-
-    values = [row, lax.ppermute(row, both, route(0)), lax.ppermute(row, both, route(1))]
-
-    sums = column_products((y == core).astype(jnp.int32).reshape(1), live_cols, row, near_u, far_u)
-    parts = sums.reshape(2, half, steps * width)
-    keep = lax.dynamic_index_in_dim(parts, core, 0, keepdims=False)
-    give = lax.dynamic_index_in_dim(parts, 1 - core, 0, keepdims=False)
-    got = keep + lax.ppermute(give, "pcol", flip_core)
-    got = got + lax.ppermute(got, "pcol", [(d, d ^ 2) for d in range(n_col)])
-    got = got + lax.ppermute(got, "pcol", [(d, d ^ 4) for d in range(n_col)])
-    got = got + lax.ppermute(got, "pcol", [(d, (n_col // 4 - 1 - d // 4) * 4 + d % 4) for d in range(n_col)])
+    def turn(k, x, h, c):
+        return at(k // 2, k % 2) * n_col + x * 4 + h * 2 + c, device(x, k // 2 % 2, k % 2, x % 2 * 2 + h, c)
+
+    places = [(h, c, zz, yy) for h in range(2) for c in range(2) for zz in range(n_z) for yy in range(2)]
+
+    def slide(place, start, end):
+        h, c, zz, yy = place
+        return device(start, h, c, zz, yy), device(end, h, c, zz, yy)
+
+    x = q // 4
+    first = lax.ppermute(row, both, [turn(k, *place) for k in range(4) for place in grid])
+    second = lax.ppermute(row, both, [turn(k, *place) for k in range(4, steps) for place in grid])
+    odd0 = lax.ppermute(first, both, [slide(pl_, pl_[2] // 2 + 2, 0) for pl_ in places])
+    odd1 = lax.ppermute(second, both, [slide(pl_, pl_[2] // 2 + 2, 1) for pl_ in places if pl_[0] == 0])
+    route = [slide(pl_, 0, 1) for pl_ in places if pl_[2] // 2 == 0 and pl_[0] == 0]
+    route += [slide(pl_, 1, 0) for pl_ in places if pl_[2] // 2 == 1]
+    moved = lax.ppermute(jnp.where(x == 0, second, first), both, route)
+    mine = jnp.where(x == 0, first, second)
+    values = [row, jnp.where(x == z // 2, mine, moved), jnp.where(x == 0, odd0, odd1)]
+
+    sums = column_products(values[1:], lower, live)
 
     def here(perm):
         return [(s * n_col + d, t * n_col + d) for s, t in perm for d in range(steps)]
 
-    got = got[None]
-    got = join(y, got, lax.ppermute(got, both, here(flip_y)))
-    got = join(z % 2, got, lax.ppermute(got, both, here(flip_z)))
-    last = steps - 4
-    rise = lax.ppermute(got, both, here([(s, t) for s, t in mirror if s < 4]))
-    fall = lax.ppermute(got[:last], both, here([(s, t) for s, t in mirror if s >= 4]))
-    upper = z // 2 == 1
-    got = jnp.concatenate([jnp.where(upper, rise, got), jnp.where(upper, got[:last], fall)])
-    other = lax.ppermute(got, "pcol", [(d, d ^ 1) for d in range(steps)])
-    sums = got, other
+    for perm in (flip_y, flip_z, mirror):
+        sums = sums + lax.ppermute(sums, both, here(perm))
+    turns = [lax.ppermute(sums, "pcol", [(d, (d + t) % steps) for d in range(steps)]) for t in (2, 4)]
+    sums = [sums, *turns]
+    sums += [lax.ppermute(v, "pcol", [(d, d ^ 1) for d in range(steps)]) for v in sums]
+    slots = [(q + steps - t) % steps for t in (0, 2, 4)]
+    slots += [s ^ 1 for s in slots]
 
     has_row, has_col = p < steps, q < steps
     info = jnp.stack([has_row, has_col, has_row & ~has_col, has_col & ~has_row]).astype(jnp.int32)
     whole = patch(info, values, whole)
-    info = jnp.stack([p, q, core]).astype(jnp.int32)
+    info = jnp.stack([p, q, core, *slots]).astype(jnp.int32)
     block = corner_blocks(info, live_corner, sums, corner, dinv)
     info = jnp.stack([has_row & has_col]).astype(jnp.int32)
     whole = patch_first(info, block, whole)

time: 295 us -> 243 us (0.82)
  the two profiles are of different devices: /device:TPU:33 before, /device:TPU:25 now
where the time goes in v1:
time: 243 us; the launch traced here: 242 us
  waiting for transfers between devices  112 us (46%)
  starting transfers between devices  65.1 us (27%)
  Pallas kernels  45.6 us (19%)
  other arithmetic  9.78 us (4%)
  local copies, waits for them, and re-layouts  9.22 us (4%)
    ppermute x3, waiting for transfers between devices, per_device(): sums = sums + lax.ppermute(sums, both, here(perm))  30.4 us
    ppermute x1, waiting for transfers between devices, per_device(): up = lax.ppermute(up, 'prow', ring(1))  26.3 us
    pallas_call x2, Pallas kernels, products(): pl.pallas_call(product_kernel, grid_spec=pltpu.PrefetchScalarGridSpec(num...  23.5 us
    ppermute x3, starting transfers between devices, per_device(): sums = sums + lax.ppermute(sums, both, here(perm))  16.8 us
    ppermute x3, starting transfers between devices, per_device(): lax.ppermute(v, 'pcol', [(d, d ^ 1) for d in range(steps)])  16.2 us
    ppermute x1, waiting for transfers between devices, per_device(): up2 = lax.ppermute(up2 + up[0], 'prow', near(1))  13.8 us
    ppermute x1, waiting for transfers between devices, per_device(): full = keep + lax.ppermute(give, 'prow', [(d, d ^ 1) for d in range(steps)])  11.1 us
    ppermute x1, waiting for transfers between devices, per_device(): lax.ppermute(row, both, [turn(k, *place) for k in range(4) for place in g...  10.3 us
  transfers between devices with their start and end apart: 23, of which 13 were waited for; matrix products, arithmetic and copies ran while one was open for 4% of the time, Pallas kernels for 11%

profile of v1, /device:TPU:25, one launch (start us, length us, event | category | flops | bytes accessed | tf_op | source)
XLA Modules:
  0.0 241.9 jit_solution(12212789527287036683)
XLA Ops:
  0.0 0.9 slice.39
  1.5 0.9 slice.36
  3.0 1.6 collective-permute-done
  4.5 1.7 collective-permute-start.1
  6.3 3.3 %collective-permute-start.2 = (bf16[2,6,64,128]{3,2,1,0:T(8,128)(2,1)S(1)}, bf16[2,6,64,128]{3,2,1,0:T(8,128)(2,1)S(1)}, u32[]{:S(2)}, u32[]{:S(2)}) collective-permute-start(bf16[2,6,64,128]{3,2,1,0:T(8,128)(2,1)S(1)} %maximum_select_fusion), channel_id=1, source_target_pairs={{0,64},{16,80},{32,96},{48,112},{64,0},{80,16},{96,32},{112,48},{1... | collective-permute-start | bytes 589832 | tf_op jit(solution)/shard_map/ppermute | solution.py:345
  11.0 0.9 collective-permute-done.1
  11.8 4.8 %collective-permute-done.2 = bf16[2,6,64,128]{3,2,1,0:T(8,128)(2,1)S(1)} collective-permute-done((bf16[2,6,64,128]{3,2,1,0:T(8,128)(2,1)S(1)}, bf16[2,6,64,128]{3,2,1,0:T(8,128)(2,1)S(1)}, u32[]{:S(2)}, u32[]{:S(2)}) %collective-permute-start.2) | collective-permute-done | bytes 196640 | tf_op jit(solution)/shard_map/ppermute | solution.py:345
  16.8 3.1 %collective-permute-start.4 = (bf16[6,6,64,128]{3,2,1,0:T(8,128)(2,1)S(1)}, bf16[6,6,64,128]{3,2,1,0:T(8,128)(2,1)S(1)}, u32[]{:S(2)}, u32[]{:S(2)}) collective-permute-start(bf16[6,6,64,128]{3,2,1,0:T(8,128)(2,1)S(1)} %pad_maximum_fusion.refs_2_.refs_6_), channel_id=1, source_target_pairs={{0,1},{1,0},{2,3},{3,2},{4,5},{5,4},{6,7},{7,6},{8,9},{9,8},{10,11... | collective-permute-start | bytes 1769480 | tf_op jit(solution)/shard_map/ppermute | solution.py:351
  19.9 10.8 %products.2 = (f32[18,9,128,128]{3,2,1,0:T(8,128)}, f32[6,128,1152]{2,1,0:T(8,128)}) custom-call(s32[8,6]{1,0:T(8,128)} %slice.46.live, f32[18,9,128,128]{3,2,1,0:T(8,128)} %bitcast.65, bf16[18,6,128,128]{3,2,1,0:T(8,128)(2,1)} %bitcast.67), custom_call_target="tpu_custom_call" | custom-call | flops 3623878656 | bytes 9437184 | tf_op jit(solution)/shard_map/products/pallas_call | solution.py:66
  30.7 1.3 slice.35.live
  33.2 12.7 %products.3 = (f32[18,9,128,128]{3,2,1,0:T(8,128)}, f32[6,128,1152]{2,1,0:T(8,128)}) custom-call(s32[10,6]{1,0:T(8,128)} %slice.47.live, f32[18,9,128,128]{3,2,1,0:T(8,128)} %bitcast.66, bf16[18,6,128,128]{3,2,1,0:T(8,128)(2,1)} %bitcast.68, f32[18,9,128,128]{3,2,1,0:T(8,128)} %get-tuple-element.15.refs_0_), custom_call_target="tpu_custom_call", output_to_operand_aliasing={{0}: (3, {})} | custom-call | flops 4529848320 | bytes 11796480 | tf_op jit(solution)/shard_map/products/pallas_call | solution.py:66
  45.9 0.8 copy-done.4
  46.7 7.3 %eliminate.1 = (f32[2,128,1152]{2,1,0:T(8,128)}, f32[2,128,1152]{2,1,0:T(8,128)}, f32[128,1152]{1,0:T(8,128)}, f32[128,1152]{1,0:T(8,128)}, f32[2,128,1152]{2,1,0:T(8,128)}) custom-call(s32[9]{0:T(128)} %stack.92.take, s32[6,6]{1,0:T(8,128)} %slice.35.live, f32[6,128,1152]{2,1,0:T(8,128)} %get-tuple-element.14.refs_0_, ...), custom_call_target="tpu_custom_call" | custom-call | flops 884736000 | bytes 17694720 | tf_op jit(solution)/shard_map/eliminate/pallas_call | solution.py:122
  54.1 0.9 collective-permute-start.6
  55.0 1.7 collective-permute-start.5
  56.7 26.3 %collective-permute-done.6 = f32[2,128,1152]{2,1,0:T(8,128)S(1)} collective-permute-done((f32[2,128,1152]{2,1,0:T(8,128)}, f32[2,128,1152]{2,1,0:T(8,128)S(1)}, u32[]{:S(2)}, u32[]{:S(2)}) %collective-permute-start.6) | collective-permute-done | bytes 1179680 | tf_op jit(solution)/shard_map/ppermute | solution.py:374
  83.0 1.1 fusion.3
  84.1 2.1 collective-permute-start.7
  86.3 1.3 collective-permute-start.8
  87.6 13.8 %collective-permute-done.7 = f32[128,1152]{1,0:T(8,128)S(1)} collective-permute-done((f32[128,1152]{1,0:T(8,128)S(1)}, f32[128,1152]{1,0:T(8,128)S(1)}, u32[]{:S(2)}, u32[]{:S(2)}) %collective-permute-start.7) | collective-permute-done | bytes 589856 | tf_op jit(solution)/shard_map/ppermute | solution.py:376
  102.2 1.0 broadcast_select_fusion
  103.2 2.4 collective-permute-start.9
  106.3 1.1 fusion.6
  107.5 11.1 %collective-permute-done.9 = f32[128,1152]{1,0:T(8,128)} collective-permute-done((f32[128,1152]{1,0:T(8,128)}, f32[128,1152]{1,0:T(8,128)}, u32[]{:S(2)}, u32[]{:S(2)}) %collective-permute-start.9) | collective-permute-done | bytes 589856 | tf_op jit(solution)/shard_map/ppermute | solution.py:380
  118.6 2.4 %add_select_fusion.refs_0_ = f32[128,1152]{1,0:T(8,128)} fusion(f32[128,1152]{1,0:T(8,128)} %collective-permute-done.9, pred[]{:T(512)S(6)} %eq.59, pred[1152]{0:T(1024)(128)(4,1)S(1)} %broadcast_bitcast_fusion, f32[128,1152]{1,0:T(8,128)} %copy-done.2, f32[2,128,1152]{2,1,0:T(8,128)S(1)} %collective-permute-done.5, f32[2,128,1152]{2,1,0:T(8,128)S(1)} %copy-done.1, ...), kind=kLoop, calls=%fused_computation.12 | loop fusion | flops 1032192 | bytes 4719745 | tf_op jit(solution)/shard_map/jit(_where)/select_n | solution.py:382
  121.7 3.0 %collective-permute-start.10 = (f32[128,1152]{1,0:T(8,128)}, f32[128,1152]{1,0:T(8,128)S(1)}, u32[]{:S(2)}, u32[]{:S(2)}) collective-permute-start(f32[128,1152]{1,0:T(8,128)} %add_select_fusion.refs_0_), channel_id=1, source_target_pairs={{0,0},{1,16},{2,32},{3,48},{4,68},{5,84},{6,100},{7,116},{8,8},{9,... | collective-permute-start | bytes 1769480 | tf_op jit(solution)/shard_map/ppermute | solution.py:394
  124.8 10.3 %collective-permute-done.10 = f32[128,1152]{1,0:T(8,128)S(1)} collective-permute-done((f32[128,1152]{1,0:T(8,128)}, f32[128,1152]{1,0:T(8,128)S(1)}, u32[]{:S(2)}, u32[]{:S(2)}) %collective-permute-start.10) | collective-permute-done | bytes 589856 | tf_op jit(solution)/shard_map/ppermute | solution.py:394
  135.8 1.3 collective-permute-start.13
  137.9 0.9 select_select_fusion.refs_0_.refs_1_
  138.8 9.1 %collective-permute-done.13 = f32[128,1152]{1,0:T(8,128)S(1)} collective-permute-done((f32[128,1152]{1,0:T(8,128)S(1)}, f32[128,1152]{1,0:T(8,128)S(1)}, u32[]{:S(2)}, u32[]{:S(2)}) %collective-permute-start.13) | collective-permute-done | bytes 589856 | tf_op jit(solution)/shard_map/ppermute | solution.py:396
  148.0 0.9 broadcast_select_fusion.1.refs_1_.refs_2_
  148.9 4.2 %column.1 = f32[128,768]{1,0:T(8,128)} custom-call(s32[18,6]{1,0:T(8,128)} %copy-done.12, f32[128,1152]{1,0:T(8,128)} %select_select_fusion.refs_0_.refs_1_, f32[128,1152]{1,0:T(8,128)} %broadcast_select_fusion.1.refs_1_.refs_2_, bf16[18,6,128,128]{3,2,1,0:T(8,128)(2,1)} %bitcast.69), custom_call_target="tpu_custom_call" | custom-call | flops 905969664 | bytes 6000000 | tf_op jit(solution)/shard_map/column/pallas_call | solution.py:158
  153.1 12.9 %collective-permute-start.15 = (f32[128,768]{1,0:T(8,128)}, f32[128,768]{1,0:T(8,128)S(1)}, u32[]{:S(2)}, u32[]{:S(2)}) collective-permute-start(f32[128,768]{1,0:T(8,128)} %column.1), channel_id=1, source_target_pairs={{0,16},{1,17},{2,18},{3,19},{4,20},{5,21},{16,0},{17,1},{18,2},{19... | collective-permute-start | bytes 1179656 | tf_op jit(solution)/shard_map/ppermute | solution.py:410
  166.0 8.9 %collective-permute-done.15 = f32[128,768]{1,0:T(8,128)S(1)} collective-permute-done((f32[128,768]{1,0:T(8,128)}, f32[128,768]{1,0:T(8,128)S(1)}, u32[]{:S(2)}, u32[]{:S(2)}) %collective-permute-start.15) | collective-permute-done | bytes 393248 | tf_op jit(solution)/shard_map/ppermute | solution.py:410
  174.9 1.1 add.178
  176.0 1.9 collective-permute-start.16
  177.9 10.6 %collective-permute-done.16 = f32[128,768]{1,0:T(8,128)S(1)} collective-permute-done((f32[128,768]{1,0:T(8,128)S(1)}, f32[128,768]{1,0:T(8,128)S(1)}, u32[]{:S(2)}, u32[]{:S(2)}) %collective-permute-start.16) | collective-permute-done | bytes 393248 | tf_op jit(solution)/shard_map/ppermute | solution.py:410
  188.5 2.0 collective-permute-start.17
  190.6 10.8 %collective-permute-done.17 = f32[128,768]{1,0:T(8,128)S(1)} collective-permute-done((f32[128,768]{1,0:T(8,128)S(1)}, f32[128,768]{1,0:T(8,128)S(1)}, u32[]{:S(2)}, u32[]{:S(2)}) %collective-permute-start.17) | collective-permute-done | bytes 393248 | tf_op jit(solution)/shard_map/ppermute | solution.py:410
  201.5 5.8 %collective-permute-start.18 = (f32[128,768]{1,0:T(8,128)S(1)}, f32[128,768]{1,0:T(8,128)S(1)}, u32[]{:S(2)}, u32[]{:S(2)}) collective-permute-start(f32[128,768]{1,0:T(8,128)S(1)} %add.180.refs_0_), channel_id=1, source_target_pairs={{0,2},{1,3},{2,4},{3,5},{4,0},{5,1},{16,18},{17,19},{18,20},{19,21... | collective-permute-start | bytes 1179656 | tf_op jit(solution)/shard_map/ppermute | solution.py:411
  207.3 2.1 collective-permute-start.19
  209.5 4.7 %collective-permute-start.20 = (f32[128,768]{1,0:T(8,128)S(1)}, f32[128,768]{1,0:T(8,128)S(1)}, u32[]{:S(2)}, u32[]{:S(2)}) collective-permute-start(f32[128,768]{1,0:T(8,128)S(1)} %add.180.refs_0_), channel_id=1, source_target_pairs={{0,1},{1,0},{2,3},{3,2},{4,5},{5,4},{16,17},{17,16},{18,19},{19,18... | collective-permute-start | bytes 1179656 | tf_op jit(solution)/shard_map/ppermute | solution.py:413
  214.2 6.2 %collective-permute-start.21 = (f32[128,768]{1,0:T(8,128)S(1)}, f32[128,768]{1,0:T(8,128)S(1)}, u32[]{:S(2)}, u32[]{:S(2)}) collective-permute-start(f32[128,768]{1,0:T(8,128)S(1)} %collective-permute-done.18.refs_1_), channel_id=1, source_target_pairs={{0,1},{1,0},{2,3},{3,2},{4,5},{5,4},{16,17},{17,16},{18,19},{19,18... | collective-permute-start | bytes 1179656 | tf_op jit(solution)/shard_map/ppermute | solution.py:413
  220.4 2.5 %collective-permute-done.19.refs_2_ = f32[128,768]{1,0:T(8,128)S(1)} collective-permute-done((f32[128,768]{1,0:T(8,128)S(1)}, f32[128,768]{1,0:T(8,128)S(1)}, u32[]{:S(2)}, u32[]{:S(2)}) %collective-permute-start.19) | collective-permute-done | bytes 393248 | tf_op jit(solution)/shard_map/ppermute | solution.py:411
  222.9 5.3 %collective-permute-start.22 = (f32[128,768]{1,0:T(8,128)S(1)}, f32[128,768]{1,0:T(8,128)S(1)}, u32[]{:S(2)}, u32[]{:S(2)}) collective-permute-start(f32[128,768]{1,0:T(8,128)S(1)} %collective-permute-done.19.refs_2_), channel_id=1, source_target_pairs={{0,1},{1,0},{2,3},{3,2},{4,5},{5,4},{16,17},{17,16},{18,19},{19,18... | collective-permute-start | bytes 1179656 | tf_op jit(solution)/shard_map/ppermute | solution.py:413
  229.5 3.0 %patch.1._ = f32[18,9,128,128]{3,2,1,0:T(8,128)} custom-call(s32[4]{0:T(128)} %add_convert_fusion.info, f32[128,1152]{1,0:T(8,128)} %add_select_fusion.refs_0_, f32[128,1152]{1,0:T(8,128)} %select_select_fusion.refs_0_.refs_1_, f32[128,1152]{1,0:T(8,128)} %broadcast_select_fusion.1.refs_1_.refs_2_, ...), custom_call_target="tpu_custom_call", output_to_operand_aliasing={{}: (4, {})} | custom-call | flops 100000000 | bytes 4000000 | tf_op jit(solution)/shard_map/patch/pallas_call | solution.py:275
  234.3 6.0 %corner.1.block_ref = f32[128,128]{1,0:T(8,128)} custom-call(s32[9]{0:T(128)} %stack.83.info, s32[6,6]{1,0:T(8,128)} %slice.35.live, f32[128,768]{1,0:T(8,128)} %copy-done.5, f32[128,768]{1,0:T(8,128)} %copy-done.7, f32[128,768]{1,0:T(8,128)} %copy-done.8, f32[128,768]{1,0:T(8,128)} %copy-done.9, f32[128,768]{1,0:T(8,128)} %copy-done.10, ...), custom_call_target="tpu_custom_call" | custom-call | flops 1000000000 | bytes 1000000 | tf_op jit(solution)/shard_map/corner/pallas_call | solution.py:209
  240.3 1.5 patch_first.1
  (69 shorter events, 10.7 us)
Async XLA Ops:
  1.0 3.5 %collective-permute-start = (bf16[1,6,64,128]{3,2,1,0:T(8,128)(2,1)S(1)}, bf16[1,6,64,128]{3,2,1,0:T(8,128)(2,1)S(1)}, u32[]{:S(2)}, u32[]{:S(2)}) collective-permute-start(bf16[1,6,64,128]{3,2,1,0:T(8,128)(2,1)S(1)} %dynamic-slice_bitcast_fusion), channel_id=1, source_target_pairs={{0,16},{16,0},{32,48},{48,32},{64,80},{80,64},{96,112},{112,96},{1... | collective-permute-start | bytes 294920 | tf_op jit(solution)/shard_map/ppermute | solution.py:344
  2.5 14.2 %copy-start.13 = (s32[144,6]{0,1:T(8,128)}, s32[144,6]{0,1:T(8,128)S(1)}, u32[]{:S(2)}) copy-start(s32[144,6]{0,1:T(8,128)S(1)} %copy.14) | copy-start | bytes 10372
  4.5 7.3 %collective-permute-start.1 = (bf16[2,6,64,128]{3,2,1,0:T(8,128)(2,1)S(1)}, bf16[2,6,64,128]{3,2,1,0:T(8,128)(2,1)S(1)}, u32[]{:S(2)}, u32[]{:S(2)}) collective-permute-start(bf16[2,6,64,128]{3,2,1,0:T(8,128)(2,1)S(1)} %maximum_select_fusion), channel_id=1, source_target_pairs={{0,32},{16,48},{32,64},{48,80},{64,96},{80,112},{96,0},{112,16},{1... | collective-permute-start | bytes 589832 | tf_op jit(solution)/shard_map/ppermute | solution.py:345
  6.3 10.4 %collective-permute-start.2 = (bf16[2,6,64,128]{3,2,1,0:T(8,128)(2,1)S(1)}, bf16[2,6,64,128]{3,2,1,0:T(8,128)(2,1)S(1)}, u32[]{:S(2)}, u32[]{:S(2)}) collective-permute-start(bf16[2,6,64,128]{3,2,1,0:T(8,128)(2,1)S(1)} %maximum_select_fusion), channel_id=1, source_target_pairs={{0,64},{16,80},{32,96},{48,112},{64,0},{80,16},{96,32},{112,48},{1... | collective-permute-start | bytes 589832 | tf_op jit(solution)/shard_map/ppermute | solution.py:345
  9.6 7.1 %collective-permute-start.3 = (bf16[2,6,64,128]{3,2,1,0:T(8,128)(2,1)S(1)}, bf16[2,6,64,128]{3,2,1,0:T(8,128)(2,1)S(1)}, u32[]{:S(2)}, u32[]{:S(2)}) collective-permute-start(bf16[2,6,64,128]{3,2,1,0:T(8,128)(2,1)S(1)} %maximum_select_fusion), channel_id=1, source_target_pairs={{0,96},{16,112},{32,0},{48,16},{64,32},{80,48},{96,64},{112,80},{1... | collective-permute-start | bytes 589832 | tf_op jit(solution)/shard_map/ppermute | solution.py:345
  10.4 21.6 %copy-start.12 = (s32[18,6]{1,0:T(8,128)}, s32[18,6]{1,0:T(8,128)S(1)}, u32[]{:S(2)}) copy-start(s32[18,6]{1,0:T(8,128)S(1)} %fusion.7.live) | copy-start | bytes 1300
  16.8 13.9 %copy-start = (bf16[6,6,64,128]{3,2,1,0:T(8,128)(2,1)}, bf16[6,6,64,128]{3,2,1,0:T(8,128)(2,1)S(1)}, u32[]{:S(2)}) copy-start(bf16[6,6,64,128]{3,2,1,0:T(8,128)(2,1)S(1)} %pad_maximum_fusion.refs_2_.refs_6_) | copy-start | bytes 1769476
  16.8 29.1 %collective-permute-start.4 = (bf16[6,6,64,128]{3,2,1,0:T(8,128)(2,1)S(1)}, bf16[6,6,64,128]{3,2,1,0:T(8,128)(2,1)S(1)}, u32[]{:S(2)}, u32[]{:S(2)}) collective-permute-start(bf16[6,6,64,128]{3,2,1,0:T(8,128)(2,1)S(1)} %pad_maximum_fusion.refs_2_.refs_6_), channel_id=1, source_target_pairs={{0,1},{1,0},{2,3},{3,2},{4,5},{5,4},{6,7},{7,6},{8,9},{9,8},{10,11... | collective-permute-start | bytes 1769480 | tf_op jit(solution)/shard_map/ppermute | solution.py:351
  45.9 0.8 copy-start.4
  54.1 32.1 %copy-start.6 = (f32[128,1152]{1,0:T(8,128)S(1)}, f32[128,1152]{1,0:T(8,128)}, u32[]{:S(2)}) copy-start(f32[128,1152]{1,0:T(8,128)} %get-tuple-element.21) | copy-start | bytes 1769476
  54.1 28.9 %collective-permute-start.6 = (f32[2,128,1152]{2,1,0:T(8,128)}, f32[2,128,1152]{2,1,0:T(8,128)S(1)}, u32[]{:S(2)}, u32[]{:S(2)}) collective-permute-start(f32[2,128,1152]{2,1,0:T(8,128)} %get-tuple-element.20), channel_id=1, source_target_pairs={{0,32},{16,48},{32,64},{48,80},{64,96},{80,112},{96,0},{112,16},{1... | collective-permute-start | bytes 3538952 | tf_op jit(solution)/shard_map/ppermute | solution.py:374
  55.0 31.2 %collective-permute-start.5 = (f32[2,128,1152]{2,1,0:T(8,128)}, f32[2,128,1152]{2,1,0:T(8,128)S(1)}, u32[]{:S(2)}, u32[]{:S(2)}) collective-permute-start(f32[2,128,1152]{2,1,0:T(8,128)} %get-tuple-element.18), channel_id=1, source_target_pairs={{0,96},{16,112},{32,0},{48,16},{64,32},{80,48},{96,64},{112,80},{1... | collective-permute-start | bytes 3538952 | tf_op jit(solution)/shard_map/ppermute | solution.py:375
  84.1 18.1 %copy-start.1 = (f32[2,128,1152]{2,1,0:T(8,128)S(1)}, f32[2,128,1152]{2,1,0:T(8,128)}, u32[]{:S(2)}) copy-start(f32[2,128,1152]{2,1,0:T(8,128)} %get-tuple-element.17) | copy-start | bytes 3538948
  84.1 17.3 %collective-permute-start.7 = (f32[128,1152]{1,0:T(8,128)S(1)}, f32[128,1152]{1,0:T(8,128)S(1)}, u32[]{:S(2)}, u32[]{:S(2)}) collective-permute-start(f32[128,1152]{1,0:T(8,128)S(1)} %fusion.3), channel_id=1, source_target_pairs={{0,32},{16,48},{32,64},{48,80},{96,0},{112,16},{1,33},{17,49},{33,... | collective-permute-start | bytes 1769480 | tf_op jit(solution)/shard_map/ppermute | solution.py:376
  86.3 15.9 %collective-permute-start.8 = (f32[128,1152]{1,0:T(8,128)S(1)}, f32[128,1152]{1,0:T(8,128)S(1)}, u32[]{:S(2)}, u32[]{:S(2)}) collective-permute-start(f32[128,1152]{1,0:T(8,128)S(1)} %fusion), channel_id=1, source_target_pairs={{32,0},{48,16},{64,32},{80,48},{96,64},{112,80},{33,1},{49,17},{65... | collective-permute-start | bytes 1769480 | tf_op jit(solution)/shard_map/ppermute | solution.py:377
  101.4 1.8 copy-start.2
  102.2 1.0 copy-start.3
  102.2 3.4 %copy-start.14 = (s32[144,6]{0,1:T(8,128)S(1)}, s32[144,6]{0,1:T(8,128)}, u32[]{:S(2)}) copy-start(s32[144,6]{0,1:T(8,128)} %copy-done.13) | copy-start | bytes 10372
  103.2 15.4 %collective-permute-start.9 = (f32[128,1152]{1,0:T(8,128)}, f32[128,1152]{1,0:T(8,128)}, u32[]{:S(2)}, u32[]{:S(2)}) collective-permute-start(f32[128,1152]{1,0:T(8,128)} %broadcast_select_fusion), channel_id=1, source_target_pairs={{0,16},{16,0},{32,48},{48,32},{64,80},{80,64},{1,17},{17,1},{33,49... | collective-permute-start | bytes 1769480 | tf_op jit(solution)/shard_map/ppermute | solution.py:380
  121.0 3.7 %collective-permute-start.11 = (f32[128,1152]{1,0:T(8,128)}, f32[128,1152]{1,0:T(8,128)S(1)}, u32[]{:S(2)}, u32[]{:S(2)}) collective-permute-start(f32[128,1152]{1,0:T(8,128)} %add_select_fusion.refs_0_), channel_id=1, source_target_pairs={{64,0},{65,16},{66,32},{67,48},{68,68},{69,84},{70,100},{71,116},{... | collective-permute-start | bytes 1769480 | tf_op jit(solution)/shard_map/ppermute | solution.py:395
  121.7 13.3 %collective-permute-start.10 = (f32[128,1152]{1,0:T(8,128)}, f32[128,1152]{1,0:T(8,128)S(1)}, u32[]{:S(2)}, u32[]{:S(2)}) collective-permute-start(f32[128,1152]{1,0:T(8,128)} %add_select_fusion.refs_0_), channel_id=1, source_target_pairs={{0,0},{1,16},{2,32},{3,48},{4,68},{5,84},{6,100},{7,116},{8,8},{9,... | collective-permute-start | bytes 1769480 | tf_op jit(solution)/shard_map/ppermute | solution.py:394
  135.1 2.7 %collective-permute-start.12 = (f32[128,1152]{1,0:T(8,128)S(1)}, f32[128,1152]{1,0:T(8,128)S(1)}, u32[]{:S(2)}, u32[]{:S(2)}) collective-permute-start(f32[128,1152]{1,0:T(8,128)S(1)} %broadcast_select_fusion.2), channel_id=1, source_target_pairs={{0,4},{16,20},{32,36},{48,52},{1,5},{17,21},{33,37},{49,53},{68,64... | collective-permute-start | bytes 1769480 | tf_op jit(solution)/shard_map/ppermute | solution.py:400
  135.8 12.1 %collective-permute-start.13 = (f32[128,1152]{1,0:T(8,128)S(1)}, f32[128,1152]{1,0:T(8,128)S(1)}, u32[]{:S(2)}, u32[]{:S(2)}) collective-permute-start(f32[128,1152]{1,0:T(8,128)S(1)} %collective-permute-done.10), channel_id=1, source_target_pairs={{8,0},{24,16},{40,32},{56,48},{76,64},{92,80},{108,96},{124,112},{... | collective-permute-start | bytes 1769480 | tf_op jit(solution)/shard_map/ppermute | solution.py:396
  137.1 10.8 %collective-permute-start.14 = (f32[128,1152]{1,0:T(8,128)S(1)}, f32[128,1152]{1,0:T(8,128)S(1)}, u32[]{:S(2)}, u32[]{:S(2)}) collective-permute-start(f32[128,1152]{1,0:T(8,128)S(1)} %collective-permute-done.11), channel_id=1, source_target_pairs={{8,4},{24,20},{40,36},{56,52},{76,68},{92,84},{108,100},{124,116},... | collective-permute-start | bytes 1769480 | tf_op jit(solution)/shard_map/ppermute | solution.py:397
  153.1 21.8 %collective-permute-start.15 = (f32[128,768]{1,0:T(8,128)}, f32[128,768]{1,0:T(8,128)S(1)}, u32[]{:S(2)}, u32[]{:S(2)}) collective-permute-start(f32[128,768]{1,0:T(8,128)} %column.1), channel_id=1, source_target_pairs={{0,16},{1,17},{2,18},{3,19},{4,20},{5,21},{16,0},{17,1},{18,2},{19... | collective-permute-start | bytes 1179656 | tf_op jit(solution)/shard_map/ppermute | solution.py:410
  176.0 12.5 %collective-permute-start.16 = (f32[128,768]{1,0:T(8,128)S(1)}, f32[128,768]{1,0:T(8,128)S(1)}, u32[]{:S(2)}, u32[]{:S(2)}) collective-permute-start(f32[128,768]{1,0:T(8,128)S(1)} %add.178), channel_id=1, source_target_pairs={{0,32},{1,33},{2,34},{3,35},{4,36},{5,37},{16,48},{17,49},{18,50},... | collective-permute-start | bytes 1179656 | tf_op jit(solution)/shard_map/ppermute | solution.py:410
  188.5 12.9 %collective-permute-start.17 = (f32[128,768]{1,0:T(8,128)S(1)}, f32[128,768]{1,0:T(8,128)S(1)}, u32[]{:S(2)}, u32[]{:S(2)}) collective-permute-start(f32[128,768]{1,0:T(8,128)S(1)} %add.179), channel_id=1, source_target_pairs={{0,96},{1,97},{2,98},{3,99},{4,100},{5,101},{16,112},{17,113},{18,... | collective-permute-start | bytes 1179656 | tf_op jit(solution)/shard_map/ppermute | solution.py:410
  201.5 31.1 %copy-start.5 = (f32[128,768]{1,0:T(8,128)}, f32[128,768]{1,0:T(8,128)S(1)}, u32[]{:S(2)}) copy-start(f32[128,768]{1,0:T(8,128)S(1)} %add.180.refs_0_) | copy-start | bytes 1179652
  201.5 12.7 %collective-permute-start.18 = (f32[128,768]{1,0:T(8,128)S(1)}, f32[128,768]{1,0:T(8,128)S(1)}, u32[]{:S(2)}, u32[]{:S(2)}) collective-permute-start(f32[128,768]{1,0:T(8,128)S(1)} %add.180.refs_0_), channel_id=1, source_target_pairs={{0,2},{1,3},{2,4},{3,5},{4,0},{5,1},{16,18},{17,19},{18,20},{19,21... | collective-permute-start | bytes 1179656 | tf_op jit(solution)/shard_map/ppermute | solution.py:411
  207.3 15.6 %collective-permute-start.19 = (f32[128,768]{1,0:T(8,128)S(1)}, f32[128,768]{1,0:T(8,128)S(1)}, u32[]{:S(2)}, u32[]{:S(2)}) collective-permute-start(f32[128,768]{1,0:T(8,128)S(1)} %add.180.refs_0_), channel_id=1, source_target_pairs={{0,4},{1,5},{2,0},{3,1},{4,2},{5,3},{16,20},{17,21},{18,16},{19,17... | collective-permute-start | bytes 1179656 | tf_op jit(solution)/shard_map/ppermute | solution.py:411
  209.5 23.1 %collective-permute-start.20 = (f32[128,768]{1,0:T(8,128)S(1)}, f32[128,768]{1,0:T(8,128)S(1)}, u32[]{:S(2)}, u32[]{:S(2)}) collective-permute-start(f32[128,768]{1,0:T(8,128)S(1)} %add.180.refs_0_), channel_id=1, source_target_pairs={{0,1},{1,0},{2,3},{3,2},{4,5},{5,4},{16,17},{17,16},{18,19},{19,18... | collective-permute-start | bytes 1179656 | tf_op jit(solution)/shard_map/ppermute | solution.py:413
  214.2 18.4 %copy-start.7 = (f32[128,768]{1,0:T(8,128)}, f32[128,768]{1,0:T(8,128)S(1)}, u32[]{:S(2)}) copy-start(f32[128,768]{1,0:T(8,128)S(1)} %collective-permute-done.18.refs_1_) | copy-start | bytes 1179652
  214.2 18.4 %collective-permute-start.21 = (f32[128,768]{1,0:T(8,128)S(1)}, f32[128,768]{1,0:T(8,128)S(1)}, u32[]{:S(2)}, u32[]{:S(2)}) collective-permute-start(f32[128,768]{1,0:T(8,128)S(1)} %collective-permute-done.18.refs_1_), channel_id=1, source_target_pairs={{0,1},{1,0},{2,3},{3,2},{4,5},{5,4},{16,17},{17,16},{18,19},{19,18... | collective-permute-start | bytes 1179656 | tf_op jit(solution)/shard_map/ppermute | solution.py:413
  222.9 9.7 %copy-start.8 = (f32[128,768]{1,0:T(8,128)}, f32[128,768]{1,0:T(8,128)S(1)}, u32[]{:S(2)}) copy-start(f32[128,768]{1,0:T(8,128)S(1)} %collective-permute-done.19.refs_2_) | copy-start | bytes 1179652
  222.9 9.7 %collective-permute-start.22 = (f32[128,768]{1,0:T(8,128)S(1)}, f32[128,768]{1,0:T(8,128)S(1)}, u32[]{:S(2)}, u32[]{:S(2)}) collective-permute-start(f32[128,768]{1,0:T(8,128)S(1)} %collective-permute-done.19.refs_2_), channel_id=1, source_target_pairs={{0,1},{1,0},{2,3},{3,2},{4,5},{5,4},{16,17},{17,16},{18,19},{19,18... | collective-permute-start | bytes 1179656 | tf_op jit(solution)/shard_map/ppermute | solution.py:413
  232.6 0.8 copy-start.9
  232.6 0.9 copy-start.10
  233.5 0.8 copy-start.11

commit v2 on v1

--- a/solution.py
+++ b/solution.py
@@ -8,6 +8,7 @@
 
 F32, BF16 = jnp.float32, jnp.bfloat16
 PARTS = ((0, 8), (8, 10))
+SIZES = (3, 4, 4)
 VMEM = pl.BlockSpec(memory_space=pltpu.VMEM)
 SMEM = pl.BlockSpec(memory_space=pltpu.SMEM)
 ANY = pl.BlockSpec(memory_space=pl.ANY)
@@ -91,7 +92,8 @@
 
 
 def eliminate_kernel(take, live, *refs):
-    *part_refs, u_ref, v_ref, up_ref, down_ref, up2_ref, down2_ref, own_ref, w_ref = refs
+    *part_refs, u_ref, v_ref = refs[: -2 * len(SIZES) - 1]
+    places, w_ref = refs[-2 * len(SIZES) - 1 : -1], refs[-1]
     steps = w_ref.shape[0]
     high, low = [], []
     for k in reversed(range(steps)):
@@ -101,7 +103,7 @@
         if high:
             blocks = []
             for j in range(k + 1, steps):
-                block = stacked(take[8], u_ref[j, k], v_ref[j, k])
+                block = stacked(take[0], u_ref[j, k], v_ref[j, k])
                 blocks.append(jnp.where(live[j, k] > 0, block, jnp.zeros_like(block)).T)
             left = jnp.concatenate(blocks + blocks, axis=1)
             total = total + dot(left, jnp.concatenate(high[::-1] + low[::-1], axis=0))
@@ -110,28 +112,75 @@
         a, b = halves(total)
         high.append(a)
         low.append(b)
-    places = [up_ref.at[0], up_ref.at[1], down_ref.at[0], down_ref.at[1], up2_ref, down2_ref, own_ref.at[0], own_ref.at[1]]
-    for n, place in enumerate(places):
-        place[...] = w_ref[take[n]]
+    at = 1
+    for n, ref in enumerate(places):
+        count, _, wide = ref.shape
+        for m in range(count):
+            ref[m] = w_ref[take[at], :, pl.ds(n // 2 * wide, wide)]
+            at += 1
 
 
 def eliminate(parts, corner, live, take):
     _, width, wide = parts[0].shape
-    one = jax.ShapeDtypeStruct((width, wide), F32)
-    two = jax.ShapeDtypeStruct((2, width, wide), F32)
+    shapes = [jax.ShapeDtypeStruct((n, width, wide // len(SIZES)), F32) for n in SIZES for _ in range(2)]
     return pl.pallas_call(
         eliminate_kernel,
         in_specs=[SMEM, SMEM] + [VMEM] * (len(parts) + 2),
-        out_specs=[VMEM] * 5,
-        out_shape=[two, two, one, one, two],
+        out_specs=[VMEM] * len(shapes),
+        out_shape=shapes,
         scratch_shapes=[pltpu.VMEM(parts[0].shape, F32)],
         cost_estimate=pl.CostEstimate(flops=1000 * parts[0].size, bytes_accessed=20 * parts[0].size, transcendentals=0),
         name="eliminate",
     )(take, live, *parts, *corner)
 
 
+def halving_kernel(take, *refs):
+    given, places = refs[: len(refs) // 2], refs[len(refs) // 2 :]
+    at = 0
+    for n, ref in enumerate(places):
+        stay_ref, came_ref = given[n // 2 * 2], given[n // 2 * 2 + 1]
+        for m in range(ref.shape[0]):
+            ref[m] = stay_ref[take[at]] + came_ref[take[at]]
+            at += 1
+
+
+def halving(take, count, given):
+    _, width, wide = given[0].shape
+    shapes = [jax.ShapeDtypeStruct((count, width, wide), F32)] * len(given)
+    return pl.pallas_call(
+        halving_kernel,
+        in_specs=[SMEM] + [VMEM] * len(given),
+        out_specs=[VMEM] * len(given),
+        out_shape=shapes,
+        cost_estimate=pl.CostEstimate(flops=10**8, bytes_accessed=16 * width * wide * len(given), transcendentals=0),
+        name="halving",
+    )(take, *given)
+
+
+def row_kernel(live, *refs):
+    *given, row_ref = refs
+    width = row_ref.shape[0]
+    count = given[0].shape[2] // width
+    for n in range(row_ref.shape[1] // width):
+        part = pl.ds(n % count * width, width)
+        value = given[n // count * 2][0, :, part] + given[n // count * 2 + 1][0, :, part]
+        row_ref[:, pl.ds(n * width, width)] = jnp.where(live[n] > 0, value, jnp.zeros_like(value))
+
+
+def masked_row(live, given):
+    _, width, wide = given[0].shape
+    return pl.pallas_call(
+        row_kernel,
+        in_specs=[SMEM] + [VMEM] * len(given),
+        out_specs=VMEM,
+        out_shape=jax.ShapeDtypeStruct((width, wide * len(given) // 2), F32),
+        cost_estimate=pl.CostEstimate(flops=10**7, bytes_accessed=8 * width * wide * len(given), transcendentals=0),
+        name="row",
+    )(live, *given)
+
+
 def column_kernel(live, *refs):
-    *value_refs, u_ref, out_ref = refs
+    *value_refs, u_ref, upper_ref, lower_ref = refs
     _, steps, width, _ = u_ref.shape
     total, a = None, 0
     for even_ref, odd_ref in zip(value_refs[::2], value_refs[1::2]):
@@ -150,7 +199,8 @@
             total = term if total is None else total + term
             a += 2
     total = total[:width] + total[width:]
-    out_ref[...] = total
+    upper_ref[...] = total[: width // 2]
+    lower_ref[...] = total[width // 2 :]
 
 
 def column_products(values, lower, live):
@@ -158,8 +208,8 @@
     return pl.pallas_call(
         column_kernel,
         in_specs=[SMEM] + [VMEM] * (len(values) + 1),
-        out_specs=VMEM,
-        out_shape=jax.ShapeDtypeStruct((width, steps * width), F32),
+        out_specs=[VMEM] * 2,
+        out_shape=[jax.ShapeDtypeStruct((width // 2, steps * width), F32)] * 2,
         cost_estimate=pl.CostEstimate(flops=4 * row_blocks * steps * width**3, bytes_accessed=6 * 10**6, transcendentals=0),
         name="column",
     )(live, *values, lower)
@@ -350,8 +400,6 @@
     corner = jnp.concatenate(corner)
     corner = corner, lax.ppermute(corner, "pcol", flip_core)
 
-    n_dest = steps // 2
-
     both, grid = ("prow", "pcol"), [(x, h, c) for x in range(n_col // 4) for h in range(2) for c in range(2)]
 
     def device(x, h, c, zz, yy):
@@ -362,24 +410,53 @@
         whole, part = products(blocks, lower, live, whole, first, count)
         parts.append(part)
 
-    def near(shift):
-        return [(s, d) for s, d in ring(shift) if d < steps]
-
-    def slot(zz, par):
-        return jnp.minimum(zz % n_z, n_dest - 1) * 2 + par
-
-    take = [slot(z + 2, 0), slot(z + 1, 1), slot(z + 2, 1), slot(z - 1, 0)]
-    take += [slot(z + 1, 0), slot(z - 1, 1), slot(z, 0), slot(z, 1), core]
-    up, down, up2, down2, own = eliminate(parts, corner, live_corner, jnp.stack(take).astype(jnp.int32))
-    up = lax.ppermute(up, "prow", ring(1))
-    down = lax.ppermute(down, "prow", ring(-1))
-    up2 = lax.ppermute(up2 + up[0], "prow", near(1))
-    down2 = lax.ppermute(down2 + down[0], "prow", near(-1))
-    even, odd = own[0] + down[1] + up2, own[1] + up[1] + down2
-    keep, give = jnp.where(y == 0, even, odd), jnp.where(y == 0, odd, even)
-    full = keep + lax.ppermute(give, "prow", [(d, d ^ 1) for d in range(steps)])
-    mask = jnp.broadcast_to(row_live[:, None], (cols, width)).reshape(1, cols * width)
-    row = jnp.where(mask, full, jnp.zeros_like(full))
+    outer, low = (z == 0) | (z == n_z - 1), z < 2
+    mine, other = y, 1 - y
+
+    def table(*rows):
+        return jnp.stack([jnp.asarray(v, jnp.int32) for row in rows for v in row])
+
+    def either(flag, yes, no):
+        return [jnp.where(flag, a, b) for a, b in zip(yes, no)]
+
+    ends, middle = (0, 1, 0, 0), (2, 3, 4, 5)
+    front, back = (0, 1, 2, 3), (4, 5, 0, 0)
+    take = table(
+        [core],
+        [other, 2 + other, 4 + other],
+        [mine, 2 + mine, 4 + mine],
+        either(outer, middle, ends),
+        either(outer, ends, middle),
+        either(low, back, front),
+        either(low, front, back),
+    )
+    send_a, keep_a, send_b, keep_b, send_c, keep_c = eliminate(parts, corner, live_corner, take)
+    over_m = [(s, d) for s, d in mirror if d < steps]
+    came_a = lax.ppermute(send_a, "prow", flip_y)
+    came_b = lax.ppermute(send_b, "prow", flip_z)
+    came_c = lax.ppermute(send_c, "prow", mirror)
+    take = table(
+        either(outer, (1, 2), (0, 0)),
+        either(outer, (0, 0), (1, 2)),
+        either(z == 1, (2, 3), (0, 1)),
+        either(z == 2, (2, 3), (0, 1)),
+        either(low, (other, 2 + other), (other, other)),
+        either(low, (mine, 2 + mine), (mine, mine)),
+    )
+    given = [keep_a, came_a, keep_b, came_b, keep_c, came_c]
+    send_a, keep_a, send_b, keep_b, send_c, keep_c = halving(take, 2, given)
+    came_a = lax.ppermute(send_a, "prow", flip_z)
+    came_b = lax.ppermute(send_b, "prow", over_m)
+    came_c = lax.ppermute(send_c, "prow", flip_y)
+    take = table(
+        [jnp.where(z == 1, 1, 0), jnp.where(z == 2, 1, 0), other, mine, jnp.where(z == 0, 1, 0), jnp.where(z == 1, 1, 0)]
+    )
+    given = [keep_a, came_a, keep_b, came_b, keep_c, came_c]
+    send_a, keep_a, send_b, keep_b, send_c, keep_c = halving(take, 1, given)
+    came_a = lax.ppermute(send_a, "prow", over_m)
+    came_b = lax.ppermute(send_b, "prow", [(s, d) for s, d in flip_y if d < steps])
+    came_c = lax.ppermute(send_c, "prow", [(s, d) for s, d in flip_z if d < steps])
+    row = masked_row(row_live.astype(jnp.int32), [keep_a, came_a, keep_b, came_b, keep_c, came_c])
 
     def turn(k, x, h, c):
         return at(k // 2, k % 2) * n_col + x * 4 + h * 2 + c, device(x, k // 2 % 2, k % 2, x % 2 * 2 + h, c)
@@ -401,14 +478,26 @@
     mine = jnp.where(x == 0, first, second)
     values = [row, jnp.where(x == z // 2, mine, moved), jnp.where(x == 0, odd0, odd1)]
 
-    sums = column_products(values[1:], lower, live)
+    upper, under = column_products(values[1:], lower, live)
 
     def here(perm):
         return [(s * n_col + d, t * n_col + d) for s, t in perm for d in range(steps)]
 
-    for perm in (flip_y, flip_z, mirror):
-        sums = sums + lax.ppermute(sums, both, here(perm))
-    turns = [lax.ppermute(sums, "pcol", [(d, (d + t) % steps) for d in range(steps)]) for t in (2, 4)]
+    orders = (flip_y, flip_z), (flip_z, mirror), (mirror, flip_y)
+    for (one, two) in orders:
+        came = lax.ppermute(upper, both, here(one)), lax.ppermute(under, both, here(two))
+        upper, under = upper + came[0], under + came[1]
+    sums = jnp.concatenate([upper, under])
+
+    def around(t):
+        route = []
+        for d in range(steps):
+            to = (d + t) % steps
+            flip = d // 2 % 2 ^ to // 2 % 2
+            route += [(s * n_col + d, (s ^ flip) * n_col + to) for s in range(n_row)]
+        return route
+
+    turns = [lax.ppermute(sums, both, around(t)) for t in (2, 4)]
     sums = [sums, *turns]
     sums += [lax.ppermute(v, "pcol", [(d, d ^ 1) for d in range(steps)]) for v in sums]
     slots = [(q + steps - t) % steps for t in (0, 2, 4)]

time: 243 us -> 226 us (0.930)
  waiting for transfers between devices: 112 us -> 68.4 us
  starting transfers between devices: 65.1 us -> 83 us
  Pallas kernels: 45.6 us -> 54.3 us
  other arithmetic: 9.78 us -> 5.66 us
  local copies, waits for them, and re-layouts: 9.22 us -> 12.2 us
    ppermute x10 -> x17, waiting for transfers between devices: 84.8 us -> 43.4 us  [the longest x1 13.5 us: per_device(): came_a = lax.ppermute(send_a, 'prow', flip_y)]
    ppermute x10 -> x17, starting transfers between devices: 33.2 us -> 51.5 us  [the longest x3 18.8 us: per_device(): lax.ppermute(upper, both, here(one))]
    pallas_call x0 -> x3, Pallas kernels: none -> 8.88 us  [the longest x2 6.65 us: halving(): pl.pallas_call(halving_kernel, in_specs=[SMEM] + [VMEM] * len(given), out...]
    select_n x2 -> x0, other arithmetic: 3.46 us -> none  [the longest x1 2.42 us: per_device(): row = jnp.where(mask, full, jnp.zeros_like(full))]
    unnamed x30 -> x36, local copies, waits for them, and re-layouts: 2.46 us -> 4.94 us
  transfers between devices with their start and end apart: 23 -> 30, of which waited for: 13 -> 15; matrix products, arithmetic and copies ran while one was open for 4% -> 5% of each run, Pallas kernels for 11% -> 12%
where the time goes in v2:
time: 226 us; the launch traced here: 224 us
  starting transfers between devices  83 us (37%)
  waiting for transfers between devices  68.4 us (30%)
  Pallas kernels  54.3 us (24%)
  local copies, waits for them, and re-layouts  12.2 us (5%)
  other arithmetic  5.66 us (3%)
    pallas_call x2, Pallas kernels, products(): pl.pallas_call(product_kernel, grid_spec=pltpu.PrefetchScalarGridSpec(num...  23.5 us
    ppermute x3, starting transfers between devices, per_device(): lax.ppermute(upper, both, here(one))  18.8 us
    ppermute x3, starting transfers between devices, per_device(): lax.ppermute(v, 'pcol', [(d, d ^ 1) for d in range(steps)])  14 us
    ppermute x1, waiting for transfers between devices, per_device(): came_a = lax.ppermute(send_a, 'prow', flip_y)  13.5 us
    ppermute x3, starting transfers between devices, per_device(): lax.ppermute(under, both, here(two))  12.7 us
    ppermute x1, waiting for transfers between devices, per_device(): lax.ppermute(first, both, [slide(pl_, pl_[2] // 2 + 2, 0) for pl_ in plac...  9 us
    ppermute x1, waiting for transfers between devices, per_device(): lax.ppermute(row, both, [turn(k, *place) for k in range(4) for place in g...  8.78 us
    ppermute x2, starting transfers between devices, per_device(): turns = [lax.ppermute(sums, both, around(t)) for t in (2, 4)]  8.17 us
  transfers between devices with their start and end apart: 30, of which 15 were waited for; matrix products, arithmetic and copies ran while one was open for 5% of the time, Pallas kernels for 12%

profile of v2, /device:TPU:25, one launch (start us, length us, event | category | flops | bytes accessed | tf_op | source)
XLA Modules:
  0.0 224.3 jit_solution(15687212461158873113)
XLA Ops:
  3.0 1.6 collective-permute-done
  4.5 1.7 collective-permute-start.1
  6.3 3.3 %collective-permute-start.2 = (bf16[2,6,64,128]{3,2,1,0:T(8,128)(2,1)S(1)}, bf16[2,6,64,128]{3,2,1,0:T(8,128)(2,1)S(1)}, u32[]{:S(2)}, u32[]{:S(2)}) collective-permute-start(bf16[2,6,64,128]{3,2,1,0:T(8,128)(2,1)S(1)} %maximum_select_fusion), channel_id=1, source_target_pairs={{0,64},{16,80},{32,96},{48,112},{64,0},{80,16},{96,32},{112,48},{1... | collective-permute-start | bytes 589832 | tf_op jit(solution)/shard_map/ppermute | solution.py:395
  11.8 4.8 %collective-permute-done.2 = bf16[2,6,64,128]{3,2,1,0:T(8,128)(2,1)S(1)} collective-permute-done((bf16[2,6,64,128]{3,2,1,0:T(8,128)(2,1)S(1)}, bf16[2,6,64,128]{3,2,1,0:T(8,128)(2,1)S(1)}, u32[]{:S(2)}, u32[]{:S(2)}) %collective-permute-start.2) | collective-permute-done | bytes 196640 | tf_op jit(solution)/shard_map/ppermute | solution.py:395
  16.8 3.1 %collective-permute-start.4 = (bf16[6,6,64,128]{3,2,1,0:T(8,128)(2,1)S(1)}, bf16[6,6,64,128]{3,2,1,0:T(8,128)(2,1)S(1)}, u32[]{:S(2)}, u32[]{:S(2)}) collective-permute-start(bf16[6,6,64,128]{3,2,1,0:T(8,128)(2,1)S(1)} %pad_maximum_fusion.refs_2_.refs_6_), channel_id=1, source_target_pairs={{0,1},{1,0},{2,3},{3,2},{4,5},{5,4},{6,7},{7,6},{8,9},{9,8},{10,11... | collective-permute-start | bytes 1769480 | tf_op jit(solution)/shard_map/ppermute | solution.py:401
  19.9 10.8 %products.2 = (f32[18,9,128,128]{3,2,1,0:T(8,128)}, f32[6,128,1152]{2,1,0:T(8,128)}) custom-call(s32[8,6]{1,0:T(8,128)} %slice.22.live, f32[18,9,128,128]{3,2,1,0:T(8,128)} %bitcast.64, bf16[18,6,128,128]{3,2,1,0:T(8,128)(2,1)} %bitcast.66), custom_call_target="tpu_custom_call" | custom-call | flops 3623878656 | bytes 9437184 | tf_op jit(solution)/shard_map/products/pallas_call | solution.py:67
  30.7 1.3 slice.17.live
  33.2 12.7 %products.3 = (f32[18,9,128,128]{3,2,1,0:T(8,128)}, f32[6,128,1152]{2,1,0:T(8,128)}) custom-call(s32[10,6]{1,0:T(8,128)} %slice.23.live, f32[18,9,128,128]{3,2,1,0:T(8,128)} %bitcast.65, bf16[18,6,128,128]{3,2,1,0:T(8,128)(2,1)} %bitcast.67, f32[18,9,128,128]{3,2,1,0:T(8,128)} %get-tuple-element.30.refs_0_), custom_call_target="tpu_custom_call", output_to_operand_aliasing={{0}: (3, {})} | custom-call | flops 4529848320 | bytes 11796480 | tf_op jit(solution)/shard_map/products/pallas_call | solution.py:67
  46.7 7.2 %eliminate.1 = (f32[3,128,384]{2,1,0:T(8,128)}, f32[3,128,384]{2,1,0:T(8,128)}, f32[4,128,384]{2,1,0:T(8,128)}, f32[4,128,384]{2,1,0:T(8,128)}, f32[4,128,384]{2,1,0:T(8,128)}, /*index=5*/f32[4,128,384]{2,1,0:T(8,128)}) custom-call(s32[23]{0:T(128)} %stack.207.take, s32[6,6]{1,0:T(8,128)} %slice.17.live, f32[6,128,1152]{2,1,0:T(8,128)} %get-tuple-element.29.refs_0_, ...), custom_call_target="tpu_custom_call" | custom-call | flops 884736000 | bytes 17694720 | tf_op jit(solution)/shard_map/eliminate/pallas_call | solution.py:126
  54.8 1.3 collective-permute-start.7
  57.2 13.5 %collective-permute-done.5.refs_1_ = f32[3,128,384]{2,1,0:T(8,128)S(1)} collective-permute-done((f32[3,128,384]{2,1,0:T(8,128)}, f32[3,128,384]{2,1,0:T(8,128)S(1)}, u32[]{:S(2)}, u32[]{:S(2)}) %collective-permute-start.5) | collective-permute-done | bytes 589856 | tf_op jit(solution)/shard_map/ppermute | solution.py:435
  70.7 2.5 %collective-permute-done.6.refs_3_ = f32[4,128,384]{2,1,0:T(8,128)S(1)} collective-permute-done((f32[4,128,384]{2,1,0:T(8,128)}, f32[4,128,384]{2,1,0:T(8,128)S(1)}, u32[]{:S(2)}, u32[]{:S(2)}) %collective-permute-start.6) | collective-permute-done | bytes 786464 | tf_op jit(solution)/shard_map/ppermute | solution.py:436
  73.2 1.9 collective-permute-done.7.refs_5_
  76.0 3.9 %halving.2 = (f32[2,128,384]{2,1,0:T(8,128)}, f32[2,128,384]{2,1,0:T(8,128)}, f32[2,128,384]{2,1,0:T(8,128)}, f32[2,128,384]{2,1,0:T(8,128)}, f32[2,128,384]{2,1,0:T(8,128)}, /*index=5*/f32[2,128,384]{2,1,0:T(8,128)}) custom-call(s32[12]{0:T(128)} %stack.188.take, f32[3,128,384]{2,1,0:T(8,128)} %get-tuple-element.32.refs_0_, f32[3,128,384]{2,1,0:T(8,128)} %copy-done.5, ...), custom_call_target="tpu_custom_call" | custom-call | flops 100000000 | bytes 4718592 | tf_op jit(solution)/shard_map/halving/pallas_call | solution.py:150
  79.9 1.3 collective-permute-start.9
  82.6 7.0 %collective-permute-done.8.refs_1_ = f32[2,128,384]{2,1,0:T(8,128)S(1)} collective-permute-done((f32[2,128,384]{2,1,0:T(8,128)}, f32[2,128,384]{2,1,0:T(8,128)S(1)}, u32[]{:S(2)}, u32[]{:S(2)}) %collective-permute-start.8) | collective-permute-done | bytes 393248 | tf_op jit(solution)/shard_map/ppermute | solution.py:448
  89.6 3.1 %collective-permute-done.9.refs_3_ = f32[2,128,384]{2,1,0:T(8,128)S(1)} collective-permute-done((f32[2,128,384]{2,1,0:T(8,128)}, f32[2,128,384]{2,1,0:T(8,128)S(1)}, u32[]{:S(2)}, u32[]{:S(2)}) %collective-permute-start.9) | collective-permute-done | bytes 393248 | tf_op jit(solution)/shard_map/ppermute | solution.py:449
  93.6 2.7 %halving.3 = (f32[1,128,384]{2,1,0:T(8,128)}, f32[1,128,384]{2,1,0:T(8,128)}, f32[1,128,384]{2,1,0:T(8,128)}, f32[1,128,384]{2,1,0:T(8,128)}, f32[1,128,384]{2,1,0:T(8,128)}, /*index=5*/f32[1,128,384]{2,1,0:T(8,128)}) custom-call(s32[6]{0:T(128)} %stack.177.take, f32[2,128,384]{2,1,0:T(8,128)} %get-tuple-element.38.refs_0_, f32[2,128,384]{2,1,0:T(8,128)} %copy-done.11, ...), custom_call_target="tpu_custom_call" | custom-call | flops 100000000 | bytes 4718592 | tf_op jit(solution)/shard_map/halving/pallas_call | solution.py:150
  96.4 1.3 collective-permute-start.11
  97.7 2.4 %collective-permute-start.12 = (f32[1,128,384]{2,1,0:T(8,128)}, f32[1,128,384]{2,1,0:T(8,128)S(1)}, u32[]{:S(2)}, u32[]{:S(2)}) collective-permute-start(f32[1,128,384]{2,1,0:T(8,128)} %get-tuple-element.47), channel_id=1, source_target_pairs={{0,16},{16,0},{32,48},{48,32},{64,80},{80,64},{1,17},{17,1},{33,49... | collective-permute-start | bytes 589832 | tf_op jit(solution)/shard_map/ppermute | solution.py:457
  100.0 3.6 %collective-permute-start.13 = (f32[1,128,384]{2,1,0:T(8,128)}, f32[1,128,384]{2,1,0:T(8,128)S(1)}, u32[]{:S(2)}, u32[]{:S(2)}) collective-permute-start(f32[1,128,384]{2,1,0:T(8,128)} %get-tuple-element.49), channel_id=1, source_target_pairs={{0,32},{16,48},{32,0},{48,16},{96,64},{112,80},{1,33},{17,49},{33,... | collective-permute-start | bytes 589832 | tf_op jit(solution)/shard_map/ppermute | solution.py:458
  104.3 2.8 %collective-permute-done.13.refs_5_ = f32[1,128,384]{2,1,0:T(8,128)S(1)} collective-permute-done((f32[1,128,384]{2,1,0:T(8,128)}, f32[1,128,384]{2,1,0:T(8,128)S(1)}, u32[]{:S(2)}, u32[]{:S(2)}) %collective-permute-start.13) | collective-permute-done | bytes 196640 | tf_op jit(solution)/shard_map/ppermute | solution.py:458
  107.7 2.2 row.1.refs_0_
  110.7 4.5 %collective-permute-start.14 = (f32[128,1152]{1,0:T(8,128)}, f32[128,1152]{1,0:T(8,128)S(1)}, u32[]{:S(2)}, u32[]{:S(2)}) collective-permute-start(f32[128,1152]{1,0:T(8,128)} %row.1.refs_0_), channel_id=1, source_target_pairs={{0,0},{1,16},{2,32},{3,48},{4,68},{5,84},{6,100},{7,116},{8,8},{9,... | collective-permute-start | bytes 1769480 | tf_op jit(solution)/shard_map/ppermute | solution.py:471
  115.2 8.8 %collective-permute-done.14 = f32[128,1152]{1,0:T(8,128)S(1)} collective-permute-done((f32[128,1152]{1,0:T(8,128)}, f32[128,1152]{1,0:T(8,128)S(1)}, u32[]{:S(2)}, u32[]{:S(2)}) %collective-permute-start.14) | collective-permute-done | bytes 589856 | tf_op jit(solution)/shard_map/ppermute | solution.py:471
  124.8 1.3 collective-permute-start.17
  127.9 9.0 %collective-permute-done.17 = f32[128,1152]{1,0:T(8,128)S(1)} collective-permute-done((f32[128,1152]{1,0:T(8,128)S(1)}, f32[128,1152]{1,0:T(8,128)S(1)}, u32[]{:S(2)}, u32[]{:S(2)}) %collective-permute-start.17) | collective-permute-done | bytes 589856 | tf_op jit(solution)/shard_map/ppermute | solution.py:473
  137.8 4.2 %column.1 = (f32[64,768]{1,0:T(8,128)}, f32[64,768]{1,0:T(8,128)}) custom-call(s32[18,6]{1,0:T(8,128)} %copy-done.17, f32[128,1152]{1,0:T(8,128)} %select_select_fusion.refs_0_.refs_1_, f32[128,1152]{1,0:T(8,128)} %broadcast_select_fusion.refs_1_.refs_2_, bf16[18,6,128,128]{3,2,1,0:T(8,128)(2,1)} %bitcast.68), custom_call_target="tpu_custom_call" | custom-call | flops 905969664 | bytes 6000000 | tf_op jit(solution)/shard_map/column/pallas_call | solution.py:208
  142.0 1.9 collective-permute-start.22
  143.9 14.7 %collective-permute-start.19 = (f32[64,768]{1,0:T(8,128)}, f32[64,768]{1,0:T(8,128)S(1)}, u32[]{:S(2)}, u32[]{:S(2)}) collective-permute-start(f32[64,768]{1,0:T(8,128)} %get-tuple-element.50), channel_id=1, source_target_pairs={{0,16},{1,17},{2,18},{3,19},{4,20},{5,21},{16,0},{17,1},{18,2},{19... | collective-permute-start | bytes 589832 | tf_op jit(solution)/shard_map/ppermute | solution.py:488
  158.7 1.0 add.134
  159.6 4.5 %collective-permute-start.23 = (f32[64,768]{1,0:T(8,128)S(1)}, f32[64,768]{1,0:T(8,128)S(1)}, u32[]{:S(2)}, u32[]{:S(2)}) collective-permute-start(f32[64,768]{1,0:T(8,128)S(1)} %add.134), channel_id=1, source_target_pairs={{0,96},{1,97},{2,98},{3,99},{4,100},{5,101},{16,112},{17,113},{18,... | collective-permute-start | bytes 589832 | tf_op jit(solution)/shard_map/ppermute | solution.py:488
  164.1 1.0 add.131
  165.1 2.0 collective-permute-start.20
  167.1 1.5 collective-permute-done.23
  168.6 6.3 %collective-permute-start.24 = (f32[64,768]{1,0:T(8,128)S(1)}, f32[64,768]{1,0:T(8,128)S(1)}, u32[]{:S(2)}, u32[]{:S(2)}) collective-permute-start(f32[64,768]{1,0:T(8,128)S(1)} %add.135), channel_id=1, source_target_pairs={{0,16},{1,17},{2,18},{3,19},{4,20},{5,21},{16,0},{17,1},{18,2},{19... | collective-permute-start | bytes 589832 | tf_op jit(solution)/shard_map/ppermute | solution.py:488
  175.0 2.1 collective-permute-start.21
  177.1 2.8 %collective-permute-done.24 = f32[64,768]{1,0:T(8,128)S(1)} collective-permute-done((f32[64,768]{1,0:T(8,128)S(1)}, f32[64,768]{1,0:T(8,128)S(1)}, u32[]{:S(2)}, u32[]{:S(2)}) %collective-permute-start.24) | collective-permute-done | bytes 196640 | tf_op jit(solution)/shard_map/ppermute | solution.py:488
  179.9 4.0 %collective-permute-done.21 = f32[64,768]{1,0:T(8,128)S(1)} collective-permute-done((f32[64,768]{1,0:T(8,128)S(1)}, f32[64,768]{1,0:T(8,128)S(1)}, u32[]{:S(2)}, u32[]{:S(2)}) %collective-permute-start.21) | collective-permute-done | bytes 196640 | tf_op jit(solution)/shard_map/ppermute | solution.py:488
  184.0 6.3 %collective-permute-start.25 = (f32[128,768]{1,0:T(8,128)S(1)}, f32[128,768]{1,0:T(8,128)S(1)}, u32[]{:S(2)}, u32[]{:S(2)}) collective-permute-start(f32[128,768]{1,0:T(8,128)S(1)} %pad_maximum_fusion.1.refs_0_), channel_id=1, source_target_pairs={{0,18},{16,2},{32,50},{48,34},{64,82},{80,66},{96,114},{112,98},{1... | collective-permute-start | bytes 1179656 | tf_op jit(solution)/shard_map/ppermute | solution.py:500
  190.2 1.9 collective-permute-start.26
  192.2 4.5 %collective-permute-start.27 = (f32[128,768]{1,0:T(8,128)S(1)}, f32[128,768]{1,0:T(8,128)S(1)}, u32[]{:S(2)}, u32[]{:S(2)}) collective-permute-start(f32[128,768]{1,0:T(8,128)S(1)} %pad_maximum_fusion.1.refs_0_), channel_id=1, source_target_pairs={{0,1},{1,0},{2,3},{3,2},{4,5},{5,4},{16,17},{17,16},{18,19},{19,18... | collective-permute-start | bytes 1179656 | tf_op jit(solution)/shard_map/ppermute | solution.py:502
  196.7 4.8 %collective-permute-start.28 = (f32[128,768]{1,0:T(8,128)S(1)}, f32[128,768]{1,0:T(8,128)S(1)}, u32[]{:S(2)}, u32[]{:S(2)}) collective-permute-start(f32[128,768]{1,0:T(8,128)S(1)} %collective-permute-done.25.refs_1_), channel_id=1, source_target_pairs={{0,1},{1,0},{2,3},{3,2},{4,5},{5,4},{16,17},{17,16},{18,19},{19,18... | collective-permute-start | bytes 1179656 | tf_op jit(solution)/shard_map/ppermute | solution.py:502
  201.5 4.4 %collective-permute-done.26.refs_2_ = f32[128,768]{1,0:T(8,128)S(1)} collective-permute-done((f32[128,768]{1,0:T(8,128)S(1)}, f32[128,768]{1,0:T(8,128)S(1)}, u32[]{:S(2)}, u32[]{:S(2)}) %collective-permute-start.26) | collective-permute-done | bytes 393248 | tf_op jit(solution)/shard_map/ppermute | solution.py:500
  205.8 4.8 %collective-permute-start.29 = (f32[128,768]{1,0:T(8,128)S(1)}, f32[128,768]{1,0:T(8,128)S(1)}, u32[]{:S(2)}, u32[]{:S(2)}) collective-permute-start(f32[128,768]{1,0:T(8,128)S(1)} %collective-permute-done.26.refs_2_), channel_id=1, source_target_pairs={{0,1},{1,0},{2,3},{3,2},{4,5},{5,4},{16,17},{17,16},{18,19},{19,18... | collective-permute-start | bytes 1179656 | tf_op jit(solution)/shard_map/ppermute | solution.py:502
  211.9 3.0 %patch.1._ = f32[18,9,128,128]{3,2,1,0:T(8,128)} custom-call(s32[4]{0:T(128)} %add_convert_fusion.info, f32[128,1152]{1,0:T(8,128)} %row.1.refs_0_, f32[128,1152]{1,0:T(8,128)} %select_select_fusion.refs_0_.refs_1_, f32[128,1152]{1,0:T(8,128)} %broadcast_select_fusion.refs_1_.refs_2_, ...), custom_call_target="tpu_custom_call", output_to_operand_aliasing={{}: (4, {})} | custom-call | flops 100000000 | bytes 4000000 | tf_op jit(solution)/shard_map/patch/pallas_call | solution.py:325
  216.6 6.0 %corner.1.block_ref = f32[128,128]{1,0:T(8,128)} custom-call(s32[9]{0:T(128)} %stack.171.info, s32[6,6]{1,0:T(8,128)} %slice.17.live, f32[128,768]{1,0:T(8,128)} %copy-done.2, f32[128,768]{1,0:T(8,128)} %copy-done.6, f32[128,768]{1,0:T(8,128)} %copy-done.7, f32[128,768]{1,0:T(8,128)} %copy-done.8, f32[128,768]{1,0:T(8,128)} %copy-done.9, ...), custom_call_target="tpu_custom_call" | custom-call | flops 1000000000 | bytes 1000000 | tf_op jit(solution)/shard_map/corner/pallas_call | solution.py:259
  222.7 1.5 patch_first.1
  (93 shorter events, 21.1 us)
Async XLA Ops:
  1.0 3.5 %collective-permute-start = (bf16[1,6,64,128]{3,2,1,0:T(8,128)(2,1)S(1)}, bf16[1,6,64,128]{3,2,1,0:T(8,128)(2,1)S(1)}, u32[]{:S(2)}, u32[]{:S(2)}) collective-permute-start(bf16[1,6,64,128]{3,2,1,0:T(8,128)(2,1)S(1)} %dynamic-slice_bitcast_fusion), channel_id=1, source_target_pairs={{0,16},{16,0},{32,48},{48,32},{64,80},{80,64},{96,112},{112,96},{1... | collective-permute-start | bytes 294920 | tf_op jit(solution)/shard_map/ppermute | solution.py:394
  4.5 7.3 %collective-permute-start.1 = (bf16[2,6,64,128]{3,2,1,0:T(8,128)(2,1)S(1)}, bf16[2,6,64,128]{3,2,1,0:T(8,128)(2,1)S(1)}, u32[]{:S(2)}, u32[]{:S(2)}) collective-permute-start(bf16[2,6,64,128]{3,2,1,0:T(8,128)(2,1)S(1)} %maximum_select_fusion), channel_id=1, source_target_pairs={{0,32},{16,48},{32,64},{48,80},{64,96},{80,112},{96,0},{112,16},{1... | collective-permute-start | bytes 589832 | tf_op jit(solution)/shard_map/ppermute | solution.py:395
  6.3 10.4 %collective-permute-start.2 = (bf16[2,6,64,128]{3,2,1,0:T(8,128)(2,1)S(1)}, bf16[2,6,64,128]{3,2,1,0:T(8,128)(2,1)S(1)}, u32[]{:S(2)}, u32[]{:S(2)}) collective-permute-start(bf16[2,6,64,128]{3,2,1,0:T(8,128)(2,1)S(1)} %maximum_select_fusion), channel_id=1, source_target_pairs={{0,64},{16,80},{32,96},{48,112},{64,0},{80,16},{96,32},{112,48},{1... | collective-permute-start | bytes 589832 | tf_op jit(solution)/shard_map/ppermute | solution.py:395
  9.6 7.1 %collective-permute-start.3 = (bf16[2,6,64,128]{3,2,1,0:T(8,128)(2,1)S(1)}, bf16[2,6,64,128]{3,2,1,0:T(8,128)(2,1)S(1)}, u32[]{:S(2)}, u32[]{:S(2)}) collective-permute-start(bf16[2,6,64,128]{3,2,1,0:T(8,128)(2,1)S(1)} %maximum_select_fusion), channel_id=1, source_target_pairs={{0,96},{16,112},{32,0},{48,16},{64,32},{80,48},{96,64},{112,80},{1... | collective-permute-start | bytes 589832 | tf_op jit(solution)/shard_map/ppermute | solution.py:395
  10.4 35.5 %copy-start.17 = (s32[18,6]{1,0:T(8,128)}, s32[18,6]{1,0:T(8,128)S(1)}, u32[]{:S(2)}) copy-start(s32[18,6]{1,0:T(8,128)S(1)} %fusion.1.live) | copy-start | bytes 1300
  16.8 29.0 %copy-start = (bf16[6,6,64,128]{3,2,1,0:T(8,128)(2,1)}, bf16[6,6,64,128]{3,2,1,0:T(8,128)(2,1)S(1)}, u32[]{:S(2)}) copy-start(bf16[6,6,64,128]{3,2,1,0:T(8,128)(2,1)S(1)} %pad_maximum_fusion.refs_2_.refs_6_) | copy-start | bytes 1769476
  16.8 29.0 %collective-permute-start.4 = (bf16[6,6,64,128]{3,2,1,0:T(8,128)(2,1)S(1)}, bf16[6,6,64,128]{3,2,1,0:T(8,128)(2,1)S(1)}, u32[]{:S(2)}, u32[]{:S(2)}) collective-permute-start(bf16[6,6,64,128]{3,2,1,0:T(8,128)(2,1)S(1)} %pad_maximum_fusion.refs_2_.refs_6_), channel_id=1, source_target_pairs={{0,1},{1,0},{2,3},{3,2},{4,5},{5,4},{6,7},{7,6},{8,9},{9,8},{10,11... | collective-permute-start | bytes 1769480 | tf_op jit(solution)/shard_map/ppermute | solution.py:401
  45.9 0.8 copy-start.1
  53.9 19.3 %collective-permute-start.6 = (f32[4,128,384]{2,1,0:T(8,128)}, f32[4,128,384]{2,1,0:T(8,128)S(1)}, u32[]{:S(2)}, u32[]{:S(2)}) collective-permute-start(f32[4,128,384]{2,1,0:T(8,128)} %get-tuple-element.35), channel_id=1, source_target_pairs={{0,32},{16,48},{32,0},{48,16},{64,96},{80,112},{96,64},{112,80},{1... | collective-permute-start | bytes 2359304 | tf_op jit(solution)/shard_map/ppermute | solution.py:436
  54.8 20.2 %collective-permute-start.7 = (f32[4,128,384]{2,1,0:T(8,128)}, f32[4,128,384]{2,1,0:T(8,128)S(1)}, u32[]{:S(2)}, u32[]{:S(2)}) collective-permute-start(f32[4,128,384]{2,1,0:T(8,128)} %get-tuple-element.37), channel_id=1, source_target_pairs={{0,96},{16,112},{32,64},{48,80},{64,32},{80,48},{96,0},{112,16},{1... | collective-permute-start | bytes 2359304 | tf_op jit(solution)/shard_map/ppermute | solution.py:437
  56.1 14.5 %collective-permute-start.5 = (f32[3,128,384]{2,1,0:T(8,128)}, f32[3,128,384]{2,1,0:T(8,128)S(1)}, u32[]{:S(2)}, u32[]{:S(2)}) collective-permute-start(f32[3,128,384]{2,1,0:T(8,128)} %get-tuple-element.33), channel_id=1, source_target_pairs={{0,16},{16,0},{32,48},{48,32},{64,80},{80,64},{96,112},{112,96},{1... | collective-permute-start | bytes 1769480 | tf_op jit(solution)/shard_map/ppermute | solution.py:435
  70.7 4.4 %copy-start.5 = (f32[3,128,384]{2,1,0:T(8,128)}, f32[3,128,384]{2,1,0:T(8,128)S(1)}, u32[]{:S(2)}) copy-start(f32[3,128,384]{2,1,0:T(8,128)S(1)} %collective-permute-done.5.refs_1_) | copy-start | bytes 1769476
  73.2 1.9 copy-start.3
  75.1 0.9 copy-start.4
  79.9 9.7 %collective-permute-start.8 = (f32[2,128,384]{2,1,0:T(8,128)}, f32[2,128,384]{2,1,0:T(8,128)S(1)}, u32[]{:S(2)}, u32[]{:S(2)}) collective-permute-start(f32[2,128,384]{2,1,0:T(8,128)} %get-tuple-element.39), channel_id=1, source_target_pairs={{0,32},{16,48},{32,0},{48,16},{64,96},{80,112},{96,64},{112,80},{1... | collective-permute-start | bytes 1179656 | tf_op jit(solution)/shard_map/ppermute | solution.py:448
  79.9 12.8 %collective-permute-start.9 = (f32[2,128,384]{2,1,0:T(8,128)}, f32[2,128,384]{2,1,0:T(8,128)S(1)}, u32[]{:S(2)}, u32[]{:S(2)}) collective-permute-start(f32[2,128,384]{2,1,0:T(8,128)} %get-tuple-element.41), channel_id=1, source_target_pairs={{32,64},{48,80},{64,32},{80,48},{96,0},{112,16},{33,65},{49,81},{6... | collective-permute-start | bytes 1179656 | tf_op jit(solution)/shard_map/ppermute | solution.py:449
  81.2 11.5 %collective-permute-start.10 = (f32[2,128,384]{2,1,0:T(8,128)}, f32[2,128,384]{2,1,0:T(8,128)S(1)}, u32[]{:S(2)}, u32[]{:S(2)}) collective-permute-start(f32[2,128,384]{2,1,0:T(8,128)} %get-tuple-element.43), channel_id=1, source_target_pairs={{0,16},{16,0},{32,48},{48,32},{64,80},{80,64},{96,112},{112,96},{1... | collective-permute-start | bytes 1179656 | tf_op jit(solution)/shard_map/ppermute | solution.py:450
  89.6 3.1 %copy-start.11 = (f32[2,128,384]{2,1,0:T(8,128)}, f32[2,128,384]{2,1,0:T(8,128)S(1)}, u32[]{:S(2)}) copy-start(f32[2,128,384]{2,1,0:T(8,128)S(1)} %collective-permute-done.8.refs_1_) | copy-start | bytes 1179652
  92.7 0.8 copy-start.12
  92.7 0.9 copy-start.13
  96.4 7.9 %collective-permute-start.11 = (f32[1,128,384]{2,1,0:T(8,128)}, f32[1,128,384]{2,1,0:T(8,128)S(1)}, u32[]{:S(2)}, u32[]{:S(2)}) collective-permute-start(f32[1,128,384]{2,1,0:T(8,128)} %get-tuple-element.45), channel_id=1, source_target_pairs={{32,64},{48,80},{64,32},{80,48},{96,0},{112,16},{33,65},{49,81},{6... | collective-permute-start | bytes 589832 | tf_op jit(solution)/shard_map/ppermute | solution.py:456
  97.7 6.6 %collective-permute-start.12 = (f32[1,128,384]{2,1,0:T(8,128)}, f32[1,128,384]{2,1,0:T(8,128)S(1)}, u32[]{:S(2)}, u32[]{:S(2)}) collective-permute-start(f32[1,128,384]{2,1,0:T(8,128)} %get-tuple-element.47), channel_id=1, source_target_pairs={{0,16},{16,0},{32,48},{48,32},{64,80},{80,64},{1,17},{17,1},{33,49... | collective-permute-start | bytes 589832 | tf_op jit(solution)/shard_map/ppermute | solution.py:457
  100.0 7.0 %collective-permute-start.13 = (f32[1,128,384]{2,1,0:T(8,128)}, f32[1,128,384]{2,1,0:T(8,128)S(1)}, u32[]{:S(2)}, u32[]{:S(2)}) collective-permute-start(f32[1,128,384]{2,1,0:T(8,128)} %get-tuple-element.49), channel_id=1, source_target_pairs={{0,32},{16,48},{32,0},{48,16},{96,64},{112,80},{1,33},{17,49},{33,... | collective-permute-start | bytes 589832 | tf_op jit(solution)/shard_map/ppermute | solution.py:458
  104.3 2.8 %copy-start.14 = (f32[1,128,384]{2,1,0:T(8,128)}, f32[1,128,384]{2,1,0:T(8,128)S(1)}, u32[]{:S(2)}) copy-start(f32[1,128,384]{2,1,0:T(8,128)S(1)} %collective-permute-done.11.refs_1_) | copy-start | bytes 589828
  104.3 2.8 %copy-start.15 = (f32[1,128,384]{2,1,0:T(8,128)}, f32[1,128,384]{2,1,0:T(8,128)S(1)}, u32[]{:S(2)}) copy-start(f32[1,128,384]{2,1,0:T(8,128)S(1)} %collective-permute-done.12.refs_3_) | copy-start | bytes 589828
  107.1 0.7 copy-start.16
  110.0 5.2 %collective-permute-start.15 = (f32[128,1152]{1,0:T(8,128)}, f32[128,1152]{1,0:T(8,128)S(1)}, u32[]{:S(2)}, u32[]{:S(2)}) collective-permute-start(f32[128,1152]{1,0:T(8,128)} %row.1.refs_0_), channel_id=1, source_target_pairs={{64,0},{65,16},{66,32},{67,48},{68,68},{69,84},{70,100},{71,116},{... | collective-permute-start | bytes 1769480 | tf_op jit(solution)/shard_map/ppermute | solution.py:472
  110.7 13.3 %collective-permute-start.14 = (f32[128,1152]{1,0:T(8,128)}, f32[128,1152]{1,0:T(8,128)S(1)}, u32[]{:S(2)}, u32[]{:S(2)}) collective-permute-start(f32[128,1152]{1,0:T(8,128)} %row.1.refs_0_), channel_id=1, source_target_pairs={{0,0},{1,16},{2,32},{3,48},{4,68},{5,84},{6,100},{7,116},{8,8},{9,... | collective-permute-start | bytes 1769480 | tf_op jit(solution)/shard_map/ppermute | solution.py:471
  124.1 2.9 %collective-permute-start.16 = (f32[128,1152]{1,0:T(8,128)S(1)}, f32[128,1152]{1,0:T(8,128)S(1)}, u32[]{:S(2)}, u32[]{:S(2)}) collective-permute-start(f32[128,1152]{1,0:T(8,128)S(1)} %broadcast_select_fusion.1), channel_id=1, source_target_pairs={{0,4},{16,20},{32,36},{48,52},{1,5},{17,21},{33,37},{49,53},{68,64... | collective-permute-start | bytes 1769480 | tf_op jit(solution)/shard_map/ppermute | solution.py:477
  124.8 12.1 %collective-permute-start.17 = (f32[128,1152]{1,0:T(8,128)S(1)}, f32[128,1152]{1,0:T(8,128)S(1)}, u32[]{:S(2)}, u32[]{:S(2)}) collective-permute-start(f32[128,1152]{1,0:T(8,128)S(1)} %collective-permute-done.14), channel_id=1, source_target_pairs={{8,0},{24,16},{40,32},{56,48},{76,64},{92,80},{108,96},{124,112},{... | collective-permute-start | bytes 1769480 | tf_op jit(solution)/shard_map/ppermute | solution.py:473
  126.1 10.8 %collective-permute-start.18 = (f32[128,1152]{1,0:T(8,128)S(1)}, f32[128,1152]{1,0:T(8,128)S(1)}, u32[]{:S(2)}, u32[]{:S(2)}) collective-permute-start(f32[128,1152]{1,0:T(8,128)S(1)} %collective-permute-done.15), channel_id=1, source_target_pairs={{8,4},{24,20},{40,36},{56,52},{76,68},{92,84},{108,100},{124,116},... | collective-permute-start | bytes 1769480 | tf_op jit(solution)/shard_map/ppermute | solution.py:474
  142.0 16.6 %collective-permute-start.22 = (f32[64,768]{1,0:T(8,128)}, f32[64,768]{1,0:T(8,128)S(1)}, u32[]{:S(2)}, u32[]{:S(2)}) collective-permute-start(f32[64,768]{1,0:T(8,128)} %get-tuple-element.51), channel_id=1, source_target_pairs={{0,32},{1,33},{2,34},{3,35},{4,36},{5,37},{16,48},{17,49},{18,50},... | collective-permute-start | bytes 589832 | tf_op jit(solution)/shard_map/ppermute | solution.py:488
  143.9 20.2 %collective-permute-start.19 = (f32[64,768]{1,0:T(8,128)}, f32[64,768]{1,0:T(8,128)S(1)}, u32[]{:S(2)}, u32[]{:S(2)}) collective-permute-start(f32[64,768]{1,0:T(8,128)} %get-tuple-element.50), channel_id=1, source_target_pairs={{0,16},{1,17},{2,18},{3,19},{4,20},{5,21},{16,0},{17,1},{18,2},{19... | collective-permute-start | bytes 589832 | tf_op jit(solution)/shard_map/ppermute | solution.py:488
  159.6 9.0 %collective-permute-start.23 = (f32[64,768]{1,0:T(8,128)S(1)}, f32[64,768]{1,0:T(8,128)S(1)}, u32[]{:S(2)}, u32[]{:S(2)}) collective-permute-start(f32[64,768]{1,0:T(8,128)S(1)} %add.134), channel_id=1, source_target_pairs={{0,96},{1,97},{2,98},{3,99},{4,100},{5,101},{16,112},{17,113},{18,... | collective-permute-start | bytes 589832 | tf_op jit(solution)/shard_map/ppermute | solution.py:488
  165.1 9.8 %collective-permute-start.20 = (f32[64,768]{1,0:T(8,128)S(1)}, f32[64,768]{1,0:T(8,128)S(1)}, u32[]{:S(2)}, u32[]{:S(2)}) collective-permute-start(f32[64,768]{1,0:T(8,128)S(1)} %add.131), channel_id=1, source_target_pairs={{0,32},{1,33},{2,34},{3,35},{4,36},{5,37},{16,48},{17,49},{18,50},... | collective-permute-start | bytes 589832 | tf_op jit(solution)/shard_map/ppermute | solution.py:488
  168.6 11.2 %collective-permute-start.24 = (f32[64,768]{1,0:T(8,128)S(1)}, f32[64,768]{1,0:T(8,128)S(1)}, u32[]{:S(2)}, u32[]{:S(2)}) collective-permute-start(f32[64,768]{1,0:T(8,128)S(1)} %add.135), channel_id=1, source_target_pairs={{0,16},{1,17},{2,18},{3,19},{4,20},{5,21},{16,0},{17,1},{18,2},{19... | collective-permute-start | bytes 589832 | tf_op jit(solution)/shard_map/ppermute | solution.py:488
  175.0 8.9 %collective-permute-start.21 = (f32[64,768]{1,0:T(8,128)S(1)}, f32[64,768]{1,0:T(8,128)S(1)}, u32[]{:S(2)}, u32[]{:S(2)}) collective-permute-start(f32[64,768]{1,0:T(8,128)S(1)} %add.132), channel_id=1, source_target_pairs={{0,96},{1,97},{2,98},{3,99},{4,100},{5,101},{16,112},{17,113},{18,... | collective-permute-start | bytes 589832 | tf_op jit(solution)/shard_map/ppermute | solution.py:488
  184.0 31.0 %copy-start.2 = (f32[128,768]{1,0:T(8,128)}, f32[128,768]{1,0:T(8,128)S(1)}, u32[]{:S(2)}) copy-start(f32[128,768]{1,0:T(8,128)S(1)} %pad_maximum_fusion.1.refs_0_) | copy-start | bytes 1179652
  184.0 12.7 %collective-permute-start.25 = (f32[128,768]{1,0:T(8,128)S(1)}, f32[128,768]{1,0:T(8,128)S(1)}, u32[]{:S(2)}, u32[]{:S(2)}) collective-permute-start(f32[128,768]{1,0:T(8,128)S(1)} %pad_maximum_fusion.1.refs_0_), channel_id=1, source_target_pairs={{0,18},{16,2},{32,50},{48,34},{64,82},{80,66},{96,114},{112,98},{1... | collective-permute-start | bytes 1179656 | tf_op jit(solution)/shard_map/ppermute | solution.py:500
  190.2 15.6 %collective-permute-start.26 = (f32[128,768]{1,0:T(8,128)S(1)}, f32[128,768]{1,0:T(8,128)S(1)}, u32[]{:S(2)}, u32[]{:S(2)}) collective-permute-start(f32[128,768]{1,0:T(8,128)S(1)} %pad_maximum_fusion.1.refs_0_), channel_id=1, source_target_pairs={{0,4},{16,20},{32,36},{48,52},{64,68},{80,84},{96,100},{112,116},{... | collective-permute-start | bytes 1179656 | tf_op jit(solution)/shard_map/ppermute | solution.py:500
  192.2 22.8 %collective-permute-start.27 = (f32[128,768]{1,0:T(8,128)S(1)}, f32[128,768]{1,0:T(8,128)S(1)}, u32[]{:S(2)}, u32[]{:S(2)}) collective-permute-start(f32[128,768]{1,0:T(8,128)S(1)} %pad_maximum_fusion.1.refs_0_), channel_id=1, source_target_pairs={{0,1},{1,0},{2,3},{3,2},{4,5},{5,4},{16,17},{17,16},{18,19},{19,18... | collective-permute-start | bytes 1179656 | tf_op jit(solution)/shard_map/ppermute | solution.py:502
  196.7 18.3 %copy-start.6 = (f32[128,768]{1,0:T(8,128)}, f32[128,768]{1,0:T(8,128)S(1)}, u32[]{:S(2)}) copy-start(f32[128,768]{1,0:T(8,128)S(1)} %collective-permute-done.25.refs_1_) | copy-start | bytes 1179652
  196.7 18.3 %collective-permute-start.28 = (f32[128,768]{1,0:T(8,128)S(1)}, f32[128,768]{1,0:T(8,128)S(1)}, u32[]{:S(2)}, u32[]{:S(2)}) collective-permute-start(f32[128,768]{1,0:T(8,128)S(1)} %collective-permute-done.25.refs_1_), channel_id=1, source_target_pairs={{0,1},{1,0},{2,3},{3,2},{4,5},{5,4},{16,17},{17,16},{18,19},{19,18... | collective-permute-start | bytes 1179656 | tf_op jit(solution)/shard_map/ppermute | solution.py:502
  205.8 9.1 %copy-start.7 = (f32[128,768]{1,0:T(8,128)}, f32[128,768]{1,0:T(8,128)S(1)}, u32[]{:S(2)}) copy-start(f32[128,768]{1,0:T(8,128)S(1)} %collective-permute-done.26.refs_2_) | copy-start | bytes 1179652
  205.8 9.2 %collective-permute-start.29 = (f32[128,768]{1,0:T(8,128)S(1)}, f32[128,768]{1,0:T(8,128)S(1)}, u32[]{:S(2)}, u32[]{:S(2)}) collective-permute-start(f32[128,768]{1,0:T(8,128)S(1)} %collective-permute-done.26.refs_2_), channel_id=1, source_target_pairs={{0,1},{1,0},{2,3},{3,2},{4,5},{5,4},{16,17},{17,16},{18,19},{19,18... | collective-permute-start | bytes 1179656 | tf_op jit(solution)/shard_map/ppermute | solution.py:502
  215.0 0.8 copy-start.8
  215.0 0.9 copy-start.9
  215.9 0.7 copy-start.10

commit v3 on v2

v3 whole, which is shorter than its diff:
```python
import functools

import jax
import jax.numpy as jnp
from jax import lax
from jax.experimental import pallas as pl
from jax.experimental.pallas import tpu as pltpu
from jax.sharding import PartitionSpec as P


F32, BF16 = jnp.float32, jnp.bfloat16
PARTS = ((0, 8), (8, 10))
SIZES = (3, 4, 4)
CORNER, COLS, IDS = 18, 24, 33
VMEM = pl.BlockSpec(memory_space=pltpu.VMEM)
SMEM = pl.BlockSpec(memory_space=pltpu.SMEM)
ANY = pl.BlockSpec(memory_space=pl.ANY)


def halves(value):
    high = value.astype(BF16)
    return high, (value - high.astype(F32)).astype(BF16)


def stacked(core, own, other):
    return jnp.concatenate([jnp.where(core > 0, other, own), jnp.where(core > 0, own, other)], axis=0)


def dot(left, right):
    return jnp.dot(left, right, preferred_element_type=F32)


def product_kernel(start, masks, x_ref, u_ref, *refs):
    copy_ref, out_ref = refs[-2:]
    step = pl.program_id(0)
    rows, cols, _, _ = x_ref.shape
    steps = u_ref.shape[1]
    left, high, low = [], [], []
    for r in range(rows):
        wide = []
        for k in range(steps):
            block = u_ref[r, k]
            wide.append(jnp.where(masks[start + step * rows + r, k] > 0, block, jnp.zeros_like(block)))
        left.append(jnp.concatenate(wide, axis=1))
        value = jnp.concatenate([x_ref[r, c] for c in range(cols)], axis=1)
        for c in range(cols):
            copy_ref[r, c] = x_ref[r, c]
        a, b = halves(value)
        high.append(a)
        low.append(b)
    left = jnp.concatenate(left, axis=0).T
    both = jnp.concatenate([left, left], axis=1)
    term = dot(both, jnp.concatenate(high + low, axis=0))
    term = term.reshape(out_ref.shape)

    @pl.when(step == 0)
    def _():
        out_ref[...] = term

    @pl.when(step > 0)
    def _():
        out_ref[...] += term


def products(blocks, lower, masks, whole, first, count, rows=2):
    _, cols, width, _ = blocks.shape
    steps = lower.shape[1]
    start = first // rows
    known = [] if whole is None else [whole]
    return pl.pallas_call(
        functools.partial(product_kernel, first),
        grid_spec=pltpu.PrefetchScalarGridSpec(
            num_scalar_prefetch=1,
            grid=(count // rows,),
            in_specs=[
                pl.BlockSpec((rows, cols, width, width), lambda i, _: (start + i, 0, 0, 0)),
                pl.BlockSpec((rows, steps, width, width), lambda i, _: (start + i, 0, 0, 0)),
            ]
            + [ANY] * len(known),
            out_specs=[
                pl.BlockSpec((rows, cols, width, width), lambda i, _: (start + i, 0, 0, 0)),
                pl.BlockSpec((steps, width, cols * width), lambda i, _: (0, 0, 0)),
            ],
        ),
        out_shape=[
            jax.ShapeDtypeStruct(blocks.shape, F32),
            jax.ShapeDtypeStruct((steps, width, cols * width), F32),
        ],
        input_output_aliases={3: 0} if known else {},
        cost_estimate=pl.CostEstimate(
            flops=4 * count * cols * steps * width**3, bytes_accessed=8 * count * cols * width**2, transcendentals=0
        ),
        name="products",
    )(masks, blocks, lower, *known)


def first_pieces(z, y):
    outer, low, other = (z == 0) | (z == 3), z < 2, 1 - y

    def either(flag, yes, no):
        return [jnp.where(flag, a, b) for a, b in zip(yes, no)]

    ends, middle = (0, 1, 0, 0), (2, 3, 4, 5)
    front, back = (0, 1, 2, 3), (4, 5, 0, 0)
    return [
        [other, 2 + other, 4 + other],
        [y, 2 + y, 4 + y],
        either(outer, middle, ends),
        either(outer, ends, middle),
        either(low, back, front),
        either(low, front, back),
    ]


def later_pieces(group, stage, z, y):
    outer, low, other = (z == 0) | (z == 3), z < 2, 1 - y
    one, two = jnp.where(z == 1, 1, 0), jnp.where(z == 2, 1, 0)
    if stage == 2:
        return [
            ([jnp.where(outer, 1, 0), jnp.where(outer, 2, 0)], [jnp.where(outer, 0, 1), jnp.where(outer, 0, 2)]),
            ([2 * one, 2 * one + 1], [2 * two, 2 * two + 1]),
            ([other, jnp.where(low, 2 + other, other)], [y, jnp.where(low, 2 + y, y)]),
        ][group]
    return [([one], [two]), ([other], [y]), ([jnp.where(z == 0, 1, 0)], [one])][group]


def place_of(masks):
    p, q = masks[IDS, 0], masks[IDS, 1]
    return p, q, p // 2, p % 2


def eliminate_kernel(masks, *refs):
    *part_refs, u_ref, v_ref = refs[: -2 * len(SIZES) - 1]
    places, w_ref = refs[-2 * len(SIZES) - 1 : -1], refs[-1]
    steps = w_ref.shape[0]
    _, q, z, y = place_of(masks)
    high, low = [], []
    for k in reversed(range(steps)):
        total = part_refs[0][k]
        for ref in part_refs[1:]:
            total = total + ref[k]
        if high:
            blocks = []
            for j in range(k + 1, steps):
                block = stacked(q % 2, u_ref[j, k], v_ref[j, k])
                blocks.append(jnp.where(masks[CORNER + j, k] > 0, block, jnp.zeros_like(block)).T)
            left = jnp.concatenate(blocks + blocks, axis=1)
            total = total + dot(left, jnp.concatenate(high[::-1] + low[::-1], axis=0))
        total = -total
        w_ref[k] = total
        a, b = halves(total)
        high.append(a)
        low.append(b)
    for n, (ref, pieces) in enumerate(zip(places, first_pieces(z, y))):
        for m, k in enumerate(pieces):
            ref[m] = w_ref[k, :, pl.ds(n // 2 * ref.shape[2], ref.shape[2])]


def eliminate(masks, parts, corner):
    _, width, wide = parts[0].shape
    shapes = [jax.ShapeDtypeStruct((n, width, wide // len(SIZES)), F32) for n in SIZES for _ in range(2)]
    return pl.pallas_call(
        eliminate_kernel,
        in_specs=[SMEM] + [VMEM] * (len(parts) + 2),
        out_specs=[VMEM] * len(shapes),
        out_shape=shapes,
        scratch_shapes=[pltpu.VMEM(parts[0].shape, F32)],
        cost_estimate=pl.CostEstimate(flops=1000 * parts[0].size, bytes_accessed=20 * parts[0].size, transcendentals=0),
        name="eliminate",
    )(masks, *parts, *corner)


def halving_kernel(group, stage, masks, stay_ref, came_ref, send_ref, keep_ref):
    _, _, z, y = place_of(masks)
    for ref, pieces in zip((send_ref, keep_ref), later_pieces(group, stage, z, y)):
        for m, n in enumerate(pieces):
            ref[m] = stay_ref[n] + came_ref[n]


def halving(masks, group, stage, stay, came):
    _, width, wide = stay.shape
    return pl.pallas_call(
        functools.partial(halving_kernel, group, stage),
        in_specs=[SMEM, VMEM, VMEM],
        out_specs=[VMEM] * 2,
        out_shape=[jax.ShapeDtypeStruct((4 - stage, width, wide), F32)] * 2,
        cost_estimate=pl.CostEstimate(flops=10**8, bytes_accessed=32 * width * wide, transcendentals=0),
        name="halving",
    )(masks, stay, came)


def row_kernel(masks, *refs):
    *given, row_ref = refs
    width = row_ref.shape[0]
    count = given[0].shape[2] // width
    p, _, _, _ = place_of(masks)
    k = jnp.minimum(p, COLS - CORNER - 1)
    for n in range(row_ref.shape[1] // width):
        part = pl.ds(n % count * width, width)
        value = given[n // count * 2][0, :, part] + given[n // count * 2 + 1][0, :, part]
        row_ref[:, pl.ds(n * width, width)] = jnp.where(masks[COLS + n, k] > 0, value, jnp.zeros_like(value))


def masked_row(masks, given):
    _, width, wide = given[0].shape
    return pl.pallas_call(
        row_kernel,
        in_specs=[SMEM] + [VMEM] * len(given),
        out_specs=VMEM,
        out_shape=jax.ShapeDtypeStruct((width, wide * len(given) // 2), F32),
        cost_estimate=pl.CostEstimate(flops=10**7, bytes_accessed=8 * width * wide * len(given), transcendentals=0),
        name="row",
    )(masks, *given)


def column_kernel(masks, *refs):
    *value_refs, u_ref, upper_ref, lower_ref = refs
    _, steps, width, _ = u_ref.shape
    total, a = None, 0
    for even_ref, odd_ref in zip(value_refs[::2], value_refs[1::2]):
        for c in range(even_ref.shape[1] // width):
            part = pl.ds(c * width, width)
            value = jnp.concatenate([even_ref[:, part], odd_ref[:, part]], axis=1)
            left = jnp.concatenate(halves(value), axis=0)
            right = []
            for r in (a, a + 1):
                wide = []
                for k in range(steps):
                    block = u_ref[r, k]
                    wide.append(jnp.where(masks[r, k] > 0, block, jnp.zeros_like(block)))
                right.append(jnp.concatenate(wide, axis=1))
            term = dot(left, jnp.concatenate(right, axis=0))
            total = term if total is None else total + term
            a += 2
    total = total[:width] + total[width:]
    upper_ref[...] = total[: width // 2]
    lower_ref[...] = total[width // 2 :]


def column_products(values, lower, masks):
    row_blocks, steps, width, _ = lower.shape
    return pl.pallas_call(
        column_kernel,
        in_specs=[SMEM] + [VMEM] * (len(values) + 1),
        out_specs=[VMEM] * 2,
        out_shape=[jax.ShapeDtypeStruct((width // 2, steps * width), F32)] * 2,
        cost_estimate=pl.CostEstimate(flops=4 * row_blocks * steps * width**3, bytes_accessed=6 * 10**6, transcendentals=0),
        name="column",
    )(masks, *values, lower)


def corner_kernel(masks, *refs):
    *sum_refs, u_ref, v_ref, dinv_ref, _, out_ref, x_ref, h_ref, sem_ref = refs
    steps, width, _ = dinv_ref.shape
    p, q, _, _ = place_of(masks)
    for n, ref in enumerate(sum_refs):
        slot = (q + steps - n % 3 * 2) % steps
        h_ref[slot if n < 3 else slot + 1 - slot % 2 * 2] = ref[...]
    for k in reversed(range(steps)):
        here = pl.ds(k * width, width)
        later = steps - 1 - k
        if later:
            right = []
            for j in range(k + 1, steps):
                block = stacked(q % 2, u_ref[j, k], v_ref[j, k])
                right.append(jnp.where(masks[CORNER + j, k] > 0, block, jnp.zeros_like(block)))
            right = jnp.concatenate(right, axis=0)
            both = jnp.concatenate([right, right], axis=0)
            rest = pl.ds((k + 1) * width, later * width)
            known = jnp.concatenate(halves(x_ref[rest, rest]), axis=1)
            value = dot(known, both)
            turned = []
            for i in range(k + 1, steps):
                at = (i - k - 1) * width
                block = -(value[at : at + width] + h_ref[i, :, here])
                block = jnp.where(masks[CORNER + i, k] > 0, block, jnp.zeros_like(block))
                x_ref[pl.ds(i * width, width), here] = block
                turned.append(block.T)
            turned = jnp.concatenate(turned, axis=1)
            x_ref[here, rest] = turned
            tail = dot(jnp.concatenate(halves(turned), axis=1), both)
            x_ref[here, here] = dinv_ref[k].T - h_ref[k, :, here] - tail
        else:
            x_ref[here, here] = dinv_ref[k].T - h_ref[k, :, here]
    for k in range(steps):
        for j in range(steps):

            @pl.when((p == k) & (q == j))
            def _():
                block = x_ref.at[pl.ds(k * width, width), pl.ds(j * width, width)]
                copy = pltpu.make_async_copy(block, out_ref.at[0, 0], sem_ref)
                copy.start()
                copy.wait()


def corner_blocks(masks, sums, corner, dinv, whole):
    steps, width, _ = dinv.shape
    return pl.pallas_call(
        corner_kernel,
        in_specs=[SMEM] + [VMEM] * (len(sums) + 3) + [ANY],
        out_specs=ANY,
        out_shape=jax.ShapeDtypeStruct(whole.shape, F32),
        scratch_shapes=[
            pltpu.VMEM((steps * width, steps * width), F32),
            pltpu.VMEM((steps, width, steps * width), F32),
            pltpu.SemaphoreType.DMA,
        ],
        input_output_aliases={4 + len(sums): 0},
        cost_estimate=pl.CostEstimate(flops=10**9, bytes_accessed=10**6, transcendentals=0),
        name="corner",
    )(masks, *sums, *corner, dinv, whole)


def patch_kernel(masks, *refs):
    *value_refs, _, out_ref, turned_ref, sem_ref = refs
    row_blocks, cols, width, _ = out_ref.shape
    p, q, _, _ = place_of(masks)
    has_row, has_col = p < COLS - CORNER, q < COLS - CORNER
    row_first, col_first = has_row & (q >= COLS - CORNER), has_col & (p >= COLS - CORNER)
    rows, columns = [], []
    for row_ref, even_ref, odd_ref in zip(value_refs[::3], value_refs[1::3], value_refs[2::3]):
        for c in range(row_ref.shape[1] // width):
            rows.append((row_ref, pl.ds(c * width, width)))
            columns.append((even_ref, pl.ds(c * width, width)))
            columns.append((odd_ref, pl.ds(c * width, width)))

    def row_copy(c):
        return pltpu.make_async_copy(rows[c][0].at[:, rows[c][1]], out_ref.at[0, c], sem_ref.at[c])

    def col_copy(a):
        return pltpu.make_async_copy(turned_ref.at[a], out_ref.at[a, 0], sem_ref.at[cols + a])

    @pl.when(has_row)
    def _():
        for c in range(1, cols):
            row_copy(c).start()

    @pl.when(row_first)
    def _():
        row_copy(0).start()

    @pl.when(has_col)
    def _():
        for a in range(row_blocks):
            turned_ref[a] = columns[a][0][:, columns[a][1]].T
        for a in range(1, row_blocks):
            col_copy(a).start()
        for a in range(1, row_blocks):
            col_copy(a).wait()

    @pl.when(col_first)
    def _():
        col_copy(0).start()
        col_copy(0).wait()

    @pl.when(has_row)
    def _():
        for c in range(1, cols):
            row_copy(c).wait()

    @pl.when(row_first)
    def _():
        row_copy(0).wait()


def patch(masks, values, whole):
    row_blocks, cols, width, _ = whole.shape
    return pl.pallas_call(
        patch_kernel,
        in_specs=[SMEM] + [VMEM] * len(values) + [ANY],
        out_specs=ANY,
        out_shape=jax.ShapeDtypeStruct(whole.shape, F32),
        scratch_shapes=[pltpu.VMEM((row_blocks, width, width), F32), pltpu.SemaphoreType.DMA((row_blocks + cols,))],
        input_output_aliases={1 + len(values): 0},
        cost_estimate=pl.CostEstimate(flops=10**8, bytes_accessed=4 * 10**6, transcendentals=0),
        name="patch",
    )(masks, *values, whole)


def per_device(ainv_in, ufactor, dinv, pattern):
    row_blocks, _, cols, _, width, _ = ainv_in.shape
    steps = dinv.shape[0]
    n_row, n_col = lax.axis_size("prow"), lax.axis_size("pcol")
    blocks = ainv_in.reshape(row_blocks, cols, width, width)
    lower = ufactor.reshape(row_blocks, steps, width, width)
    p, q = lax.axis_index("prow"), lax.axis_index("pcol")
    z, y, core = p // 2, p % 2, q % 2
    n_z = n_row // 2
    row_ids = jnp.arange(row_blocks, dtype=jnp.int32) * n_row + p
    col_ids = jnp.arange(cols, dtype=jnp.int32) * n_col + q

    flags = pattern[:, :steps]
    mine = lax.dynamic_index_in_dim(flags.reshape(row_blocks, n_row, steps), p, 1, keepdims=False)
    live = (mine > 0) & (row_ids >= steps)[:, None]
    mine = lax.dynamic_index_in_dim(flags.reshape(cols, n_col, steps), q, 1, keepdims=False)
    live_cols = (mine > 0) & (col_ids >= steps)[:, None]
    ids = jnp.where(jnp.arange(steps) == 0, p, q).astype(jnp.int32)
    masks = jnp.concatenate([live.astype(jnp.int32), flags[:steps], live_cols.astype(jnp.int32), ids[None]])

    def at(zz, yy):
        return zz % n_z * 2 + yy

    flip_y = [(d, d ^ 1) for d in range(n_row)]
    flip_z = [(d, d ^ 2) for d in range(n_row)]
    mirror = [(d, at(n_z - 1 - d // 2, d % 2)) for d in range(n_row)]
    flip_core = [(d, d ^ 1) for d in range(n_col)]

    half = width // 2
    mine = lax.dynamic_slice(lower, (0, 0, core * half, 0), (1, steps, half, width))

    def join(bit, own, other):
        return jnp.where(bit == 0, jnp.concatenate([own, other]), jnp.concatenate([other, own]))

    def ring(shift):
        return [(at(zz, yy), at(zz + shift, yy)) for zz in range(n_z) for yy in range(2)]

    pair = join(y, mine, lax.ppermute(mine, "prow", flip_y))
    moved = [pair] + [lax.ppermute(pair, "prow", ring(shift)) for shift in (1, 2, 3)]
    corner = []
    for t in range(steps // 2):
        away = (z - t) % n_z
        corner.append(jnp.where(away == 0, moved[0], jnp.where(away == 1, moved[1], jnp.where(away == 2, moved[2], moved[3]))))
    corner = jnp.concatenate(corner)
    corner = corner, lax.ppermute(corner, "pcol", flip_core)

    both, grid = ("prow", "pcol"), [(x, h, c) for x in range(n_col // 4) for h in range(2) for c in range(2)]

    def device(x, h, c, zz, yy):
        return at(zz, yy) * n_col + x * 4 + h * 2 + c

    whole, parts = None, []
    for first, count in PARTS:
        whole, part = products(blocks, lower, masks, whole, first, count)
        parts.append(part)

    over_m = [(s, d) for s, d in mirror if d < steps]
    over_y = [(s, d) for s, d in flip_y if d < steps]
    over_z = [(s, d) for s, d in flip_z if d < steps]
    routes = (flip_y, flip_z, over_m), (flip_z, over_m, over_y), (mirror, flip_y, over_z)
    pieces = eliminate(masks, parts, corner)
    held = [(pieces[2 * n], pieces[2 * n + 1]) for n in range(len(SIZES))]
    for stage in range(3):
        held = [(lax.ppermute(send, "prow", routes[n][stage]), keep) for n, (send, keep) in enumerate(held)]
        if stage < 2:
            held = [halving(masks, n, stage + 2, keep, came) for n, (came, keep) in enumerate(held)]
    row = masked_row(masks, [v for came, keep in held for v in (keep, came)])

    def turn(k, x, h, c):
        return at(k // 2, k % 2) * n_col + x * 4 + h * 2 + c, device(x, k // 2 % 2, k % 2, x % 2 * 2 + h, c)

    places = [(h, c, zz, yy) for h in range(2) for c in range(2) for zz in range(n_z) for yy in range(2)]

    def slide(place, start, end):
        h, c, zz, yy = place
        return device(start, h, c, zz, yy), device(end, h, c, zz, yy)

    x = q // 4
    first = lax.ppermute(row, both, [turn(k, *place) for k in range(4) for place in grid])
    second = lax.ppermute(row, both, [turn(k, *place) for k in range(4, steps) for place in grid])
    odd0 = lax.ppermute(first, both, [slide(pl_, pl_[2] // 2 + 2, 0) for pl_ in places])
    odd1 = lax.ppermute(second, both, [slide(pl_, pl_[2] // 2 + 2, 1) for pl_ in places if pl_[0] == 0])
    route = [slide(pl_, 0, 1) for pl_ in places if pl_[2] // 2 == 0 and pl_[0] == 0]
    route += [slide(pl_, 1, 0) for pl_ in places if pl_[2] // 2 == 1]
    moved = lax.ppermute(jnp.where(x == 0, second, first), both, route)
    mine = jnp.where(x == 0, first, second)
    values = [row, jnp.where(x == z // 2, mine, moved), jnp.where(x == 0, odd0, odd1)]

    upper, under = column_products(values[1:], lower, masks)

    def here(perm):
        return [(s * n_col + d, t * n_col + d) for s, t in perm for d in range(steps)]

    orders = (flip_y, flip_z), (flip_z, mirror), (mirror, flip_y)
    for (one, two) in orders:
        came = lax.ppermute(upper, both, here(one)), lax.ppermute(under, both, here(two))
        upper, under = upper + came[0], under + came[1]
    sums = jnp.concatenate([upper, under])

    def around(t):
        route = []
        for d in range(steps):
            to = (d + t) % steps
            flip = d // 2 % 2 ^ to // 2 % 2
            route += [(s * n_col + d, (s ^ flip) * n_col + to) for s in range(n_row)]
        return route

    turns = [lax.ppermute(sums, both, around(t)) for t in (2, 4)]
    sums = [sums, *turns]
    sums += [lax.ppermute(v, "pcol", [(d, d ^ 1) for d in range(steps)]) for v in sums]
    whole = patch(masks, values, whole)
    whole = corner_blocks(masks, sums, corner, dinv, whole)
    return whole.reshape(ainv_in.shape)


def solution(mesh):
    placed = (
        P(None, "prow", None, "pcol", None, None),
        P(None, "prow", None, None, None),
        P(),
        P(),
    )
    return jax.shard_map(
        per_device,
        mesh=mesh,
        in_specs=placed,
        out_specs=P(None, "prow", None, "pcol", None, None),
        check_vma=False,
    )
```

time: 226 us -> 220 us (0.973)
  the two profiles are of different devices: /device:TPU:25 before, /device:TPU:0 now
where the time goes in v3:
time: 220 us; the launch traced here: 217 us
  waiting for transfers between devices  78.3 us (36%)
  starting transfers between devices  62.2 us (28%)
  Pallas kernels  59.8 us (27%)
  local copies, waits for them, and re-layouts  11.6 us (5%)
  other arithmetic  4.68 us (2%)
    pallas_call x2, Pallas kernels, products(): pl.pallas_call(functools.partial(product_kernel, first), grid_spec=pltpu....  24 us
    ppermute x9, waiting for transfers between devices, per_device(): lax.ppermute(send, 'prow', routes[n][stage])  22.5 us
    ppermute x1, waiting for transfers between devices, per_device(): lax.ppermute(row, both, [turn(k, *place) for k in range(4, steps) for pla...  15.2 us
    ppermute x9, starting transfers between devices, per_device(): lax.ppermute(send, 'prow', routes[n][stage])  14.4 us
    pallas_call x6, Pallas kernels, halving(): pl.pallas_call(functools.partial(halving_kernel, group, stage), in_specs=...  12.8 us
    ppermute x2, waiting for transfers between devices, per_device(): turns = [lax.ppermute(sums, both, around(t)) for t in (2, 4)]  11.9 us
    ppermute x3, starting transfers between devices, per_device(): lax.ppermute(upper, both, here(one))  10.4 us
    ppermute x3, waiting for transfers between devices, per_device(): lax.ppermute(under, both, here(two))  8.35 us
  transfers between devices with their start and end apart: 30, of which 15 were waited for; matrix products, arithmetic and copies ran while one was open for 3% of the time, Pallas kernels for 18%

profile of v3, /device:TPU:0, one launch (start us, length us, event | category | flops | bytes accessed | tf_op | source)
XLA Modules:
  0.0 217.2 jit_solution(14440093680011477517)
XLA Ops:
  0.9 1.7 collective-permute-start
  5.5 2.1 collective-permute-start.1
  7.6 3.6 %collective-permute-start.2 = (bf16[2,6,64,128]{3,2,1,0:T(8,128)(2,1)S(1)}, bf16[2,6,64,128]{3,2,1,0:T(8,128)(2,1)S(1)}, u32[]{:S(2)}, u32[]{:S(2)}) collective-permute-start(bf16[2,6,64,128]{3,2,1,0:T(8,128)(2,1)S(1)} %maximum_select_fusion), channel_id=1, source_target_pairs={{0,64},{16,80},{32,96},{48,112},{64,0},{80,16},{96,32},{112,48},{1... | collective-permute-start | bytes 589832 | tf_op jit(solution)/shard_map/ppermute | solution.py:418
  13.0 1.6 collective-permute-done.1
  14.6 4.6 %collective-permute-done.2 = bf16[2,6,64,128]{3,2,1,0:T(8,128)(2,1)S(1)} collective-permute-done((bf16[2,6,64,128]{3,2,1,0:T(8,128)(2,1)S(1)}, bf16[2,6,64,128]{3,2,1,0:T(8,128)(2,1)S(1)}, u32[]{:S(2)}, u32[]{:S(2)}) %collective-permute-start.2) | collective-permute-done | bytes 196640 | tf_op jit(solution)/shard_map/ppermute | solution.py:418
  19.5 11.1 %products.2 = (f32[18,9,128,128]{3,2,1,0:T(8,128)}, f32[6,128,1152]{2,1,0:T(8,128)}) custom-call(s32[34,6]{1,0:T(8,128)} %copy.36.masks, f32[18,9,128,128]{3,2,1,0:T(8,128)} %bitcast.11, bf16[18,6,128,128]{3,2,1,0:T(8,128)(2,1)} %bitcast.13), custom_call_target="tpu_custom_call" | custom-call | flops 3623878656 | bytes 9437184 | tf_op jit(solution)/shard_map/products/pallas_call | solution.py:70
  30.6 12.9 %products.3 = (f32[18,9,128,128]{3,2,1,0:T(8,128)}, f32[6,128,1152]{2,1,0:T(8,128)}) custom-call(s32[34,6]{1,0:T(8,128)} %copy.36.masks, f32[18,9,128,128]{3,2,1,0:T(8,128)} %bitcast.12, bf16[18,6,128,128]{3,2,1,0:T(8,128)(2,1)} %bitcast.14, f32[18,9,128,128]{3,2,1,0:T(8,128)} %get-tuple-element.30.refs_0_), custom_call_target="tpu_custom_call", output_to_operand_aliasing={{0}: (3, {})} | custom-call | flops 4529848320 | bytes 11796480 | tf_op jit(solution)/shard_map/products/pallas_call | solution.py:70
  44.3 7.8 %eliminate.1 = (f32[3,128,384]{2,1,0:T(8,128)}, f32[3,128,384]{2,1,0:T(8,128)}, f32[4,128,384]{2,1,0:T(8,128)}, f32[4,128,384]{2,1,0:T(8,128)}, f32[4,128,384]{2,1,0:T(8,128)}, /*index=5*/f32[4,128,384]{2,1,0:T(8,128)}) custom-call(s32[34,6]{1,0:T(8,128)} %copy.36.masks, f32[6,128,1152]{2,1,0:T(8,128)} %get-tuple-element.29.refs_0_, ...), custom_call_target="tpu_custom_call" | custom-call | flops 884736000 | bytes 17694720 | tf_op jit(solution)/shard_map/eliminate/pallas_call | solution.py:162
  53.3 1.6 collective-permute-start.11
  56.2 14.1 %collective-permute-done.5.came_ref = f32[3,128,384]{2,1,0:T(8,128)S(1)} collective-permute-done((f32[3,128,384]{2,1,0:T(8,128)}, f32[3,128,384]{2,1,0:T(8,128)S(1)}, u32[]{:S(2)}, u32[]{:S(2)}) %collective-permute-start.5) | collective-permute-done | bytes 589856 | tf_op jit(solution)/shard_map/ppermute | solution.py:443
  71.1 2.2 %halving.6 = (f32[2,128,384]{2,1,0:T(8,128)}, f32[2,128,384]{2,1,0:T(8,128)}) custom-call(s32[34,6]{1,0:T(8,128)} %copy.36.masks, f32[3,128,384]{2,1,0:T(8,128)} %get-tuple-element.32.stay_ref, f32[3,128,384]{2,1,0:T(8,128)} %copy-done.5), custom_call_target="tpu_custom_call" | custom-call | flops 100000000 | bytes 1572864 | tf_op jit(solution)/shard_map/halving/pallas_call | solution.py:182
  75.0 2.4 %halving.8 = (f32[2,128,384]{2,1,0:T(8,128)}, f32[2,128,384]{2,1,0:T(8,128)}) custom-call(s32[34,6]{1,0:T(8,128)} %copy.36.masks, f32[4,128,384]{2,1,0:T(8,128)} %get-tuple-element.38.stay_ref, f32[4,128,384]{2,1,0:T(8,128)} %copy-done.4), custom_call_target="tpu_custom_call" | custom-call | flops 100000000 | bytes 1572864 | tf_op jit(solution)/shard_map/halving/pallas_call | solution.py:182
  77.4 1.3 collective-permute-start.9
  79.6 2.4 %halving.10 = (f32[2,128,384]{2,1,0:T(8,128)}, f32[2,128,384]{2,1,0:T(8,128)}) custom-call(s32[34,6]{1,0:T(8,128)} %copy.36.masks, f32[4,128,384]{2,1,0:T(8,128)} %get-tuple-element.44.stay_ref, f32[4,128,384]{2,1,0:T(8,128)} %copy-done.3), custom_call_target="tpu_custom_call" | custom-call | flops 100000000 | bytes 1572864 | tf_op jit(solution)/shard_map/halving/pallas_call | solution.py:182
  84.4 1.9 halving.7
  86.4 1.3 collective-permute-start.7
  87.7 2.9 %collective-permute-done.9.came_ref = f32[2,128,384]{2,1,0:T(8,128)S(1)} collective-permute-done((f32[2,128,384]{2,1,0:T(8,128)}, f32[2,128,384]{2,1,0:T(8,128)S(1)}, u32[]{:S(2)}, u32[]{:S(2)}) %collective-permute-start.9) | collective-permute-done | bytes 393248 | tf_op jit(solution)/shard_map/ppermute | solution.py:443
  91.3 1.9 halving.9
  93.2 3.1 %collective-permute-start.10 = (f32[1,128,384]{2,1,0:T(8,128)}, f32[1,128,384]{2,1,0:T(8,128)S(1)}, u32[]{:S(2)}, u32[]{:S(2)}) collective-permute-start(f32[1,128,384]{2,1,0:T(8,128)} %get-tuple-element.43), channel_id=1, source_target_pairs={{0,16},{16,0},{32,48},{48,32},{64,80},{80,64},{1,17},{17,1},{33,49... | collective-permute-start | bytes 589832 | tf_op jit(solution)/shard_map/ppermute | solution.py:443
  97.1 1.9 halving.11
  99.0 2.7 %collective-permute-start.13 = (f32[1,128,384]{2,1,0:T(8,128)}, f32[1,128,384]{2,1,0:T(8,128)S(1)}, u32[]{:S(2)}, u32[]{:S(2)}) collective-permute-start(f32[1,128,384]{2,1,0:T(8,128)} %get-tuple-element.49), channel_id=1, source_target_pairs={{0,32},{16,48},{32,0},{48,16},{96,64},{112,80},{1,33},{17,49},{33,... | collective-permute-start | bytes 589832 | tf_op jit(solution)/shard_map/ppermute | solution.py:443
  101.8 5.0 %collective-permute-done.13.refs_5_ = f32[1,128,384]{2,1,0:T(8,128)S(1)} collective-permute-done((f32[1,128,384]{2,1,0:T(8,128)}, f32[1,128,384]{2,1,0:T(8,128)S(1)}, u32[]{:S(2)}, u32[]{:S(2)}) %collective-permute-start.13) | collective-permute-done | bytes 196640 | tf_op jit(solution)/shard_map/ppermute | solution.py:443
  107.5 2.2 %row.1.refs_0_ = f32[128,1152]{1,0:T(8,128)} custom-call(s32[34,6]{1,0:T(8,128)} %copy.36.masks, f32[1,128,384]{2,1,0:T(8,128)} %get-tuple-element.36.refs_0_, f32[1,128,384]{2,1,0:T(8,128)} %copy-done.14, f32[1,128,384]{2,1,0:T(8,128)} %get-tuple-element.42.refs_2_, f32[1,128,384]{2,1,0:T(8,128)} %copy-done.15, f32[1,128,384]{2,1,0:T(8,128)} %get-tuple-element.48.refs_4_, ...), custom_call_target="tpu_custom_call" | custom-call | flops 10000000 | bytes 2359296 | tf_op jit(solution)/shard_map/row/pallas_call | solution.py:206
  109.7 1.3 collective-permute-start.15
  111.0 1.7 collective-permute-start.14
  112.7 15.2 %collective-permute-done.15 = f32[128,1152]{1,0:T(8,128)S(1)} collective-permute-done((f32[128,1152]{1,0:T(8,128)}, f32[128,1152]{1,0:T(8,128)S(1)}, u32[]{:S(2)}, u32[]{:S(2)}) %collective-permute-start.15) | collective-permute-done | bytes 589856 | tf_op jit(solution)/shard_map/ppermute | solution.py:459
  128.0 4.7 %collective-permute-start.16 = (f32[128,1152]{1,0:T(8,128)S(1)}, f32[128,1152]{1,0:T(8,128)S(1)}, u32[]{:S(2)}, u32[]{:S(2)}) collective-permute-start(f32[128,1152]{1,0:T(8,128)S(1)} %broadcast_select_fusion.1), channel_id=1, source_target_pairs={{0,4},{16,20},{32,36},{48,52},{1,5},{17,21},{33,37},{49,53},{68,64... | collective-permute-start | bytes 1769480 | tf_op jit(solution)/shard_map/ppermute | solution.py:464
  132.7 1.3 collective-permute-start.17
  134.9 5.1 %collective-permute-done.16 = f32[128,1152]{1,0:T(8,128)S(1)} collective-permute-done((f32[128,1152]{1,0:T(8,128)S(1)}, f32[128,1152]{1,0:T(8,128)S(1)}, u32[]{:S(2)}, u32[]{:S(2)}) %collective-permute-start.16) | collective-permute-done | bytes 589856 | tf_op jit(solution)/shard_map/ppermute | solution.py:464
  141.0 5.0 %collective-permute-done.17 = f32[128,1152]{1,0:T(8,128)S(1)} collective-permute-done((f32[128,1152]{1,0:T(8,128)S(1)}, f32[128,1152]{1,0:T(8,128)S(1)}, u32[]{:S(2)}, u32[]{:S(2)}) %collective-permute-start.17) | collective-permute-done | bytes 589856 | tf_op jit(solution)/shard_map/ppermute | solution.py:460
  146.9 4.2 %column.1 = (f32[64,768]{1,0:T(8,128)}, f32[64,768]{1,0:T(8,128)}) custom-call(s32[34,6]{1,0:T(8,128)} %copy.36.masks, f32[128,1152]{1,0:T(8,128)} %select_select_fusion.refs_0_.refs_1_, f32[128,1152]{1,0:T(8,128)} %broadcast_select_fusion.refs_1_.refs_2_, bf16[18,6,128,128]{3,2,1,0:T(8,128)(2,1)} %bitcast.15), custom_call_target="tpu_custom_call" | custom-call | flops 905969664 | bytes 6000000 | tf_op jit(solution)/shard_map/column/pallas_call | solution.py:242
  151.1 2.3 %collective-permute-start.22 = (f32[64,768]{1,0:T(8,128)}, f32[64,768]{1,0:T(8,128)S(1)}, u32[]{:S(2)}, u32[]{:S(2)}) collective-permute-start(f32[64,768]{1,0:T(8,128)} %get-tuple-element.51), channel_id=1, source_target_pairs={{0,32},{1,33},{2,34},{3,35},{4,36},{5,37},{16,48},{17,49},{18,50},... | collective-permute-start | bytes 589832 | tf_op jit(solution)/shard_map/ppermute | solution.py:475
  153.4 3.5 %collective-permute-start.19 = (f32[64,768]{1,0:T(8,128)}, f32[64,768]{1,0:T(8,128)S(1)}, u32[]{:S(2)}, u32[]{:S(2)}) collective-permute-start(f32[64,768]{1,0:T(8,128)} %get-tuple-element.50), channel_id=1, source_target_pairs={{0,16},{1,17},{2,18},{3,19},{4,20},{5,21},{16,0},{17,1},{18,2},{19... | collective-permute-start | bytes 589832 | tf_op jit(solution)/shard_map/ppermute | solution.py:475
  156.9 3.5 %collective-permute-done.22 = f32[64,768]{1,0:T(8,128)S(1)} collective-permute-done((f32[64,768]{1,0:T(8,128)}, f32[64,768]{1,0:T(8,128)S(1)}, u32[]{:S(2)}, u32[]{:S(2)}) %collective-permute-start.22) | collective-permute-done | bytes 196640 | tf_op jit(solution)/shard_map/ppermute | solution.py:475
  161.4 1.9 collective-permute-start.23
  164.3 2.7 %collective-permute-start.20 = (f32[64,768]{1,0:T(8,128)S(1)}, f32[64,768]{1,0:T(8,128)S(1)}, u32[]{:S(2)}, u32[]{:S(2)}) collective-permute-start(f32[64,768]{1,0:T(8,128)S(1)} %add.82), channel_id=1, source_target_pairs={{0,32},{1,33},{2,34},{3,35},{4,36},{5,37},{16,48},{17,49},{18,50},... | collective-permute-start | bytes 589832 | tf_op jit(solution)/shard_map/ppermute | solution.py:475
  166.9 3.9 %collective-permute-done.23 = f32[64,768]{1,0:T(8,128)S(1)} collective-permute-done((f32[64,768]{1,0:T(8,128)S(1)}, f32[64,768]{1,0:T(8,128)S(1)}, u32[]{:S(2)}, u32[]{:S(2)}) %collective-permute-start.23) | collective-permute-done | bytes 196640 | tf_op jit(solution)/shard_map/ppermute | solution.py:475
  170.8 2.3 %collective-permute-start.24 = (f32[64,768]{1,0:T(8,128)S(1)}, f32[64,768]{1,0:T(8,128)S(1)}, u32[]{:S(2)}, u32[]{:S(2)}) collective-permute-start(f32[64,768]{1,0:T(8,128)S(1)} %add.86), channel_id=1, source_target_pairs={{0,16},{1,17},{2,18},{3,19},{4,20},{5,21},{16,0},{17,1},{18,2},{19... | collective-permute-start | bytes 589832 | tf_op jit(solution)/shard_map/ppermute | solution.py:475
  173.1 4.2 %collective-permute-start.21 = (f32[64,768]{1,0:T(8,128)S(1)}, f32[64,768]{1,0:T(8,128)S(1)}, u32[]{:S(2)}, u32[]{:S(2)}) collective-permute-start(f32[64,768]{1,0:T(8,128)S(1)} %add.83), channel_id=1, source_target_pairs={{0,96},{1,97},{2,98},{3,99},{4,100},{5,101},{16,112},{17,113},{18,... | collective-permute-start | bytes 589832 | tf_op jit(solution)/shard_map/ppermute | solution.py:475
  178.4 3.5 %collective-permute-done.21 = f32[64,768]{1,0:T(8,128)S(1)} collective-permute-done((f32[64,768]{1,0:T(8,128)S(1)}, f32[64,768]{1,0:T(8,128)S(1)}, u32[]{:S(2)}, u32[]{:S(2)}) %collective-permute-start.21) | collective-permute-done | bytes 196640 | tf_op jit(solution)/shard_map/ppermute | solution.py:475
  182.0 4.4 %collective-permute-start.25 = (f32[128,768]{1,0:T(8,128)S(1)}, f32[128,768]{1,0:T(8,128)S(1)}, u32[]{:S(2)}, u32[]{:S(2)}) collective-permute-start(f32[128,768]{1,0:T(8,128)S(1)} %pad_maximum_fusion.1.refs_0_), channel_id=1, source_target_pairs={{0,18},{16,2},{32,50},{48,34},{64,82},{80,66},{96,114},{112,98},{1... | collective-permute-start | bytes 1179656 | tf_op jit(solution)/shard_map/ppermute | solution.py:487
  186.4 1.9 collective-permute-start.26
  188.3 1.9 collective-permute-start.27
  190.3 11.9 %collective-permute-done.25.refs_1_ = f32[128,768]{1,0:T(8,128)S(1)} collective-permute-done((f32[128,768]{1,0:T(8,128)S(1)}, f32[128,768]{1,0:T(8,128)S(1)}, u32[]{:S(2)}, u32[]{:S(2)}) %collective-permute-start.25) | collective-permute-done | bytes 393248 | tf_op jit(solution)/shard_map/ppermute | solution.py:487
  202.2 1.9 collective-permute-start.28
  204.1 2.4 %collective-permute-start.29 = (f32[128,768]{1,0:T(8,128)S(1)}, f32[128,768]{1,0:T(8,128)S(1)}, u32[]{:S(2)}, u32[]{:S(2)}) collective-permute-start(f32[128,768]{1,0:T(8,128)S(1)} %collective-permute-done.26.refs_2_), channel_id=1, source_target_pairs={{0,1},{1,0},{2,3},{3,2},{4,5},{5,4},{16,17},{17,16},{18,19},{19,18... | collective-permute-start | bytes 1179656 | tf_op jit(solution)/shard_map/ppermute | solution.py:489
  206.6 3.0 %patch.1.refs_9_ = f32[18,9,128,128]{3,2,1,0:T(8,128)} custom-call(s32[34,6]{1,0:T(8,128)} %copy.36.masks, f32[128,1152]{1,0:T(8,128)} %row.1.refs_0_, f32[128,1152]{1,0:T(8,128)} %select_select_fusion.refs_0_.refs_1_, f32[128,1152]{1,0:T(8,128)} %broadcast_select_fusion.refs_1_.refs_2_, ...), custom_call_target="tpu_custom_call", output_to_operand_aliasing={{}: (4, {})} | custom-call | flops 100000000 | bytes 4000000 | tf_op jit(solution)/shard_map/patch/pallas_call | solution.py:368
  211.3 5.8 %corner.1 = f32[18,9,128,128]{3,2,1,0:T(8,128)} custom-call(s32[34,6]{1,0:T(8,128)} %copy.36.masks, f32[128,768]{1,0:T(8,128)} %copy-done.2, f32[128,768]{1,0:T(8,128)} %copy-done.9, f32[128,768]{1,0:T(8,128)} %copy-done.10, f32[128,768]{1,0:T(8,128)} %copy-done.11, f32[128,768]{1,0:T(8,128)} %copy-done.12, ...), custom_call_target="tpu_custom_call", output_to_operand_aliasing={{}: (10, {})} | custom-call | flops 1000000000 | bytes 1000000 | tf_op jit(solution)/shard_map/corner/pallas_call | solution.py:298
  (88 shorter events, 24.6 us)
Async XLA Ops:
  0.9 4.6 %collective-permute-start = (bf16[1,6,64,128]{3,2,1,0:T(8,128)(2,1)S(1)}, bf16[1,6,64,128]{3,2,1,0:T(8,128)(2,1)S(1)}, u32[]{:S(2)}, u32[]{:S(2)}) collective-permute-start(bf16[1,6,64,128]{3,2,1,0:T(8,128)(2,1)S(1)} %dynamic-slice_bitcast_fusion), channel_id=1, source_target_pairs={{0,16},{16,0},{32,48},{48,32},{64,80},{80,64},{96,112},{112,96},{1... | collective-permute-start | bytes 294920 | tf_op jit(solution)/shard_map/ppermute | solution.py:417
  5.5 9.1 %collective-permute-start.1 = (bf16[2,6,64,128]{3,2,1,0:T(8,128)(2,1)S(1)}, bf16[2,6,64,128]{3,2,1,0:T(8,128)(2,1)S(1)}, u32[]{:S(2)}, u32[]{:S(2)}) collective-permute-start(bf16[2,6,64,128]{3,2,1,0:T(8,128)(2,1)S(1)} %maximum_select_fusion), channel_id=1, source_target_pairs={{0,32},{16,48},{32,64},{48,80},{64,96},{80,112},{96,0},{112,16},{1... | collective-permute-start | bytes 589832 | tf_op jit(solution)/shard_map/ppermute | solution.py:418
  7.6 11.6 %collective-permute-start.2 = (bf16[2,6,64,128]{3,2,1,0:T(8,128)(2,1)S(1)}, bf16[2,6,64,128]{3,2,1,0:T(8,128)(2,1)S(1)}, u32[]{:S(2)}, u32[]{:S(2)}) collective-permute-start(bf16[2,6,64,128]{3,2,1,0:T(8,128)(2,1)S(1)} %maximum_select_fusion), channel_id=1, source_target_pairs={{0,64},{16,80},{32,96},{48,112},{64,0},{80,16},{96,32},{112,48},{1... | collective-permute-start | bytes 589832 | tf_op jit(solution)/shard_map/ppermute | solution.py:418
  11.2 8.0 %collective-permute-start.3 = (bf16[2,6,64,128]{3,2,1,0:T(8,128)(2,1)S(1)}, bf16[2,6,64,128]{3,2,1,0:T(8,128)(2,1)S(1)}, u32[]{:S(2)}, u32[]{:S(2)}) collective-permute-start(bf16[2,6,64,128]{3,2,1,0:T(8,128)(2,1)S(1)} %maximum_select_fusion), channel_id=1, source_target_pairs={{0,96},{16,112},{32,0},{48,16},{64,32},{80,48},{96,64},{112,80},{1... | collective-permute-start | bytes 589832 | tf_op jit(solution)/shard_map/ppermute | solution.py:418
  19.4 24.1 %copy-start = (bf16[6,6,64,128]{3,2,1,0:T(8,128)(2,1)}, bf16[6,6,64,128]{3,2,1,0:T(8,128)(2,1)S(1)}, u32[]{:S(2)}) copy-start(bf16[6,6,64,128]{3,2,1,0:T(8,128)(2,1)S(1)} %pad_maximum_fusion.refs_2_.refs_6_) | copy-start | bytes 1769476
  19.4 24.1 %collective-permute-start.4 = (bf16[6,6,64,128]{3,2,1,0:T(8,128)(2,1)S(1)}, bf16[6,6,64,128]{3,2,1,0:T(8,128)(2,1)S(1)}, u32[]{:S(2)}, u32[]{:S(2)}) collective-permute-start(bf16[6,6,64,128]{3,2,1,0:T(8,128)(2,1)S(1)} %pad_maximum_fusion.refs_2_.refs_6_), channel_id=1, source_target_pairs={{0,1},{1,0},{2,3},{3,2},{4,5},{5,4},{6,7},{7,6},{8,9},{9,8},{10,11... | collective-permute-start | bytes 1769480 | tf_op jit(solution)/shard_map/ppermute | solution.py:424
  43.5 0.8 copy-start.1
  52.1 22.0 %collective-permute-start.8 = (f32[4,128,384]{2,1,0:T(8,128)}, f32[4,128,384]{2,1,0:T(8,128)S(1)}, u32[]{:S(2)}, u32[]{:S(2)}) collective-permute-start(f32[4,128,384]{2,1,0:T(8,128)} %get-tuple-element.39), channel_id=1, source_target_pairs={{0,32},{16,48},{32,0},{48,16},{64,96},{80,112},{96,64},{112,80},{1... | collective-permute-start | bytes 2359304 | tf_op jit(solution)/shard_map/ppermute | solution.py:443
  53.3 25.3 %collective-permute-start.11 = (f32[4,128,384]{2,1,0:T(8,128)}, f32[4,128,384]{2,1,0:T(8,128)S(1)}, u32[]{:S(2)}, u32[]{:S(2)}) collective-permute-start(f32[4,128,384]{2,1,0:T(8,128)} %get-tuple-element.45), channel_id=1, source_target_pairs={{0,96},{16,112},{32,64},{48,80},{64,32},{80,48},{96,0},{112,16},{1... | collective-permute-start | bytes 2359304 | tf_op jit(solution)/shard_map/ppermute | solution.py:443
  54.9 15.4 %collective-permute-start.5 = (f32[3,128,384]{2,1,0:T(8,128)}, f32[3,128,384]{2,1,0:T(8,128)S(1)}, u32[]{:S(2)}, u32[]{:S(2)}) collective-permute-start(f32[3,128,384]{2,1,0:T(8,128)} %get-tuple-element.33), channel_id=1, source_target_pairs={{0,16},{16,0},{32,48},{48,32},{64,80},{80,64},{96,112},{112,96},{1... | collective-permute-start | bytes 1769480 | tf_op jit(solution)/shard_map/ppermute | solution.py:443
  70.3 0.8 copy-start.5
  73.3 10.3 %collective-permute-start.6 = (f32[2,128,384]{2,1,0:T(8,128)}, f32[2,128,384]{2,1,0:T(8,128)S(1)}, u32[]{:S(2)}, u32[]{:S(2)}) collective-permute-start(f32[2,128,384]{2,1,0:T(8,128)} %get-tuple-element.35), channel_id=1, source_target_pairs={{0,32},{16,48},{32,0},{48,16},{64,96},{80,112},{96,64},{112,80},{1... | collective-permute-start | bytes 1179656 | tf_op jit(solution)/shard_map/ppermute | solution.py:443
  74.1 0.9 copy-start.4
  77.4 13.1 %collective-permute-start.9 = (f32[2,128,384]{2,1,0:T(8,128)}, f32[2,128,384]{2,1,0:T(8,128)S(1)}, u32[]{:S(2)}, u32[]{:S(2)}) collective-permute-start(f32[2,128,384]{2,1,0:T(8,128)} %get-tuple-element.41), channel_id=1, source_target_pairs={{32,64},{48,80},{64,32},{80,48},{96,0},{112,16},{33,65},{49,81},{6... | collective-permute-start | bytes 1179656 | tf_op jit(solution)/shard_map/ppermute | solution.py:443
  78.7 0.9 copy-start.3
  82.0 14.4 %collective-permute-start.12 = (f32[2,128,384]{2,1,0:T(8,128)}, f32[2,128,384]{2,1,0:T(8,128)S(1)}, u32[]{:S(2)}, u32[]{:S(2)}) collective-permute-start(f32[2,128,384]{2,1,0:T(8,128)} %get-tuple-element.47), channel_id=1, source_target_pairs={{0,16},{16,0},{32,48},{48,32},{64,80},{80,64},{96,112},{112,96},{1... | collective-permute-start | bytes 1179656 | tf_op jit(solution)/shard_map/ppermute | solution.py:443
  83.6 0.8 copy-start.8
  86.4 15.4 %collective-permute-start.7 = (f32[1,128,384]{2,1,0:T(8,128)}, f32[1,128,384]{2,1,0:T(8,128)S(1)}, u32[]{:S(2)}, u32[]{:S(2)}) collective-permute-start(f32[1,128,384]{2,1,0:T(8,128)} %get-tuple-element.37), channel_id=1, source_target_pairs={{32,64},{48,80},{64,32},{80,48},{96,0},{112,16},{33,65},{49,81},{6... | collective-permute-start | bytes 589832 | tf_op jit(solution)/shard_map/ppermute | solution.py:443
  90.5 0.8 copy-start.6
  93.2 8.6 %collective-permute-start.10 = (f32[1,128,384]{2,1,0:T(8,128)}, f32[1,128,384]{2,1,0:T(8,128)S(1)}, u32[]{:S(2)}, u32[]{:S(2)}) collective-permute-start(f32[1,128,384]{2,1,0:T(8,128)} %get-tuple-element.43), channel_id=1, source_target_pairs={{0,16},{16,0},{32,48},{48,32},{64,80},{80,64},{1,17},{17,1},{33,49... | collective-permute-start | bytes 589832 | tf_op jit(solution)/shard_map/ppermute | solution.py:443
  96.3 0.8 copy-start.7
  99.0 7.8 %collective-permute-start.13 = (f32[1,128,384]{2,1,0:T(8,128)}, f32[1,128,384]{2,1,0:T(8,128)S(1)}, u32[]{:S(2)}, u32[]{:S(2)}) collective-permute-start(f32[1,128,384]{2,1,0:T(8,128)} %get-tuple-element.49), channel_id=1, source_target_pairs={{0,32},{16,48},{32,0},{48,16},{96,64},{112,80},{1,33},{17,49},{33,... | collective-permute-start | bytes 589832 | tf_op jit(solution)/shard_map/ppermute | solution.py:443
  101.7 5.1 %copy-start.14 = (f32[1,128,384]{2,1,0:T(8,128)}, f32[1,128,384]{2,1,0:T(8,128)S(1)}, u32[]{:S(2)}) copy-start(f32[1,128,384]{2,1,0:T(8,128)S(1)} %collective-permute-done.7.refs_1_) | copy-start | bytes 589828
  101.8 5.0 %copy-start.15 = (f32[1,128,384]{2,1,0:T(8,128)}, f32[1,128,384]{2,1,0:T(8,128)S(1)}, u32[]{:S(2)}) copy-start(f32[1,128,384]{2,1,0:T(8,128)S(1)} %collective-permute-done.10.refs_3_) | copy-start | bytes 589828
  106.8 0.7 copy-start.16
  109.7 18.2 %collective-permute-start.15 = (f32[128,1152]{1,0:T(8,128)}, f32[128,1152]{1,0:T(8,128)S(1)}, u32[]{:S(2)}, u32[]{:S(2)}) collective-permute-start(f32[128,1152]{1,0:T(8,128)} %row.1.refs_0_), channel_id=1, source_target_pairs={{64,0},{65,16},{66,32},{67,48},{68,68},{69,84},{70,100},{71,116},{... | collective-permute-start | bytes 1769480 | tf_op jit(solution)/shard_map/ppermute | solution.py:459
  111.0 16.9 %collective-permute-start.14 = (f32[128,1152]{1,0:T(8,128)}, f32[128,1152]{1,0:T(8,128)S(1)}, u32[]{:S(2)}, u32[]{:S(2)}) collective-permute-start(f32[128,1152]{1,0:T(8,128)} %row.1.refs_0_), channel_id=1, source_target_pairs={{0,0},{1,16},{2,32},{3,48},{4,68},{5,84},{6,100},{7,116},{8,8},{9,... | collective-permute-start | bytes 1769480 | tf_op jit(solution)/shard_map/ppermute | solution.py:458
  128.0 12.1 %collective-permute-start.16 = (f32[128,1152]{1,0:T(8,128)S(1)}, f32[128,1152]{1,0:T(8,128)S(1)}, u32[]{:S(2)}, u32[]{:S(2)}) collective-permute-start(f32[128,1152]{1,0:T(8,128)S(1)} %broadcast_select_fusion.1), channel_id=1, source_target_pairs={{0,4},{16,20},{32,36},{48,52},{1,5},{17,21},{33,37},{49,53},{68,64... | collective-permute-start | bytes 1769480 | tf_op jit(solution)/shard_map/ppermute | solution.py:464
  132.7 13.3 %collective-permute-start.17 = (f32[128,1152]{1,0:T(8,128)S(1)}, f32[128,1152]{1,0:T(8,128)S(1)}, u32[]{:S(2)}, u32[]{:S(2)}) collective-permute-start(f32[128,1152]{1,0:T(8,128)S(1)} %collective-permute-done.14), channel_id=1, source_target_pairs={{8,0},{24,16},{40,32},{56,48},{76,64},{92,80},{108,96},{124,112},{... | collective-permute-start | bytes 1769480 | tf_op jit(solution)/shard_map/ppermute | solution.py:460
  134.0 12.0 %collective-permute-start.18 = (f32[128,1152]{1,0:T(8,128)S(1)}, f32[128,1152]{1,0:T(8,128)S(1)}, u32[]{:S(2)}, u32[]{:S(2)}) collective-permute-start(f32[128,1152]{1,0:T(8,128)S(1)} %collective-permute-done.15), channel_id=1, source_target_pairs={{8,4},{24,20},{40,36},{56,52},{76,68},{92,84},{108,100},{124,116},... | collective-permute-start | bytes 1769480 | tf_op jit(solution)/shard_map/ppermute | solution.py:461
  151.1 9.3 %collective-permute-start.22 = (f32[64,768]{1,0:T(8,128)}, f32[64,768]{1,0:T(8,128)S(1)}, u32[]{:S(2)}, u32[]{:S(2)}) collective-permute-start(f32[64,768]{1,0:T(8,128)} %get-tuple-element.51), channel_id=1, source_target_pairs={{0,32},{1,33},{2,34},{3,35},{4,36},{5,37},{16,48},{17,49},{18,50},... | collective-permute-start | bytes 589832 | tf_op jit(solution)/shard_map/ppermute | solution.py:475
  153.4 9.9 %collective-permute-start.19 = (f32[64,768]{1,0:T(8,128)}, f32[64,768]{1,0:T(8,128)S(1)}, u32[]{:S(2)}, u32[]{:S(2)}) collective-permute-start(f32[64,768]{1,0:T(8,128)} %get-tuple-element.50), channel_id=1, source_target_pairs={{0,16},{1,17},{2,18},{3,19},{4,20},{5,21},{16,0},{17,1},{18,2},{19... | collective-permute-start | bytes 589832 | tf_op jit(solution)/shard_map/ppermute | solution.py:475
  161.4 9.4 %collective-permute-start.23 = (f32[64,768]{1,0:T(8,128)S(1)}, f32[64,768]{1,0:T(8,128)S(1)}, u32[]{:S(2)}, u32[]{:S(2)}) collective-permute-start(f32[64,768]{1,0:T(8,128)S(1)} %add.85), channel_id=1, source_target_pairs={{0,96},{1,97},{2,98},{3,99},{4,100},{5,101},{16,112},{17,113},{18,... | collective-permute-start | bytes 589832 | tf_op jit(solution)/shard_map/ppermute | solution.py:475
  164.3 8.8 %collective-permute-start.20 = (f32[64,768]{1,0:T(8,128)S(1)}, f32[64,768]{1,0:T(8,128)S(1)}, u32[]{:S(2)}, u32[]{:S(2)}) collective-permute-start(f32[64,768]{1,0:T(8,128)S(1)} %add.82), channel_id=1, source_target_pairs={{0,32},{1,33},{2,34},{3,35},{4,36},{5,37},{16,48},{17,49},{18,50},... | collective-permute-start | bytes 589832 | tf_op jit(solution)/shard_map/ppermute | solution.py:475
  170.8 7.6 %collective-permute-start.24 = (f32[64,768]{1,0:T(8,128)S(1)}, f32[64,768]{1,0:T(8,128)S(1)}, u32[]{:S(2)}, u32[]{:S(2)}) collective-permute-start(f32[64,768]{1,0:T(8,128)S(1)} %add.86), channel_id=1, source_target_pairs={{0,16},{1,17},{2,18},{3,19},{4,20},{5,21},{16,0},{17,1},{18,2},{19... | collective-permute-start | bytes 589832 | tf_op jit(solution)/shard_map/ppermute | solution.py:475
  173.1 8.8 %collective-permute-start.21 = (f32[64,768]{1,0:T(8,128)S(1)}, f32[64,768]{1,0:T(8,128)S(1)}, u32[]{:S(2)}, u32[]{:S(2)}) collective-permute-start(f32[64,768]{1,0:T(8,128)S(1)} %add.83), channel_id=1, source_target_pairs={{0,96},{1,97},{2,98},{3,99},{4,100},{5,101},{16,112},{17,113},{18,... | collective-permute-start | bytes 589832 | tf_op jit(solution)/shard_map/ppermute | solution.py:475
  182.0 27.6 %copy-start.2 = (f32[128,768]{1,0:T(8,128)}, f32[128,768]{1,0:T(8,128)S(1)}, u32[]{:S(2)}) copy-start(f32[128,768]{1,0:T(8,128)S(1)} %pad_maximum_fusion.1.refs_0_) | copy-start | bytes 1179652
  182.0 20.2 %collective-permute-start.25 = (f32[128,768]{1,0:T(8,128)S(1)}, f32[128,768]{1,0:T(8,128)S(1)}, u32[]{:S(2)}, u32[]{:S(2)}) collective-permute-start(f32[128,768]{1,0:T(8,128)S(1)} %pad_maximum_fusion.1.refs_0_), channel_id=1, source_target_pairs={{0,18},{16,2},{32,50},{48,34},{64,82},{80,66},{96,114},{112,98},{1... | collective-permute-start | bytes 1179656 | tf_op jit(solution)/shard_map/ppermute | solution.py:487
  186.4 17.7 %collective-permute-start.26 = (f32[128,768]{1,0:T(8,128)S(1)}, f32[128,768]{1,0:T(8,128)S(1)}, u32[]{:S(2)}, u32[]{:S(2)}) collective-permute-start(f32[128,768]{1,0:T(8,128)S(1)} %pad_maximum_fusion.1.refs_0_), channel_id=1, source_target_pairs={{0,4},{16,20},{32,36},{48,52},{64,68},{80,84},{96,100},{112,116},{... | collective-permute-start | bytes 1179656 | tf_op jit(solution)/shard_map/ppermute | solution.py:487
  188.3 21.3 %collective-permute-start.27 = (f32[128,768]{1,0:T(8,128)S(1)}, f32[128,768]{1,0:T(8,128)S(1)}, u32[]{:S(2)}, u32[]{:S(2)}) collective-permute-start(f32[128,768]{1,0:T(8,128)S(1)} %pad_maximum_fusion.1.refs_0_), channel_id=1, source_target_pairs={{0,1},{1,0},{2,3},{3,2},{4,5},{5,4},{16,17},{17,16},{18,19},{19,18... | collective-permute-start | bytes 1179656 | tf_op jit(solution)/shard_map/ppermute | solution.py:489
  202.2 7.4 %copy-start.9 = (f32[128,768]{1,0:T(8,128)}, f32[128,768]{1,0:T(8,128)S(1)}, u32[]{:S(2)}) copy-start(f32[128,768]{1,0:T(8,128)S(1)} %collective-permute-done.25.refs_1_) | copy-start | bytes 1179652
  202.2 7.4 %collective-permute-start.28 = (f32[128,768]{1,0:T(8,128)S(1)}, f32[128,768]{1,0:T(8,128)S(1)}, u32[]{:S(2)}, u32[]{:S(2)}) collective-permute-start(f32[128,768]{1,0:T(8,128)S(1)} %collective-permute-done.25.refs_1_), channel_id=1, source_target_pairs={{0,1},{1,0},{2,3},{3,2},{4,5},{5,4},{16,17},{17,16},{18,19},{19,18... | collective-permute-start | bytes 1179656 | tf_op jit(solution)/shard_map/ppermute | solution.py:489
  204.1 5.5 %copy-start.10 = (f32[128,768]{1,0:T(8,128)}, f32[128,768]{1,0:T(8,128)S(1)}, u32[]{:S(2)}) copy-start(f32[128,768]{1,0:T(8,128)S(1)} %collective-permute-done.26.refs_2_) | copy-start | bytes 1179652
  204.1 5.5 %collective-permute-start.29 = (f32[128,768]{1,0:T(8,128)S(1)}, f32[128,768]{1,0:T(8,128)S(1)}, u32[]{:S(2)}, u32[]{:S(2)}) collective-permute-start(f32[128,768]{1,0:T(8,128)S(1)} %collective-permute-done.26.refs_2_), channel_id=1, source_target_pairs={{0,1},{1,0},{2,3},{3,2},{4,5},{5,4},{16,17},{17,16},{18,19},{19,18... | collective-permute-start | bytes 1179656 | tf_op jit(solution)/shard_map/ppermute | solution.py:489
  209.6 0.8 copy-start.11
  209.7 0.9 copy-start.12
  210.5 0.7 copy-start.13

commit v4 on v3

--- a/solution.py
+++ b/solution.py
@@ -9,7 +9,7 @@
 
 
 F32, BF16 = jnp.float32, jnp.bfloat16
-PARTS = ((0, 8), (8, 10))
+BATCHES = ((0, 1), (2,))
 SIZES = (3, 4, 4)
 CORNER, COLS, IDS = 18, 24, 33
 VMEM = pl.BlockSpec(memory_space=pltpu.VMEM)
@@ -30,27 +30,45 @@
     return jnp.dot(left, right, preferred_element_type=F32)
 
 
-def product_kernel(start, masks, x_ref, u_ref, *refs):
+def turned_kernel(masks, u_ref, out_ref):
+    rows, steps, width, _ = u_ref.shape
+    first = pl.program_id(0) * rows
+    for k in range(steps):
+        blocks = []
+        for r in range(rows):
+            block = u_ref[r, k]
+            blocks.append(jnp.where(masks[first + r, k] > 0, block, jnp.zeros_like(block)))
+        out_ref[pl.ds(k * width, width), :] = jnp.concatenate(blocks, axis=0).T
+
+
+def turned_factor(masks, lower, rows=6):
+    row_blocks, steps, width, _ = lower.shape
+    return pl.pallas_call(
+        turned_kernel,
+        grid_spec=pltpu.PrefetchScalarGridSpec(
+            num_scalar_prefetch=1,
+            grid=(row_blocks // rows,),
+            in_specs=[pl.BlockSpec((rows, steps, width, width), lambda i, _: (i, 0, 0, 0))],
+            out_specs=pl.BlockSpec((steps * width, rows * width), lambda i, _: (0, i)),
+        ),
+        out_shape=jax.ShapeDtypeStruct((steps * width, row_blocks * width), BF16),
+        cost_estimate=pl.CostEstimate(flops=2 * 10**9, bytes_accessed=4 * lower.size, transcendentals=0),
+        name="turned",
+    )(masks, lower)
+
+
+def product_kernel(x_ref, u_ref, *refs):
     copy_ref, out_ref = refs[-2:]
     step = pl.program_id(0)
     rows, cols, _, _ = x_ref.shape
-    steps = u_ref.shape[1]
-    left, high, low = [], [], []
+    high, low = [], []
     for r in range(rows):
-        wide = []
-        for k in range(steps):
-            block = u_ref[r, k]
-            wide.append(jnp.where(masks[start + step * rows + r, k] > 0, block, jnp.zeros_like(block)))
-        left.append(jnp.concatenate(wide, axis=1))
-        value = jnp.concatenate([x_ref[r, c] for c in range(cols)], axis=1)
-        for c in range(cols):
-            copy_ref[r, c] = x_ref[r, c]
-        a, b = halves(value)
+        a, b = halves(jnp.concatenate([x_ref[r, c] for c in range(cols)], axis=1))
         high.append(a)
         low.append(b)
-    left = jnp.concatenate(left, axis=0).T
-    both = jnp.concatenate([left, left], axis=1)
-    term = dot(both, jnp.concatenate(high + low, axis=0))
+    copy_ref[...] = x_ref[...]
+    left = u_ref[...]
+    term = dot(left, jnp.concatenate(high, axis=0)) + dot(left, jnp.concatenate(low, axis=0))
     term = term.reshape(out_ref.shape)
 
     @pl.when(step == 0)
@@ -62,36 +80,32 @@
         out_ref[...] += term
 
 
-def products(blocks, lower, masks, whole, first, count, rows=2):
-    _, cols, width, _ = blocks.shape
-    steps = lower.shape[1]
-    start = first // rows
-    known = [] if whole is None else [whole]
-    return pl.pallas_call(
-        functools.partial(product_kernel, first),
-        grid_spec=pltpu.PrefetchScalarGridSpec(
-            num_scalar_prefetch=1,
-            grid=(count // rows,),
-            in_specs=[
-                pl.BlockSpec((rows, cols, width, width), lambda i, _: (start + i, 0, 0, 0)),
-                pl.BlockSpec((rows, steps, width, width), lambda i, _: (start + i, 0, 0, 0)),
-            ]
-            + [ANY] * len(known),
-            out_specs=[
-                pl.BlockSpec((rows, cols, width, width), lambda i, _: (start + i, 0, 0, 0)),
-                pl.BlockSpec((steps, width, cols * width), lambda i, _: (0, 0, 0)),
-            ],
-        ),
+def products(blocks, turned, known, group, rows=6):
+    row_blocks, cols, width, _ = blocks.shape
+    tall = turned.shape[0]
+    cols = cols // len(SIZES)
+    return pl.pallas_call(
+        product_kernel,
+        grid=(row_blocks // rows,),
+        in_specs=[
+            pl.BlockSpec((rows, cols, width, width), lambda i: (i, group, 0, 0)),
+            pl.BlockSpec((tall, rows * width), lambda i: (0, i)),
+        ]
+        + [ANY] * len(known),
+        out_specs=[
+            pl.BlockSpec((rows, cols, width, width), lambda i: (i, group, 0, 0)),
+            pl.BlockSpec((tall // width, width, cols * width), lambda i: (0, 0, 0)),
+        ],
         out_shape=[
             jax.ShapeDtypeStruct(blocks.shape, F32),
-            jax.ShapeDtypeStruct((steps, width, cols * width), F32),
+            jax.ShapeDtypeStruct((tall // width, width, cols * width), F32),
         ],
-        input_output_aliases={3: 0} if known else {},
+        input_output_aliases={2: 0} if known else {},
         cost_estimate=pl.CostEstimate(
-            flops=4 * count * cols * steps * width**3, bytes_accessed=8 * count * cols * width**2, transcendentals=0
+            flops=4 * row_blocks * cols * tall * width**2, bytes_accessed=8 * row_blocks * cols * width**2, transcendentals=0
         ),
         name="products",
-    )(masks, blocks, lower, *known)
+    )(blocks, turned, *known)
 
 
 def first_pieces(z, y):
@@ -129,16 +143,12 @@
     return p, q, p // 2, p % 2
 
 
-def eliminate_kernel(masks, *refs):
-    *part_refs, u_ref, v_ref = refs[: -2 * len(SIZES) - 1]
-    places, w_ref = refs[-2 * len(SIZES) - 1 : -1], refs[-1]
+def eliminate_kernel(group, masks, part_ref, u_ref, v_ref, send_ref, keep_ref, w_ref):
     steps = w_ref.shape[0]
     _, q, z, y = place_of(masks)
     high, low = [], []
     for k in reversed(range(steps)):
-        total = part_refs[0][k]
-        for ref in part_refs[1:]:
-            total = total + ref[k]
+        total = part_ref[k]
         if high:
             blocks = []
             for j in range(k + 1, steps):
@@ -151,23 +161,22 @@
         a, b = halves(total)
         high.append(a)
         low.append(b)
-    for n, (ref, pieces) in enumerate(zip(places, first_pieces(z, y))):
+    for ref, pieces in zip((send_ref, keep_ref), first_pieces(z, y)[2 * group : 2 * group + 2]):
         for m, k in enumerate(pieces):
-            ref[m] = w_ref[k, :, pl.ds(n // 2 * ref.shape[2], ref.shape[2])]
-
-
-def eliminate(masks, parts, corner):
-    _, width, wide = parts[0].shape
-    shapes = [jax.ShapeDtypeStruct((n, width, wide // len(SIZES)), F32) for n in SIZES for _ in range(2)]
-    return pl.pallas_call(
-        eliminate_kernel,
-        in_specs=[SMEM] + [VMEM] * (len(parts) + 2),
-        out_specs=[VMEM] * len(shapes),
-        out_shape=shapes,
-        scratch_shapes=[pltpu.VMEM(parts[0].shape, F32)],
-        cost_estimate=pl.CostEstimate(flops=1000 * parts[0].size, bytes_accessed=20 * parts[0].size, transcendentals=0),
+            ref[m] = w_ref[k]
+
+
+def eliminate(masks, group, part, corner):
+    _, width, wide = part.shape
+    return pl.pallas_call(
+        functools.partial(eliminate_kernel, group),
+        in_specs=[SMEM] + [VMEM] * 3,
+        out_specs=[VMEM] * 2,
+        out_shape=[jax.ShapeDtypeStruct((SIZES[group], width, wide), F32)] * 2,
+        scratch_shapes=[pltpu.VMEM(part.shape, F32)],
+        cost_estimate=pl.CostEstimate(flops=1000 * part.size, bytes_accessed=20 * part.size, transcendentals=0),
         name="eliminate",
-    )(masks, *parts, *corner)
+    )(masks, part, *corner)
 
 
 def halving_kernel(group, stage, masks, stay_ref, came_ref, send_ref, keep_ref):
@@ -189,7 +198,7 @@
     )(masks, stay, came)
 
 
-def row_kernel(masks, *refs):
+def row_kernel(first, masks, *refs):
     *given, row_ref = refs
     width = row_ref.shape[0]
     count = given[0].shape[2] // width
@@ -198,13 +207,13 @@
     for n in range(row_ref.shape[1] // width):
         part = pl.ds(n % count * width, width)
         value = given[n // count * 2][0, :, part] + given[n // count * 2 + 1][0, :, part]
-        row_ref[:, pl.ds(n * width, width)] = jnp.where(masks[COLS + n, k] > 0, value, jnp.zeros_like(value))
-
-
-def masked_row(masks, given):
+        row_ref[:, pl.ds(n * width, width)] = jnp.where(masks[COLS + first + n, k] > 0, value, jnp.zeros_like(value))
+
+
+def masked_row(masks, first, given):
     _, width, wide = given[0].shape
     return pl.pallas_call(
-        row_kernel,
+        functools.partial(row_kernel, first),
         in_specs=[SMEM] + [VMEM] * len(given),
         out_specs=VMEM,
         out_shape=jax.ShapeDtypeStruct((width, wide * len(given) // 2), F32),
@@ -213,40 +222,43 @@
     )(masks, *given)
 
 
-def column_kernel(masks, *refs):
-    *value_refs, u_ref, upper_ref, lower_ref = refs
+def column_kernel(first, masks, even_ref, odd_ref, u_ref, *refs):
+    *given, upper_ref, lower_ref = refs
     _, steps, width, _ = u_ref.shape
-    total, a = None, 0
-    for even_ref, odd_ref in zip(value_refs[::2], value_refs[1::2]):
-        for c in range(even_ref.shape[1] // width):
-            part = pl.ds(c * width, width)
-            value = jnp.concatenate([even_ref[:, part], odd_ref[:, part]], axis=1)
-            left = jnp.concatenate(halves(value), axis=0)
-            right = []
-            for r in (a, a + 1):
-                wide = []
-                for k in range(steps):
-                    block = u_ref[r, k]
-                    wide.append(jnp.where(masks[r, k] > 0, block, jnp.zeros_like(block)))
-                right.append(jnp.concatenate(wide, axis=1))
-            term = dot(left, jnp.concatenate(right, axis=0))
-            total = term if total is None else total + term
-            a += 2
+    total = None
+    for c in range(even_ref.shape[1] // width):
+        part = pl.ds(c * width, width)
+        value = jnp.concatenate([even_ref[:, part], odd_ref[:, part]], axis=1)
+        left = jnp.concatenate(halves(value), axis=0)
+        right = []
+        for r in (2 * c, 2 * c + 1):
+            wide = []
+            for k in range(steps):
+                block = u_ref[r, k]
+                wide.append(jnp.where(masks[first + r, k] > 0, block, jnp.zeros_like(block)))
+            right.append(jnp.concatenate(wide, axis=1))
+        term = dot(left, jnp.concatenate(right, axis=0))
+        total = term if total is None else total + term
     total = total[:width] + total[width:]
-    upper_ref[...] = total[: width // 2]
-    lower_ref[...] = total[width // 2 :]
-
-
-def column_products(values, lower, masks):
-    row_blocks, steps, width, _ = lower.shape
-    return pl.pallas_call(
-        column_kernel,
-        in_specs=[SMEM] + [VMEM] * (len(values) + 1),
+    for n, ref in enumerate((upper_ref, lower_ref)):
+        value = total[n * width // 2 : (n + 1) * width // 2]
+        ref[...] = value + given[n][...] if given else value
+
+
+def column_products(masks, first, even, odd, lower, given):
+    _, steps, width, _ = lower.shape
+    count = 2 * even.shape[1] // width
+    place = first // count
+    return pl.pallas_call(
+        functools.partial(column_kernel, first),
+        grid=(1,),
+        in_specs=[SMEM, VMEM, VMEM, pl.BlockSpec((count, steps, width, width), lambda i: (place, 0, 0, 0))]
+        + [VMEM] * len(given),
         out_specs=[VMEM] * 2,
         out_shape=[jax.ShapeDtypeStruct((width // 2, steps * width), F32)] * 2,
-        cost_estimate=pl.CostEstimate(flops=4 * row_blocks * steps * width**3, bytes_accessed=6 * 10**6, transcendentals=0),
+        cost_estimate=pl.CostEstimate(flops=4 * count * steps * width**3, bytes_accessed=4 * 10**6, transcendentals=0),
         name="column",
-    )(masks, *values, lower)
+    )(masks, even, odd, lower, *given)
 
 
 def corner_kernel(masks, *refs):
@@ -428,22 +440,21 @@
     def device(x, h, c, zz, yy):
         return at(zz, yy) * n_col + x * 4 + h * 2 + c
 
-    whole, parts = None, []
-    for first, count in PARTS:
-        whole, part = products(blocks, lower, masks, whole, first, count)
-        parts.append(part)
-
     over_m = [(s, d) for s, d in mirror if d < steps]
     over_y = [(s, d) for s, d in flip_y if d < steps]
     over_z = [(s, d) for s, d in flip_z if d < steps]
     routes = (flip_y, flip_z, over_m), (flip_z, over_m, over_y), (mirror, flip_y, over_z)
-    pieces = eliminate(masks, parts, corner)
-    held = [(pieces[2 * n], pieces[2 * n + 1]) for n in range(len(SIZES))]
-    for stage in range(3):
-        held = [(lax.ppermute(send, "prow", routes[n][stage]), keep) for n, (send, keep) in enumerate(held)]
-        if stage < 2:
-            held = [halving(masks, n, stage + 2, keep, came) for n, (came, keep) in enumerate(held)]
-    row = masked_row(masks, [v for came, keep in held for v in (keep, came)])
+    turned = turned_factor(masks, lower)
+    known, sums_of = [], []
+    for group in range(len(SIZES)):
+        whole, part = products(blocks, turned, known, group)
+        send, keep = eliminate(masks, group, part, corner)
+        known = [whole, keep]
+        for stage in range(3):
+            came = lax.ppermute(send, "prow", routes[group][stage])
+            if stage < 2:
+                send, keep = halving(masks, group, stage + 2, keep, came)
+        sums_of.append((keep, came))
 
     def turn(k, x, h, c):
         return at(k // 2, k % 2) * n_col + x * 4 + h * 2 + c, device(x, k // 2 % 2, k % 2, x % 2 * 2 + h, c)
@@ -455,17 +466,22 @@
         return device(start, h, c, zz, yy), device(end, h, c, zz, yy)
 
     x = q // 4
-    first = lax.ppermute(row, both, [turn(k, *place) for k in range(4) for place in grid])
-    second = lax.ppermute(row, both, [turn(k, *place) for k in range(4, steps) for place in grid])
-    odd0 = lax.ppermute(first, both, [slide(pl_, pl_[2] // 2 + 2, 0) for pl_ in places])
-    odd1 = lax.ppermute(second, both, [slide(pl_, pl_[2] // 2 + 2, 1) for pl_ in places if pl_[0] == 0])
-    route = [slide(pl_, 0, 1) for pl_ in places if pl_[2] // 2 == 0 and pl_[0] == 0]
-    route += [slide(pl_, 1, 0) for pl_ in places if pl_[2] // 2 == 1]
-    moved = lax.ppermute(jnp.where(x == 0, second, first), both, route)
-    mine = jnp.where(x == 0, first, second)
-    values = [row, jnp.where(x == z // 2, mine, moved), jnp.where(x == 0, odd0, odd1)]
-
-    upper, under = column_products(values[1:], lower, masks)
+    values, upper = [], ()
+    for batch in BATCHES:
+        start = batch[0] * cols // len(SIZES)
+        row = masked_row(masks, start, [v for group in batch for v in sums_of[group]])
+        first = lax.ppermute(row, both, [turn(k, *place) for k in range(4) for place in grid])
+        second = lax.ppermute(row, both, [turn(k, *place) for k in range(4, steps) for place in grid])
+        odd0 = lax.ppermute(first, both, [slide(pl_, pl_[2] // 2 + 2, 0) for pl_ in places])
+        odd1 = lax.ppermute(second, both, [slide(pl_, pl_[2] // 2 + 2, 1) for pl_ in places if pl_[0] == 0])
+        route = [slide(pl_, 0, 1) for pl_ in places if pl_[2] // 2 == 0 and pl_[0] == 0]
+        route += [slide(pl_, 1, 0) for pl_ in places if pl_[2] // 2 == 1]
+        moved = lax.ppermute(jnp.where(x == 0, second, first), both, route)
+        mine = jnp.where(x == 0, first, second)
+        even, odd = jnp.where(x == z // 2, mine, moved), jnp.where(x == 0, odd0, odd1)
+        values += [row, even, odd]
+        upper = column_products(masks, 2 * start, even, odd, lower, upper)
+    upper, under = upper
 
     def here(perm):
         return [(s * n_col + d, t * n_col + d) for s, t in perm for d in range(steps)]

time: 220 us -> 234 us (1.064)
  the two profiles are of different devices: /device:TPU:0 before, /device:TPU:25 now
where the time goes in v4:
time: 234 us; the launch traced here: 232 us
  starting transfers between devices  86.9 us (37%)
  Pallas kernels  75.4 us (32%)
  waiting for transfers between devices  50.9 us (22%)
  local copies, waits for them, and re-layouts  12.3 us (5%)
  other arithmetic  5.91 us (3%)
    pallas_call x3, Pallas kernels, products(): pl.pallas_call(product_kernel, grid=(row_blocks // rows,), in_specs=[pl.B...  24.9 us
    ppermute x9, waiting for transfers between devices, per_device(): came = lax.ppermute(send, 'prow', routes[group][stage])  19.7 us
    ppermute x3, starting transfers between devices, per_device(): lax.ppermute(upper, both, here(one))  14.7 us
    ppermute x2, starting transfers between devices, per_device(): turns = [lax.ppermute(sums, both, around(t)) for t in (2, 4)]  13.4 us
    pallas_call x6, Pallas kernels, halving(): pl.pallas_call(functools.partial(halving_kernel, group, stage), in_specs=...  12.7 us
    pallas_call x3, Pallas kernels, eliminate(): pl.pallas_call(functools.partial(eliminate_kernel, group), in_specs=[SMEM...  12.7 us
    ppermute x9, starting transfers between devices, per_device(): came = lax.ppermute(send, 'prow', routes[group][stage])  12.1 us
    ppermute x3, starting transfers between devices, per_device(): lax.ppermute(under, both, here(two))  11.3 us
  transfers between devices with their start and end apart: 35, of which 14 were waited for; matrix products, arithmetic and copies ran while one was open for 3% of the time, Pallas kernels for 15%

profile of v4, /device:TPU:25, one launch (start us, length us, event | category | flops | bytes accessed | tf_op | source)
XLA Modules:
  0.0 232.2 jit_solution(643804807862555558)
XLA Ops:
  4.4 1.7 collective-permute-start.1
  6.1 3.3 %collective-permute-start.2 = (bf16[2,6,64,128]{3,2,1,0:T(8,128)(2,1)S(1)}, bf16[2,6,64,128]{3,2,1,0:T(8,128)(2,1)S(1)}, u32[]{:S(2)}, u32[]{:S(2)}) collective-permute-start(bf16[2,6,64,128]{3,2,1,0:T(8,128)(2,1)S(1)} %maximum_select_fusion), channel_id=1, source_target_pairs={{0,64},{16,80},{32,96},{48,112},{64,0},{80,16},{96,32},{112,48},{1... | collective-permute-start | bytes 589832 | tf_op jit(solution)/shard_map/ppermute | solution.py:430
  10.1 1.5 collective-permute-done.1
  11.7 4.8 %collective-permute-done.2 = bf16[2,6,64,128]{3,2,1,0:T(8,128)(2,1)S(1)} collective-permute-done((bf16[2,6,64,128]{3,2,1,0:T(8,128)(2,1)S(1)}, bf16[2,6,64,128]{3,2,1,0:T(8,128)(2,1)S(1)}, u32[]{:S(2)}, u32[]{:S(2)}) %collective-permute-start.2) | collective-permute-done | bytes 196640 | tf_op jit(solution)/shard_map/ppermute | solution.py:430
  16.7 3.1 %collective-permute-start.4 = (bf16[6,6,64,128]{3,2,1,0:T(8,128)(2,1)S(1)}, bf16[6,6,64,128]{3,2,1,0:T(8,128)(2,1)S(1)}, u32[]{:S(2)}, u32[]{:S(2)}) collective-permute-start(bf16[6,6,64,128]{3,2,1,0:T(8,128)(2,1)S(1)} %pad_maximum_fusion.u_ref.refs_6_), channel_id=1, source_target_pairs={{0,1},{1,0},{2,3},{3,2},{4,5},{5,4},{6,7},{7,6},{8,9},{9,8},{10,11... | collective-permute-start | bytes 1769480 | tf_op jit(solution)/shard_map/ppermute | solution.py:436
  21.3 6.2 %turned.1.u_ref = bf16[768,2304]{1,0:T(8,128)(2,1)} custom-call(s32[34,6]{1,0:T(8,128)} %copy.40.masks, bf16[18,6,128,128]{3,2,1,0:T(8,128)(2,1)} %bitcast.14), custom_call_target="tpu_custom_call" | custom-call | flops 2000000000 | bytes 7077888 | tf_op jit(solution)/shard_map/turned/pallas_call | solution.py:46
  27.5 8.3 %products.3 = (f32[18,9,128,128]{3,2,1,0:T(8,128)}, f32[6,128,384]{2,1,0:T(8,128)}) custom-call(f32[18,9,128,128]{3,2,1,0:T(8,128)} %bitcast.11, bf16[768,2304]{1,0:T(8,128)(2,1)} %turned.1.u_ref), custom_call_target="tpu_custom_call" | custom-call | flops 2717908992 | bytes 7077888 | tf_op jit(solution)/shard_map/products/pallas_call | solution.py:87
  36.6 4.2 %eliminate.3 = (f32[3,128,384]{2,1,0:T(8,128)}, f32[3,128,384]{2,1,0:T(8,128)}) custom-call(s32[34,6]{1,0:T(8,128)} %copy.40.masks, f32[6,128,384]{2,1,0:T(8,128)} %get-tuple-element.34.part_ref, bf16[6,6,64,128]{3,2,1,0:T(8,128)(2,1)} %copy-done, bf16[6,6,64,128]{3,2,1,0:T(8,128)(2,1)} %copy-done.1), custom_call_target="tpu_custom_call" | custom-call | flops 294912000 | bytes 5898240 | tf_op jit(solution)/shard_map/eliminate/pallas_call | solution.py:171
  40.8 8.3 %products.4 = (f32[18,9,128,128]{3,2,1,0:T(8,128)}, f32[6,128,384]{2,1,0:T(8,128)}) custom-call(f32[18,9,128,128]{3,2,1,0:T(8,128)} %bitcast.12, bf16[768,2304]{1,0:T(8,128)(2,1)} %turned.1.u_ref, f32[18,9,128,128]{3,2,1,0:T(8,128)} %get-tuple-element.33.refs_0_, f32[3,128,384]{2,1,0:T(8,128)} %get-tuple-element.35.refs_1_.stay_ref), custom_call_target="tpu_custom_call", output_to_operand_aliasing={{0}: (2, {})} | custom-call | flops 2717908992 | bytes 7077888 | tf_op jit(solution)/shard_map/products/pallas_call | solution.py:87
  49.1 4.2 %eliminate.4 = (f32[4,128,384]{2,1,0:T(8,128)}, f32[4,128,384]{2,1,0:T(8,128)}) custom-call(s32[34,6]{1,0:T(8,128)} %copy.40.masks, f32[6,128,384]{2,1,0:T(8,128)} %get-tuple-element.37.part_ref, bf16[6,6,64,128]{3,2,1,0:T(8,128)(2,1)} %copy-done, bf16[6,6,64,128]{3,2,1,0:T(8,128)(2,1)} %copy-done.1), custom_call_target="tpu_custom_call" | custom-call | flops 294912000 | bytes 5898240 | tf_op jit(solution)/shard_map/eliminate/pallas_call | solution.py:171
  53.4 8.4 %products.5 = (f32[18,9,128,128]{3,2,1,0:T(8,128)}, f32[6,128,384]{2,1,0:T(8,128)}) custom-call(f32[18,9,128,128]{3,2,1,0:T(8,128)} %bitcast.13, bf16[768,2304]{1,0:T(8,128)(2,1)} %turned.1.u_ref, f32[18,9,128,128]{3,2,1,0:T(8,128)} %get-tuple-element.36.refs_0_, f32[4,128,384]{2,1,0:T(8,128)} %get-tuple-element.38.refs_1_.stay_ref), custom_call_target="tpu_custom_call", output_to_operand_aliasing={{0}: (2, {})} | custom-call | flops 2717908992 | bytes 7077888 | tf_op jit(solution)/shard_map/products/pallas_call | solution.py:87
  61.8 4.2 %eliminate.5 = (f32[4,128,384]{2,1,0:T(8,128)}, f32[4,128,384]{2,1,0:T(8,128)}) custom-call(s32[34,6]{1,0:T(8,128)} %copy.40.masks, f32[6,128,384]{2,1,0:T(8,128)} %get-tuple-element.39.part_ref, bf16[6,6,64,128]{3,2,1,0:T(8,128)(2,1)} %copy-done, bf16[6,6,64,128]{3,2,1,0:T(8,128)(2,1)} %copy-done.1), custom_call_target="tpu_custom_call" | custom-call | flops 294912000 | bytes 5898240 | tf_op jit(solution)/shard_map/eliminate/pallas_call | solution.py:171
  66.0 1.9 collective-permute-start.5
  68.4 18.0 %collective-permute-done.5.came_ref = f32[4,128,384]{2,1,0:T(8,128)S(1)} collective-permute-done((f32[4,128,384]{2,1,0:T(8,128)}, f32[4,128,384]{2,1,0:T(8,128)S(1)}, u32[]{:S(2)}, u32[]{:S(2)}) %collective-permute-start.5) | collective-permute-done | bytes 786464 | tf_op jit(solution)/shard_map/ppermute | solution.py:454
  87.3 2.4 %halving.6 = (f32[2,128,384]{2,1,0:T(8,128)}, f32[2,128,384]{2,1,0:T(8,128)}) custom-call(s32[34,6]{1,0:T(8,128)} %copy.40.masks, f32[4,128,384]{2,1,0:T(8,128)} %get-tuple-element.40.stay_ref, f32[4,128,384]{2,1,0:T(8,128)} %copy-done.4), custom_call_target="tpu_custom_call" | custom-call | flops 100000000 | bytes 1572864 | tf_op jit(solution)/shard_map/halving/pallas_call | solution.py:191
  91.0 2.2 halving.8
  94.1 2.4 %halving.10 = (f32[2,128,384]{2,1,0:T(8,128)}, f32[2,128,384]{2,1,0:T(8,128)}) custom-call(s32[34,6]{1,0:T(8,128)} %copy.40.masks, f32[4,128,384]{2,1,0:T(8,128)} %get-tuple-element.38.refs_1_.stay_ref, f32[4,128,384]{2,1,0:T(8,128)} %copy-done.3), custom_call_target="tpu_custom_call" | custom-call | flops 100000000 | bytes 1572864 | tf_op jit(solution)/shard_map/halving/pallas_call | solution.py:191
  97.9 1.7 collective-permute-done.6.came_ref
  100.4 1.9 halving.7
  102.3 3.6 %collective-permute-start.7 = (f32[1,128,384]{2,1,0:T(8,128)}, f32[1,128,384]{2,1,0:T(8,128)S(1)}, u32[]{:S(2)}, u32[]{:S(2)}) collective-permute-start(f32[1,128,384]{2,1,0:T(8,128)} %get-tuple-element.45), channel_id=1, source_target_pairs={{0,32},{16,48},{32,0},{48,16},{96,64},{112,80},{1,33},{17,49},{33,... | collective-permute-start | bytes 589832 | tf_op jit(solution)/shard_map/ppermute | solution.py:454
  106.7 1.9 halving.9
  110.7 1.9 halving.11
  112.6 2.9 %collective-permute-start.18 = (f32[1,128,384]{2,1,0:T(8,128)}, f32[1,128,384]{2,1,0:T(8,128)S(1)}, u32[]{:S(2)}, u32[]{:S(2)}) collective-permute-start(f32[1,128,384]{2,1,0:T(8,128)} %get-tuple-element.55), channel_id=1, source_target_pairs={{0,16},{16,0},{32,48},{48,32},{64,80},{80,64},{1,17},{17,1},{33,49... | collective-permute-start | bytes 589832 | tf_op jit(solution)/shard_map/ppermute | solution.py:454
  116.2 1.7 row.2.refs_3_
  118.0 3.2 %collective-permute-start.8 = (f32[128,384]{1,0:T(8,128)}, f32[128,384]{1,0:T(8,128)S(1)}, u32[]{:S(2)}, u32[]{:S(2)}) collective-permute-start(f32[128,384]{1,0:T(8,128)} %row.2.refs_3_), channel_id=1, source_target_pairs={{0,0},{1,16},{2,32},{3,48},{4,68},{5,84},{6,100},{7,116},{8,8},{9,... | collective-permute-start | bytes 589832 | tf_op jit(solution)/shard_map/ppermute | solution.py:473
  122.6 2.0 row.3.refs_0_
  124.6 5.1 %collective-permute-start.19 = (f32[128,768]{1,0:T(8,128)}, f32[128,768]{1,0:T(8,128)S(1)}, u32[]{:S(2)}, u32[]{:S(2)}) collective-permute-start(f32[128,768]{1,0:T(8,128)} %row.3.refs_0_), channel_id=1, source_target_pairs={{0,0},{1,16},{2,32},{3,48},{4,68},{5,84},{6,100},{7,116},{8,8},{9,... | collective-permute-start | bytes 1179656 | tf_op jit(solution)/shard_map/ppermute | solution.py:473
  133.2 2.6 %collective-permute-done.19 = f32[128,768]{1,0:T(8,128)S(1)} collective-permute-done((f32[128,768]{1,0:T(8,128)}, f32[128,768]{1,0:T(8,128)S(1)}, u32[]{:S(2)}, u32[]{:S(2)}) %collective-permute-start.19) | collective-permute-done | bytes 393248 | tf_op jit(solution)/shard_map/ppermute | solution.py:473
  140.9 5.6 %collective-permute-done.22 = f32[128,768]{1,0:T(8,128)S(1)} collective-permute-done((f32[128,768]{1,0:T(8,128)S(1)}, f32[128,768]{1,0:T(8,128)S(1)}, u32[]{:S(2)}, u32[]{:S(2)}) %collective-permute-start.22) | collective-permute-done | bytes 393248 | tf_op jit(solution)/shard_map/ppermute | solution.py:475
  147.4 3.5 %column.2 = (f32[64,768]{1,0:T(8,128)}, f32[64,768]{1,0:T(8,128)}) custom-call(s32[34,6]{1,0:T(8,128)} %copy.40.masks, f32[128,768]{1,0:T(8,128)} %select_select_fusion.even_ref.refs_1_, f32[128,768]{1,0:T(8,128)} %broadcast_select_fusion.odd_ref.refs_2_, bf16[18,6,128,128]{3,2,1,0:T(8,128)(2,1)} %bitcast.15), custom_call_target="tpu_custom_call" | custom-call | flops 603979776 | bytes 4000000 | tf_op jit(solution)/shard_map/column/pallas_call | solution.py:252
  150.8 2.8 %column.3 = (f32[64,768]{1,0:T(8,128)}, f32[64,768]{1,0:T(8,128)}) custom-call(s32[34,6]{1,0:T(8,128)} %copy.40.masks, f32[128,384]{1,0:T(8,128)} %select_select_fusion.1.even_ref.refs_4_, f32[128,384]{1,0:T(8,128)} %broadcast_select_fusion.2.odd_ref.refs_5_, bf16[18,6,128,128]{3,2,1,0:T(8,128)(2,1)} %bitcast.16, f32[64,768]{1,0:T(8,128)} %get-tuple-element.56.refs_0_, ...), custom_call_target="tpu_custom_call" | custom-call | flops 301989888 | bytes 4000000 | tf_op jit(solution)/shard_map/column/pallas_call | solution.py:252
  153.6 10.0 %collective-permute-start.24 = (f32[64,768]{1,0:T(8,128)}, f32[64,768]{1,0:T(8,128)S(1)}, u32[]{:S(2)}, u32[]{:S(2)}) collective-permute-start(f32[64,768]{1,0:T(8,128)} %get-tuple-element.58), channel_id=1, source_target_pairs={{0,16},{1,17},{2,18},{3,19},{4,20},{5,21},{16,0},{17,1},{18,2},{19... | collective-permute-start | bytes 589832 | tf_op jit(solution)/shard_map/ppermute | solution.py:491
  163.7 1.9 collective-permute-start.27
  165.6 2.8 %collective-permute-done.24 = f32[64,768]{1,0:T(8,128)S(1)} collective-permute-done((f32[64,768]{1,0:T(8,128)}, f32[64,768]{1,0:T(8,128)S(1)}, u32[]{:S(2)}, u32[]{:S(2)}) %collective-permute-start.24) | collective-permute-done | bytes 196640 | tf_op jit(solution)/shard_map/ppermute | solution.py:491
  169.4 1.9 collective-permute-start.25
  173.1 4.7 %collective-permute-start.28 = (f32[64,768]{1,0:T(8,128)S(1)}, f32[64,768]{1,0:T(8,128)S(1)}, u32[]{:S(2)}, u32[]{:S(2)}) collective-permute-start(f32[64,768]{1,0:T(8,128)S(1)} %add.85), channel_id=1, source_target_pairs={{0,96},{1,97},{2,98},{3,99},{4,100},{5,101},{16,112},{17,113},{18,... | collective-permute-start | bytes 589832 | tf_op jit(solution)/shard_map/ppermute | solution.py:491
  177.9 2.8 %collective-permute-start.26 = (f32[64,768]{1,0:T(8,128)S(1)}, f32[64,768]{1,0:T(8,128)S(1)}, u32[]{:S(2)}, u32[]{:S(2)}) collective-permute-start(f32[64,768]{1,0:T(8,128)S(1)} %add.83), channel_id=1, source_target_pairs={{0,96},{1,97},{2,98},{3,99},{4,100},{5,101},{16,112},{17,113},{18,... | collective-permute-start | bytes 589832 | tf_op jit(solution)/shard_map/ppermute | solution.py:491
  181.3 4.6 %collective-permute-start.29 = (f32[64,768]{1,0:T(8,128)S(1)}, f32[64,768]{1,0:T(8,128)S(1)}, u32[]{:S(2)}, u32[]{:S(2)}) collective-permute-start(f32[64,768]{1,0:T(8,128)S(1)} %add.86), channel_id=1, source_target_pairs={{0,16},{1,17},{2,18},{3,19},{4,20},{5,21},{16,0},{17,1},{18,2},{19... | collective-permute-start | bytes 589832 | tf_op jit(solution)/shard_map/ppermute | solution.py:491
  186.0 3.0 %collective-permute-done.29 = f32[64,768]{1,0:T(8,128)S(1)} collective-permute-done((f32[64,768]{1,0:T(8,128)S(1)}, f32[64,768]{1,0:T(8,128)S(1)}, u32[]{:S(2)}, u32[]{:S(2)}) %collective-permute-start.29) | collective-permute-done | bytes 196640 | tf_op jit(solution)/shard_map/ppermute | solution.py:491
  189.1 11.5 %collective-permute-start.30 = (f32[128,768]{1,0:T(8,128)S(1)}, f32[128,768]{1,0:T(8,128)S(1)}, u32[]{:S(2)}, u32[]{:S(2)}) collective-permute-start(f32[128,768]{1,0:T(8,128)S(1)} %pad_maximum_fusion.1.refs_0_), channel_id=1, source_target_pairs={{0,18},{16,2},{32,50},{48,34},{64,82},{80,66},{96,114},{112,98},{1... | collective-permute-start | bytes 1179656 | tf_op jit(solution)/shard_map/ppermute | solution.py:503
  200.6 1.9 collective-permute-start.31
  202.6 3.3 %collective-permute-start.32 = (f32[128,768]{1,0:T(8,128)S(1)}, f32[128,768]{1,0:T(8,128)S(1)}, u32[]{:S(2)}, u32[]{:S(2)}) collective-permute-start(f32[128,768]{1,0:T(8,128)S(1)} %pad_maximum_fusion.1.refs_0_), channel_id=1, source_target_pairs={{0,1},{1,0},{2,3},{3,2},{4,5},{5,4},{16,17},{17,16},{18,19},{19,18... | collective-permute-start | bytes 1179656 | tf_op jit(solution)/shard_map/ppermute | solution.py:505
  205.9 2.4 %collective-permute-done.30.refs_1_ = f32[128,768]{1,0:T(8,128)S(1)} collective-permute-done((f32[128,768]{1,0:T(8,128)S(1)}, f32[128,768]{1,0:T(8,128)S(1)}, u32[]{:S(2)}, u32[]{:S(2)}) %collective-permute-start.30) | collective-permute-done | bytes 393248 | tf_op jit(solution)/shard_map/ppermute | solution.py:503
  208.3 4.0 %collective-permute-start.33 = (f32[128,768]{1,0:T(8,128)S(1)}, f32[128,768]{1,0:T(8,128)S(1)}, u32[]{:S(2)}, u32[]{:S(2)}) collective-permute-start(f32[128,768]{1,0:T(8,128)S(1)} %collective-permute-done.30.refs_1_), channel_id=1, source_target_pairs={{0,1},{1,0},{2,3},{3,2},{4,5},{5,4},{16,17},{17,16},{18,19},{19,18... | collective-permute-start | bytes 1179656 | tf_op jit(solution)/shard_map/ppermute | solution.py:505
  212.3 5.3 %collective-permute-done.31.refs_2_ = f32[128,768]{1,0:T(8,128)S(1)} collective-permute-done((f32[128,768]{1,0:T(8,128)S(1)}, f32[128,768]{1,0:T(8,128)S(1)}, u32[]{:S(2)}, u32[]{:S(2)}) %collective-permute-start.31) | collective-permute-done | bytes 393248 | tf_op jit(solution)/shard_map/ppermute | solution.py:503
  217.6 3.9 %collective-permute-start.34 = (f32[128,768]{1,0:T(8,128)S(1)}, f32[128,768]{1,0:T(8,128)S(1)}, u32[]{:S(2)}, u32[]{:S(2)}) collective-permute-start(f32[128,768]{1,0:T(8,128)S(1)} %collective-permute-done.31.refs_2_), channel_id=1, source_target_pairs={{0,1},{1,0},{2,3},{3,2},{4,5},{5,4},{16,17},{17,16},{18,19},{19,18... | collective-permute-start | bytes 1179656 | tf_op jit(solution)/shard_map/ppermute | solution.py:505
  221.5 3.1 %patch.1.refs_9_ = f32[18,9,128,128]{3,2,1,0:T(8,128)} custom-call(s32[34,6]{1,0:T(8,128)} %copy.40.masks, f32[128,768]{1,0:T(8,128)} %row.3.refs_0_, f32[128,768]{1,0:T(8,128)} %select_select_fusion.even_ref.refs_1_, f32[128,768]{1,0:T(8,128)} %broadcast_select_fusion.odd_ref.refs_2_, f32[128,384]{1,0:T(8,128)} %row.2.refs_3_, ...), custom_call_target="tpu_custom_call", output_to_operand_aliasing={{}: (7, {})} | custom-call | flops 100000000 | bytes 4000000 | tf_op jit(solution)/shard_map/patch/pallas_call | solution.py:380
  226.2 5.8 %corner.1 = f32[18,9,128,128]{3,2,1,0:T(8,128)} custom-call(s32[34,6]{1,0:T(8,128)} %copy.40.masks, f32[128,768]{1,0:T(8,128)} %copy-done.2, f32[128,768]{1,0:T(8,128)} %copy-done.9, f32[128,768]{1,0:T(8,128)} %copy-done.10, f32[128,768]{1,0:T(8,128)} %copy-done.11, f32[128,768]{1,0:T(8,128)} %copy-done.12, ...), custom_call_target="tpu_custom_call", output_to_operand_aliasing={{}: (10, {})} | custom-call | flops 1000000000 | bytes 1000000 | tf_op jit(solution)/shard_map/corner/pallas_call | solution.py:310
  (111 shorter events, 32.8 us)
Async XLA Ops:
  0.9 3.5 %collective-permute-start = (bf16[1,6,64,128]{3,2,1,0:T(8,128)(2,1)S(1)}, bf16[1,6,64,128]{3,2,1,0:T(8,128)(2,1)S(1)}, u32[]{:S(2)}, u32[]{:S(2)}) collective-permute-start(bf16[1,6,64,128]{3,2,1,0:T(8,128)(2,1)S(1)} %dynamic-slice_bitcast_fusion), channel_id=1, source_target_pairs={{0,16},{16,0},{32,48},{48,32},{64,80},{80,64},{96,112},{112,96},{1... | collective-permute-start | bytes 294920 | tf_op jit(solution)/shard_map/ppermute | solution.py:429
  4.4 7.3 %collective-permute-start.1 = (bf16[2,6,64,128]{3,2,1,0:T(8,128)(2,1)S(1)}, bf16[2,6,64,128]{3,2,1,0:T(8,128)(2,1)S(1)}, u32[]{:S(2)}, u32[]{:S(2)}) collective-permute-start(bf16[2,6,64,128]{3,2,1,0:T(8,128)(2,1)S(1)} %maximum_select_fusion), channel_id=1, source_target_pairs={{0,32},{16,48},{32,64},{48,80},{64,96},{80,112},{96,0},{112,16},{1... | collective-permute-start | bytes 589832 | tf_op jit(solution)/shard_map/ppermute | solution.py:430
  6.1 10.4 %collective-permute-start.2 = (bf16[2,6,64,128]{3,2,1,0:T(8,128)(2,1)S(1)}, bf16[2,6,64,128]{3,2,1,0:T(8,128)(2,1)S(1)}, u32[]{:S(2)}, u32[]{:S(2)}) collective-permute-start(bf16[2,6,64,128]{3,2,1,0:T(8,128)(2,1)S(1)} %maximum_select_fusion), channel_id=1, source_target_pairs={{0,64},{16,80},{32,96},{48,112},{64,0},{80,16},{96,32},{112,48},{1... | collective-permute-start | bytes 589832 | tf_op jit(solution)/shard_map/ppermute | solution.py:430
  9.4 7.1 %collective-permute-start.3 = (bf16[2,6,64,128]{3,2,1,0:T(8,128)(2,1)S(1)}, bf16[2,6,64,128]{3,2,1,0:T(8,128)(2,1)S(1)}, u32[]{:S(2)}, u32[]{:S(2)}) collective-permute-start(bf16[2,6,64,128]{3,2,1,0:T(8,128)(2,1)S(1)} %maximum_select_fusion), channel_id=1, source_target_pairs={{0,96},{16,112},{32,0},{48,16},{64,32},{80,48},{96,64},{112,80},{1... | collective-permute-start | bytes 589832 | tf_op jit(solution)/shard_map/ppermute | solution.py:430
  16.7 19.1 %copy-start = (bf16[6,6,64,128]{3,2,1,0:T(8,128)(2,1)}, bf16[6,6,64,128]{3,2,1,0:T(8,128)(2,1)S(1)}, u32[]{:S(2)}) copy-start(bf16[6,6,64,128]{3,2,1,0:T(8,128)(2,1)S(1)} %pad_maximum_fusion.u_ref.refs_6_) | copy-start | bytes 1769476
  16.7 19.1 %collective-permute-start.4 = (bf16[6,6,64,128]{3,2,1,0:T(8,128)(2,1)S(1)}, bf16[6,6,64,128]{3,2,1,0:T(8,128)(2,1)S(1)}, u32[]{:S(2)}, u32[]{:S(2)}) collective-permute-start(bf16[6,6,64,128]{3,2,1,0:T(8,128)(2,1)S(1)} %pad_maximum_fusion.u_ref.refs_6_), channel_id=1, source_target_pairs={{0,1},{1,0},{2,3},{3,2},{4,5},{5,4},{6,7},{7,6},{8,9},{9,8},{10,11... | collective-permute-start | bytes 1769480 | tf_op jit(solution)/shard_map/ppermute | solution.py:436
  35.7 0.9 copy-start.1
  53.4 14.5 %copy-start.17 = (f32[4,128,384]{2,1,0:T(8,128)S(1)}, f32[4,128,384]{2,1,0:T(8,128)}, u32[]{:S(2)}) copy-start(f32[4,128,384]{2,1,0:T(8,128)} %get-tuple-element.51) | copy-start | bytes 2359300
  53.4 14.5 %copy-start.18 = (f32[3,128,384]{2,1,0:T(8,128)S(1)}, f32[3,128,384]{2,1,0:T(8,128)}, u32[]{:S(2)}) copy-start(f32[3,128,384]{2,1,0:T(8,128)} %get-tuple-element.46) | copy-start | bytes 1769476
  66.0 20.5 %collective-permute-start.5 = (f32[4,128,384]{2,1,0:T(8,128)}, f32[4,128,384]{2,1,0:T(8,128)S(1)}, u32[]{:S(2)}, u32[]{:S(2)}) collective-permute-start(f32[4,128,384]{2,1,0:T(8,128)} %get-tuple-element.41), channel_id=1, source_target_pairs={{0,96},{16,112},{32,64},{48,80},{64,32},{80,48},{96,0},{112,16},{1... | collective-permute-start | bytes 2359304 | tf_op jit(solution)/shard_map/ppermute | solution.py:454
  67.9 25.3 %collective-permute-start.16 = (f32[4,128,384]{2,1,0:T(8,128)S(1)}, f32[4,128,384]{2,1,0:T(8,128)S(1)}, u32[]{:S(2)}, u32[]{:S(2)}) collective-permute-start(f32[4,128,384]{2,1,0:T(8,128)S(1)} %copy-done.17), channel_id=1, source_target_pairs={{0,32},{16,48},{32,0},{48,16},{64,96},{80,112},{96,64},{112,80},{1... | collective-permute-start | bytes 2359304 | tf_op jit(solution)/shard_map/ppermute | solution.py:454
  67.9 22.3 %collective-permute-start.13 = (f32[3,128,384]{2,1,0:T(8,128)S(1)}, f32[3,128,384]{2,1,0:T(8,128)S(1)}, u32[]{:S(2)}, u32[]{:S(2)}) collective-permute-start(f32[3,128,384]{2,1,0:T(8,128)S(1)} %copy-done.18), channel_id=1, source_target_pairs={{0,16},{16,0},{32,48},{48,32},{64,80},{80,64},{96,112},{112,96},{1... | collective-permute-start | bytes 1769480 | tf_op jit(solution)/shard_map/ppermute | solution.py:454
  86.4 0.9 copy-start.4
  89.7 10.0 %collective-permute-start.6 = (f32[2,128,384]{2,1,0:T(8,128)}, f32[2,128,384]{2,1,0:T(8,128)S(1)}, u32[]{:S(2)}, u32[]{:S(2)}) collective-permute-start(f32[2,128,384]{2,1,0:T(8,128)} %get-tuple-element.43), channel_id=1, source_target_pairs={{0,16},{16,0},{32,48},{48,32},{64,80},{80,64},{96,112},{112,96},{1... | collective-permute-start | bytes 1179656 | tf_op jit(solution)/shard_map/ppermute | solution.py:454
  90.1 0.8 copy-start.5
  93.2 12.7 %collective-permute-start.14 = (f32[2,128,384]{2,1,0:T(8,128)}, f32[2,128,384]{2,1,0:T(8,128)S(1)}, u32[]{:S(2)}, u32[]{:S(2)}) collective-permute-start(f32[2,128,384]{2,1,0:T(8,128)} %get-tuple-element.48), channel_id=1, source_target_pairs={{0,32},{16,48},{32,0},{48,16},{64,96},{80,112},{96,64},{112,80},{1... | collective-permute-start | bytes 1179656 | tf_op jit(solution)/shard_map/ppermute | solution.py:454
  93.2 0.9 copy-start.3
  96.5 13.5 %collective-permute-start.17 = (f32[2,128,384]{2,1,0:T(8,128)}, f32[2,128,384]{2,1,0:T(8,128)S(1)}, u32[]{:S(2)}, u32[]{:S(2)}) collective-permute-start(f32[2,128,384]{2,1,0:T(8,128)} %get-tuple-element.53), channel_id=1, source_target_pairs={{32,64},{48,80},{64,32},{80,48},{96,0},{112,16},{33,65},{49,81},{6... | collective-permute-start | bytes 1179656 | tf_op jit(solution)/shard_map/ppermute | solution.py:454
  102.3 13.2 %collective-permute-start.7 = (f32[1,128,384]{2,1,0:T(8,128)}, f32[1,128,384]{2,1,0:T(8,128)S(1)}, u32[]{:S(2)}, u32[]{:S(2)}) collective-permute-start(f32[1,128,384]{2,1,0:T(8,128)} %get-tuple-element.45), channel_id=1, source_target_pairs={{0,32},{16,48},{32,0},{48,16},{96,64},{112,80},{1,33},{17,49},{33,... | collective-permute-start | bytes 589832 | tf_op jit(solution)/shard_map/ppermute | solution.py:454
  105.9 0.8 copy-start.7
  108.6 13.2 %collective-permute-start.15 = (f32[1,128,384]{2,1,0:T(8,128)}, f32[1,128,384]{2,1,0:T(8,128)S(1)}, u32[]{:S(2)}, u32[]{:S(2)}) collective-permute-start(f32[1,128,384]{2,1,0:T(8,128)} %get-tuple-element.50), channel_id=1, source_target_pairs={{32,64},{48,80},{64,32},{80,48},{96,0},{112,16},{33,65},{49,81},{6... | collective-permute-start | bytes 589832 | tf_op jit(solution)/shard_map/ppermute | solution.py:454
  109.9 0.8 copy-start.6
  112.6 9.2 %collective-permute-start.18 = (f32[1,128,384]{2,1,0:T(8,128)}, f32[1,128,384]{2,1,0:T(8,128)S(1)}, u32[]{:S(2)}, u32[]{:S(2)}) collective-permute-start(f32[1,128,384]{2,1,0:T(8,128)} %get-tuple-element.55), channel_id=1, source_target_pairs={{0,16},{16,0},{32,48},{48,32},{64,80},{80,64},{1,17},{17,1},{33,49... | collective-permute-start | bytes 589832 | tf_op jit(solution)/shard_map/ppermute | solution.py:454
  118.0 12.5 %collective-permute-start.8 = (f32[128,384]{1,0:T(8,128)}, f32[128,384]{1,0:T(8,128)S(1)}, u32[]{:S(2)}, u32[]{:S(2)}) collective-permute-start(f32[128,384]{1,0:T(8,128)} %row.2.refs_3_), channel_id=1, source_target_pairs={{0,0},{1,16},{2,32},{3,48},{4,68},{5,84},{6,100},{7,116},{8,8},{9,... | collective-permute-start | bytes 589832 | tf_op jit(solution)/shard_map/ppermute | solution.py:473
  121.1 9.3 %collective-permute-start.9 = (f32[128,384]{1,0:T(8,128)}, f32[128,384]{1,0:T(8,128)S(1)}, u32[]{:S(2)}, u32[]{:S(2)}) collective-permute-start(f32[128,384]{1,0:T(8,128)} %row.2.refs_3_), channel_id=1, source_target_pairs={{64,0},{65,16},{66,32},{67,48},{68,68},{69,84},{70,100},{71,116},{... | collective-permute-start | bytes 589832 | tf_op jit(solution)/shard_map/ppermute | solution.py:474
  124.6 11.2 %collective-permute-start.19 = (f32[128,768]{1,0:T(8,128)}, f32[128,768]{1,0:T(8,128)S(1)}, u32[]{:S(2)}, u32[]{:S(2)}) collective-permute-start(f32[128,768]{1,0:T(8,128)} %row.3.refs_0_), channel_id=1, source_target_pairs={{0,0},{1,16},{2,32},{3,48},{4,68},{5,84},{6,100},{7,116},{8,8},{9,... | collective-permute-start | bytes 1179656 | tf_op jit(solution)/shard_map/ppermute | solution.py:473
  129.7 6.1 %collective-permute-start.20 = (f32[128,768]{1,0:T(8,128)}, f32[128,768]{1,0:T(8,128)S(1)}, u32[]{:S(2)}, u32[]{:S(2)}) collective-permute-start(f32[128,768]{1,0:T(8,128)} %row.3.refs_0_), channel_id=1, source_target_pairs={{64,0},{65,16},{66,32},{67,48},{68,68},{69,84},{70,100},{71,116},{... | collective-permute-start | bytes 1179656 | tf_op jit(solution)/shard_map/ppermute | solution.py:474
  130.5 7.4 %collective-permute-start.10 = (f32[128,384]{1,0:T(8,128)S(1)}, f32[128,384]{1,0:T(8,128)S(1)}, u32[]{:S(2)}, u32[]{:S(2)}) collective-permute-start(f32[128,384]{1,0:T(8,128)S(1)} %broadcast_select_fusion.3), channel_id=1, source_target_pairs={{0,4},{16,20},{32,36},{48,52},{1,5},{17,21},{33,37},{49,53},{68,64... | collective-permute-start | bytes 589832 | tf_op jit(solution)/shard_map/ppermute | solution.py:479
  131.2 8.2 %collective-permute-start.11 = (f32[128,384]{1,0:T(8,128)S(1)}, f32[128,384]{1,0:T(8,128)S(1)}, u32[]{:S(2)}, u32[]{:S(2)}) collective-permute-start(f32[128,384]{1,0:T(8,128)S(1)} %collective-permute-done.8), channel_id=1, source_target_pairs={{8,0},{24,16},{40,32},{56,48},{76,64},{92,80},{108,96},{124,112},{... | collective-permute-start | bytes 589832 | tf_op jit(solution)/shard_map/ppermute | solution.py:475
  132.5 6.9 %collective-permute-start.12 = (f32[128,384]{1,0:T(8,128)S(1)}, f32[128,384]{1,0:T(8,128)S(1)}, u32[]{:S(2)}, u32[]{:S(2)}) collective-permute-start(f32[128,384]{1,0:T(8,128)S(1)} %collective-permute-done.9), channel_id=1, source_target_pairs={{8,4},{24,20},{40,36},{56,52},{76,68},{92,84},{108,100},{124,116},... | collective-permute-start | bytes 589832 | tf_op jit(solution)/shard_map/ppermute | solution.py:476
  135.9 4.2 %collective-permute-start.21 = (f32[128,768]{1,0:T(8,128)S(1)}, f32[128,768]{1,0:T(8,128)S(1)}, u32[]{:S(2)}, u32[]{:S(2)}) collective-permute-start(f32[128,768]{1,0:T(8,128)S(1)} %broadcast_select_fusion.1), channel_id=1, source_target_pairs={{0,4},{16,20},{32,36},{48,52},{1,5},{17,21},{33,37},{49,53},{68,64... | collective-permute-start | bytes 1179656 | tf_op jit(solution)/shard_map/ppermute | solution.py:479
  136.6 10.0 %collective-permute-start.22 = (f32[128,768]{1,0:T(8,128)S(1)}, f32[128,768]{1,0:T(8,128)S(1)}, u32[]{:S(2)}, u32[]{:S(2)}) collective-permute-start(f32[128,768]{1,0:T(8,128)S(1)} %collective-permute-done.19), channel_id=1, source_target_pairs={{8,0},{24,16},{40,32},{56,48},{76,64},{92,80},{108,96},{124,112},{... | collective-permute-start | bytes 1179656 | tf_op jit(solution)/shard_map/ppermute | solution.py:475
  137.9 8.7 %collective-permute-start.23 = (f32[128,768]{1,0:T(8,128)S(1)}, f32[128,768]{1,0:T(8,128)S(1)}, u32[]{:S(2)}, u32[]{:S(2)}) collective-permute-start(f32[128,768]{1,0:T(8,128)S(1)} %collective-permute-done.20), channel_id=1, source_target_pairs={{8,4},{24,20},{40,36},{56,52},{76,68},{92,84},{108,100},{124,116},... | collective-permute-start | bytes 1179656 | tf_op jit(solution)/shard_map/ppermute | solution.py:476
  153.6 14.8 %collective-permute-start.24 = (f32[64,768]{1,0:T(8,128)}, f32[64,768]{1,0:T(8,128)S(1)}, u32[]{:S(2)}, u32[]{:S(2)}) collective-permute-start(f32[64,768]{1,0:T(8,128)} %get-tuple-element.58), channel_id=1, source_target_pairs={{0,16},{1,17},{2,18},{3,19},{4,20},{5,21},{16,0},{17,1},{18,2},{19... | collective-permute-start | bytes 589832 | tf_op jit(solution)/shard_map/ppermute | solution.py:491
  163.7 8.5 %collective-permute-start.27 = (f32[64,768]{1,0:T(8,128)}, f32[64,768]{1,0:T(8,128)S(1)}, u32[]{:S(2)}, u32[]{:S(2)}) collective-permute-start(f32[64,768]{1,0:T(8,128)} %get-tuple-element.59), channel_id=1, source_target_pairs={{0,32},{1,33},{2,34},{3,35},{4,36},{5,37},{16,48},{17,49},{18,50},... | collective-permute-start | bytes 589832 | tf_op jit(solution)/shard_map/ppermute | solution.py:491
  169.4 8.5 %collective-permute-start.25 = (f32[64,768]{1,0:T(8,128)S(1)}, f32[64,768]{1,0:T(8,128)S(1)}, u32[]{:S(2)}, u32[]{:S(2)}) collective-permute-start(f32[64,768]{1,0:T(8,128)S(1)} %add.82), channel_id=1, source_target_pairs={{0,32},{1,33},{2,34},{3,35},{4,36},{5,37},{16,48},{17,49},{18,50},... | collective-permute-start | bytes 589832 | tf_op jit(solution)/shard_map/ppermute | solution.py:491
  173.1 8.2 %collective-permute-start.28 = (f32[64,768]{1,0:T(8,128)S(1)}, f32[64,768]{1,0:T(8,128)S(1)}, u32[]{:S(2)}, u32[]{:S(2)}) collective-permute-start(f32[64,768]{1,0:T(8,128)S(1)} %add.85), channel_id=1, source_target_pairs={{0,96},{1,97},{2,98},{3,99},{4,100},{5,101},{16,112},{17,113},{18,... | collective-permute-start | bytes 589832 | tf_op jit(solution)/shard_map/ppermute | solution.py:491
  177.9 8.1 %collective-permute-start.26 = (f32[64,768]{1,0:T(8,128)S(1)}, f32[64,768]{1,0:T(8,128)S(1)}, u32[]{:S(2)}, u32[]{:S(2)}) collective-permute-start(f32[64,768]{1,0:T(8,128)S(1)} %add.83), channel_id=1, source_target_pairs={{0,96},{1,97},{2,98},{3,99},{4,100},{5,101},{16,112},{17,113},{18,... | collective-permute-start | bytes 589832 | tf_op jit(solution)/shard_map/ppermute | solution.py:491
  181.3 7.7 %collective-permute-start.29 = (f32[64,768]{1,0:T(8,128)S(1)}, f32[64,768]{1,0:T(8,128)S(1)}, u32[]{:S(2)}, u32[]{:S(2)}) collective-permute-start(f32[64,768]{1,0:T(8,128)S(1)} %add.86), channel_id=1, source_target_pairs={{0,16},{1,17},{2,18},{3,19},{4,20},{5,21},{16,0},{17,1},{18,2},{19... | collective-permute-start | bytes 589832 | tf_op jit(solution)/shard_map/ppermute | solution.py:491
  189.1 35.4 %copy-start.2 = (f32[128,768]{1,0:T(8,128)}, f32[128,768]{1,0:T(8,128)S(1)}, u32[]{:S(2)}) copy-start(f32[128,768]{1,0:T(8,128)S(1)} %pad_maximum_fusion.1.refs_0_) | copy-start | bytes 1179652
  189.1 19.2 %collective-permute-start.30 = (f32[128,768]{1,0:T(8,128)S(1)}, f32[128,768]{1,0:T(8,128)S(1)}, u32[]{:S(2)}, u32[]{:S(2)}) collective-permute-start(f32[128,768]{1,0:T(8,128)S(1)} %pad_maximum_fusion.1.refs_0_), channel_id=1, source_target_pairs={{0,18},{16,2},{32,50},{48,34},{64,82},{80,66},{96,114},{112,98},{1... | collective-permute-start | bytes 1179656 | tf_op jit(solution)/shard_map/ppermute | solution.py:503
  200.6 17.0 %collective-permute-start.31 = (f32[128,768]{1,0:T(8,128)S(1)}, f32[128,768]{1,0:T(8,128)S(1)}, u32[]{:S(2)}, u32[]{:S(2)}) collective-permute-start(f32[128,768]{1,0:T(8,128)S(1)} %pad_maximum_fusion.1.refs_0_), channel_id=1, source_target_pairs={{0,4},{16,20},{32,36},{48,52},{64,68},{80,84},{96,100},{112,116},{... | collective-permute-start | bytes 1179656 | tf_op jit(solution)/shard_map/ppermute | solution.py:503
  202.6 22.0 %collective-permute-start.32 = (f32[128,768]{1,0:T(8,128)S(1)}, f32[128,768]{1,0:T(8,128)S(1)}, u32[]{:S(2)}, u32[]{:S(2)}) collective-permute-start(f32[128,768]{1,0:T(8,128)S(1)} %pad_maximum_fusion.1.refs_0_), channel_id=1, source_target_pairs={{0,1},{1,0},{2,3},{3,2},{4,5},{5,4},{16,17},{17,16},{18,19},{19,18... | collective-permute-start | bytes 1179656 | tf_op jit(solution)/shard_map/ppermute | solution.py:505
  208.3 16.3 %copy-start.9 = (f32[128,768]{1,0:T(8,128)}, f32[128,768]{1,0:T(8,128)S(1)}, u32[]{:S(2)}) copy-start(f32[128,768]{1,0:T(8,128)S(1)} %collective-permute-done.30.refs_1_) | copy-start | bytes 1179652
  208.3 16.3 %collective-permute-start.33 = (f32[128,768]{1,0:T(8,128)S(1)}, f32[128,768]{1,0:T(8,128)S(1)}, u32[]{:S(2)}, u32[]{:S(2)}) collective-permute-start(f32[128,768]{1,0:T(8,128)S(1)} %collective-permute-done.30.refs_1_), channel_id=1, source_target_pairs={{0,1},{1,0},{2,3},{3,2},{4,5},{5,4},{16,17},{17,16},{18,19},{19,18... | collective-permute-start | bytes 1179656 | tf_op jit(solution)/shard_map/ppermute | solution.py:505
  217.6 7.0 %copy-start.10 = (f32[128,768]{1,0:T(8,128)}, f32[128,768]{1,0:T(8,128)S(1)}, u32[]{:S(2)}) copy-start(f32[128,768]{1,0:T(8,128)S(1)} %collective-permute-done.31.refs_2_) | copy-start | bytes 1179652
  217.6 7.0 %collective-permute-start.34 = (f32[128,768]{1,0:T(8,128)S(1)}, f32[128,768]{1,0:T(8,128)S(1)}, u32[]{:S(2)}, u32[]{:S(2)}) collective-permute-start(f32[128,768]{1,0:T(8,128)S(1)} %collective-permute-done.31.refs_2_), channel_id=1, source_target_pairs={{0,1},{1,0},{2,3},{3,2},{4,5},{5,4},{16,17},{17,16},{18,19},{19,18... | collective-permute-start | bytes 1179656 | tf_op jit(solution)/shard_map/ppermute | solution.py:505
  224.6 0.9 copy-start.12
  (6 other events, 4.3 us)

commit v5 on v3

--- a/solution.py
+++ b/solution.py
@@ -9,7 +9,7 @@
 
 
 F32, BF16 = jnp.float32, jnp.bfloat16
-PARTS = ((0, 8), (8, 10))
+PARTS = ((0, 18),)
 SIZES = (3, 4, 4)
 CORNER, COLS, IDS = 18, 24, 33
 VMEM = pl.BlockSpec(memory_space=pltpu.VMEM)
@@ -62,7 +62,7 @@
         out_ref[...] += term
 
 
-def products(blocks, lower, masks, whole, first, count, rows=2):
+def products(blocks, lower, masks, whole, first, count, rows=3):
     _, cols, width, _ = blocks.shape
     steps = lower.shape[1]
     start = first // rows
@@ -170,23 +170,38 @@
     )(masks, *parts, *corner)
 
 
-def halving_kernel(group, stage, masks, stay_ref, came_ref, send_ref, keep_ref):
-    _, _, z, y = place_of(masks)
-    for ref, pieces in zip((send_ref, keep_ref), later_pieces(group, stage, z, y)):
-        for m, n in enumerate(pieces):
-            ref[m] = stay_ref[n] + came_ref[n]
+def halving_kernel(masks, stay_a, came_a, stay_b, came_b, send_ref, keep_ref):
+    send_ref[...] = stay_a[...] + came_a[...]
+    keep_ref[...] = stay_b[...] + came_b[...]
 
 
 def halving(masks, group, stage, stay, came):
     _, width, wide = stay.shape
-    return pl.pallas_call(
-        functools.partial(halving_kernel, group, stage),
-        in_specs=[SMEM, VMEM, VMEM],
-        out_specs=[VMEM] * 2,
-        out_shape=[jax.ShapeDtypeStruct((4 - stage, width, wide), F32)] * 2,
+    count = 4 - stage
+
+    def piece(side):
+        def index(m, masks):
+            _, _, z, y = place_of(masks)
+            slots = later_pieces(group, stage, z, y)[side]
+            slot = slots[0]
+            for n in range(1, count):
+                slot = jnp.where(m == n, slots[n], slot)
+            return slot, 0, 0
+
+        return pl.BlockSpec((1, width, wide), index)
+
+    return pl.pallas_call(
+        halving_kernel,
+        grid_spec=pltpu.PrefetchScalarGridSpec(
+            num_scalar_prefetch=1,
+            grid=(count,),
+            in_specs=[piece(0), piece(0), piece(1), piece(1)],
+            out_specs=[pl.BlockSpec((1, width, wide), lambda m, _: (m, 0, 0))] * 2,
+        ),
+        out_shape=[jax.ShapeDtypeStruct((count, width, wide), F32)] * 2,
         cost_estimate=pl.CostEstimate(flops=10**8, bytes_accessed=32 * width * wide, transcendentals=0),
         name="halving",
-    )(masks, stay, came)
+    )(masks, stay, came, stay, came)
 
 
 def row_kernel(masks, *refs):
@@ -213,40 +228,41 @@
     )(masks, *given)
 
 
-def column_kernel(masks, *refs):
-    *value_refs, u_ref, upper_ref, lower_ref = refs
-    _, steps, width, _ = u_ref.shape
-    total, a = None, 0
-    for even_ref, odd_ref in zip(value_refs[::2], value_refs[1::2]):
-        for c in range(even_ref.shape[1] // width):
-            part = pl.ds(c * width, width)
-            value = jnp.concatenate([even_ref[:, part], odd_ref[:, part]], axis=1)
-            left = jnp.concatenate(halves(value), axis=0)
-            right = []
-            for r in (a, a + 1):
-                wide = []
-                for k in range(steps):
-                    block = u_ref[r, k]
-                    wide.append(jnp.where(masks[r, k] > 0, block, jnp.zeros_like(block)))
-                right.append(jnp.concatenate(wide, axis=1))
-            term = dot(left, jnp.concatenate(right, axis=0))
-            total = term if total is None else total + term
-            a += 2
+def column_kernel(parity, masks, value_ref, u_ref, *refs):
+    *given, upper_ref, lower_ref = refs
+    count, _, steps, width, _ = u_ref.shape
+    total = None
+    for c in range(0, count, 2):
+        taken = range(c, min(c + 2, count))
+        left = jnp.concatenate(halves(value_ref[:, pl.ds(c * width, len(taken) * width)]), axis=0)
+        right = []
+        for r in taken:
+            wide = []
+            for k in range(steps):
+                block = u_ref[r, 0, k]
+                wide.append(jnp.where(masks[2 * r + parity, k] > 0, block, jnp.zeros_like(block)))
+            right.append(jnp.concatenate(wide, axis=1))
+        term = dot(left, jnp.concatenate(right, axis=0))
+        total = term if total is None else total + term
     total = total[:width] + total[width:]
-    upper_ref[...] = total[: width // 2]
-    lower_ref[...] = total[width // 2 :]
-
-
-def column_products(values, lower, masks):
+    for n, ref in enumerate((upper_ref, lower_ref)):
+        value = total[n * width // 2 : (n + 1) * width // 2]
+        ref[...] = value + given[n][...] if given else value
+
+
+def column_products(masks, parity, value, lower, given):
     row_blocks, steps, width, _ = lower.shape
-    return pl.pallas_call(
-        column_kernel,
-        in_specs=[SMEM] + [VMEM] * (len(values) + 1),
+    count = row_blocks // 2
+    return pl.pallas_call(
+        functools.partial(column_kernel, parity),
+        grid=(1,),
+        in_specs=[SMEM, VMEM, pl.BlockSpec((count, 1, steps, width, width), lambda i: (0, parity, 0, 0, 0))]
+        + [VMEM] * len(given),
         out_specs=[VMEM] * 2,
         out_shape=[jax.ShapeDtypeStruct((width // 2, steps * width), F32)] * 2,
-        cost_estimate=pl.CostEstimate(flops=4 * row_blocks * steps * width**3, bytes_accessed=6 * 10**6, transcendentals=0),
+        cost_estimate=pl.CostEstimate(flops=4 * count * steps * width**3, bytes_accessed=4 * 10**6, transcendentals=0),
         name="column",
-    )(masks, *values, lower)
+    )(masks, value, lower.reshape(count, 2, steps, width, width), *given)
 
 
 def corner_kernel(masks, *refs):
@@ -465,7 +481,8 @@
     mine = jnp.where(x == 0, first, second)
     values = [row, jnp.where(x == z // 2, mine, moved), jnp.where(x == 0, odd0, odd1)]
 
-    upper, under = column_products(values[1:], lower, masks)
+    sums = column_products(masks, 0, values[1], lower, ())
+    upper, under = column_products(masks, 1, values[2], lower, sums)
 
     def here(perm):
         return [(s * n_col + d, t * n_col + d) for s, t in perm for d in range(steps)]

time: 220 us -> 216 us (0.982)
  waiting for transfers between devices: 78.3 us -> 70.3 us
    pallas_call x7 -> x8, Pallas kernels: 17 us -> 25 us  [the longest x6 18.8 us: halving(): pl.pallas_call(halving_kernel, grid_spec=pltpu.PrefetchScalarGridSpec(num...]
    ppermute x2, waiting for transfers between devices: 11.9 us -> 5.88 us  [per_device(): turns = [lax.ppermute(sums, both, around(t)) for t in (2, 4)]]
    pallas_call x2 -> x1, Pallas kernels: 24 us -> 18 us  [products(): pl.pallas_call(functools.partial(product_kernel, first), grid_spec=pltpu....]
    ppermute x9, waiting for transfers between devices: 22.5 us -> 19.4 us  [per_device(): lax.ppermute(send, 'prow', routes[n][stage])]
    ppermute x3, waiting for transfers between devices: 6.23 us -> 9 us  [per_device(): lax.ppermute(pair, 'prow', ring(shift))]
    ppermute x3, waiting for transfers between devices: 8.35 us -> 5.81 us  [per_device(): lax.ppermute(under, both, here(two))]
    ppermute x1, waiting for transfers between devices: 5.03 us -> 2.65 us  [per_device(): lax.ppermute(first, both, [slide(pl_, pl_[2] // 2 + 2, 0) for pl_ in plac...]
  transfers between devices with their start and end apart: 30 -> 30, of which waited for: 15 -> 17; matrix products, arithmetic and copies ran while one was open for 3% -> 3% of each run, Pallas kernels for 18% -> 20%
where the time goes in v5:
time: 216 us; the launch traced here: 212 us
  waiting for transfers between devices  70.3 us (33%)
  starting transfers between devices  64.1 us (30%)
  Pallas kernels  60.9 us (28%)
  local copies, waits for them, and re-layouts  11.6 us (5%)
  other arithmetic  4.68 us (2%)
    ppermute x9, waiting for transfers between devices, per_device(): lax.ppermute(send, 'prow', routes[n][stage])  19.4 us
    pallas_call x6, Pallas kernels, halving(): pl.pallas_call(halving_kernel, grid_spec=pltpu.PrefetchScalarGridSpec(num...  18.8 us
    pallas_call x1, Pallas kernels, products(): pl.pallas_call(functools.partial(product_kernel, first), grid_spec=pltpu....  18 us
    ppermute x1, waiting for transfers between devices, per_device(): lax.ppermute(row, both, [turn(k, *place) for k in range(4, steps) for pla...  16.8 us
    ppermute x9, starting transfers between devices, per_device(): lax.ppermute(send, 'prow', routes[n][stage])  14.5 us
    ppermute x3, starting transfers between devices, per_device(): lax.ppermute(upper, both, here(one))  11.3 us
    ppermute x3, waiting for transfers between devices, per_device(): lax.ppermute(pair, 'prow', ring(shift))  9 us
    unnamed x35, local copies, waits for them, and re-layouts  8.17 us
  transfers between devices with their start and end apart: 30, of which 17 were waited for; matrix products, arithmetic and copies ran while one was open for 3% of the time, Pallas kernels for 20%

profile of v5, /device:TPU:0, one launch (start us, length us, event | category | flops | bytes accessed | tf_op | source)
XLA Modules:
  0.0 212.3 jit_solution(4064169599007995546)
XLA Ops:
  0.9 1.7 collective-permute-start
  5.5 4.2 %collective-permute-start.3 = (bf16[2,6,64,128]{3,2,1,0:T(8,128)(2,1)S(1)}, bf16[2,6,64,128]{3,2,1,0:T(8,128)(2,1)S(1)}, u32[]{:S(2)}, u32[]{:S(2)}) collective-permute-start(bf16[2,6,64,128]{3,2,1,0:T(8,128)(2,1)S(1)} %maximum_select_fusion), channel_id=1, source_target_pairs={{0,96},{16,112},{32,0},{48,16},{64,32},{80,48},{96,64},{112,80},{1... | collective-permute-start | bytes 589832 | tf_op jit(solution)/shard_map/ppermute | solution.py:434
  11.8 5.6 %collective-permute-done.3 = bf16[2,6,64,128]{3,2,1,0:T(8,128)(2,1)S(1)} collective-permute-done((bf16[2,6,64,128]{3,2,1,0:T(8,128)(2,1)S(1)}, bf16[2,6,64,128]{3,2,1,0:T(8,128)(2,1)S(1)}, u32[]{:S(2)}, u32[]{:S(2)}) %collective-permute-start.3) | collective-permute-done | bytes 196640 | tf_op jit(solution)/shard_map/ppermute | solution.py:434
  17.4 1.6 collective-permute-done.2
  19.0 1.8 collective-permute-done.1
  21.1 18.0 %products.1 = (f32[18,9,128,128]{3,2,1,0:T(8,128)}, f32[6,128,1152]{2,1,0:T(8,128)}) custom-call(s32[34,6]{1,0:T(8,128)} %copy.35.masks, f32[18,9,128,128]{3,2,1,0:T(8,128)} %bitcast.15, bf16[18,6,128,128]{3,2,1,0:T(8,128)(2,1)} %bitcast.12), custom_call_target="tpu_custom_call" | custom-call | flops 8153726976 | bytes 21233664 | tf_op jit(solution)/shard_map/products/pallas_call | solution.py:70
  40.0 6.8 %eliminate.1 = (f32[3,128,384]{2,1,0:T(8,128)}, f32[3,128,384]{2,1,0:T(8,128)}, f32[4,128,384]{2,1,0:T(8,128)}, f32[4,128,384]{2,1,0:T(8,128)}, f32[4,128,384]{2,1,0:T(8,128)}, /*index=5*/f32[4,128,384]{2,1,0:T(8,128)}) custom-call(s32[34,6]{1,0:T(8,128)} %copy.35.masks, f32[6,128,1152]{2,1,0:T(8,128)} %get-tuple-element.29.refs_0_, ...), custom_call_target="tpu_custom_call" | custom-call | flops 884736000 | bytes 17694720 | tf_op jit(solution)/shard_map/eliminate/pallas_call | solution.py:162
  49.1 14.3 %collective-permute-done.5.came_a.came_b = f32[3,128,384]{2,1,0:T(8,128)S(1)} collective-permute-done((f32[3,128,384]{2,1,0:T(8,128)}, f32[3,128,384]{2,1,0:T(8,128)S(1)}, u32[]{:S(2)}, u32[]{:S(2)}) %collective-permute-start.5) | collective-permute-done | bytes 589856 | tf_op jit(solution)/shard_map/ppermute | solution.py:459
  64.2 3.2 %halving.6 = (f32[2,128,384]{2,1,0:T(8,128)}, f32[2,128,384]{2,1,0:T(8,128)}) custom-call(s32[34,6]{1,0:T(8,128)} %copy.35.masks, f32[3,128,384]{2,1,0:T(8,128)} %get-tuple-element.30.stay_a.stay_b, f32[3,128,384]{2,1,0:T(8,128)} %copy-done.4, f32[3,128,384]{2,1,0:T(8,128)} %get-tuple-element.30.stay_a.stay_b, f32[3,128,384]{2,1,0:T(8,128)} %copy-done.4), custom_call_target="tpu_custom_call" | custom-call | flops 100000000 | bytes 1572864 | tf_op jit(solution)/shard_map/halving/pallas_call | solution.py:193
  69.4 3.3 %halving.8 = (f32[2,128,384]{2,1,0:T(8,128)}, f32[2,128,384]{2,1,0:T(8,128)}) custom-call(s32[34,6]{1,0:T(8,128)} %copy.35.masks, f32[4,128,384]{2,1,0:T(8,128)} %get-tuple-element.36.stay_a.stay_b, f32[4,128,384]{2,1,0:T(8,128)} %copy-done.2, f32[4,128,384]{2,1,0:T(8,128)} %get-tuple-element.36.stay_a.stay_b, f32[4,128,384]{2,1,0:T(8,128)} %copy-done.2), custom_call_target="tpu_custom_call" | custom-call | flops 100000000 | bytes 1572864 | tf_op jit(solution)/shard_map/halving/pallas_call | solution.py:193
  72.7 1.3 collective-permute-start.9
  74.9 3.3 %halving.10 = (f32[2,128,384]{2,1,0:T(8,128)}, f32[2,128,384]{2,1,0:T(8,128)}) custom-call(s32[34,6]{1,0:T(8,128)} %copy.35.masks, f32[4,128,384]{2,1,0:T(8,128)} %get-tuple-element.42.stay_a.stay_b, f32[4,128,384]{2,1,0:T(8,128)} %copy-done.1, f32[4,128,384]{2,1,0:T(8,128)} %get-tuple-element.42.stay_a.stay_b, f32[4,128,384]{2,1,0:T(8,128)} %copy-done.1), custom_call_target="tpu_custom_call" | custom-call | flops 100000000 | bytes 1572864 | tf_op jit(solution)/shard_map/halving/pallas_call | solution.py:193
  80.1 3.0 %halving.7 = (f32[1,128,384]{2,1,0:T(8,128)}, f32[1,128,384]{2,1,0:T(8,128)}) custom-call(s32[34,6]{1,0:T(8,128)} %copy.35.masks, f32[2,128,384]{2,1,0:T(8,128)} %get-tuple-element.32.stay_a.stay_b, f32[2,128,384]{2,1,0:T(8,128)} %copy-done.7, f32[2,128,384]{2,1,0:T(8,128)} %get-tuple-element.32.stay_a.stay_b, f32[2,128,384]{2,1,0:T(8,128)} %copy-done.7), custom_call_target="tpu_custom_call" | custom-call | flops 100000000 | bytes 1572864 | tf_op jit(solution)/shard_map/halving/pallas_call | solution.py:193
  83.1 1.3 collective-permute-start.7
  84.4 1.4 collective-permute-done.9.came_a.came_b
  86.6 3.0 %halving.9 = (f32[1,128,384]{2,1,0:T(8,128)}, f32[1,128,384]{2,1,0:T(8,128)}) custom-call(s32[34,6]{1,0:T(8,128)} %copy.35.masks, f32[2,128,384]{2,1,0:T(8,128)} %get-tuple-element.38.stay_a.stay_b, f32[2,128,384]{2,1,0:T(8,128)} %copy-done.5, f32[2,128,384]{2,1,0:T(8,128)} %get-tuple-element.38.stay_a.stay_b, f32[2,128,384]{2,1,0:T(8,128)} %copy-done.5), custom_call_target="tpu_custom_call" | custom-call | flops 100000000 | bytes 1572864 | tf_op jit(solution)/shard_map/halving/pallas_call | solution.py:193
  89.6 3.1 %collective-permute-start.10 = (f32[1,128,384]{2,1,0:T(8,128)}, f32[1,128,384]{2,1,0:T(8,128)S(1)}, u32[]{:S(2)}, u32[]{:S(2)}) collective-permute-start(f32[1,128,384]{2,1,0:T(8,128)} %get-tuple-element.41), channel_id=1, source_target_pairs={{0,16},{16,0},{32,48},{48,32},{64,80},{80,64},{1,17},{17,1},{33,49... | collective-permute-start | bytes 589832 | tf_op jit(solution)/shard_map/ppermute | solution.py:459
  93.4 3.0 %halving.11 = (f32[1,128,384]{2,1,0:T(8,128)}, f32[1,128,384]{2,1,0:T(8,128)}) custom-call(s32[34,6]{1,0:T(8,128)} %copy.35.masks, f32[2,128,384]{2,1,0:T(8,128)} %get-tuple-element.44.stay_a.stay_b, f32[2,128,384]{2,1,0:T(8,128)} %copy-done.6, f32[2,128,384]{2,1,0:T(8,128)} %get-tuple-element.44.stay_a.stay_b, f32[2,128,384]{2,1,0:T(8,128)} %copy-done.6), custom_call_target="tpu_custom_call" | custom-call | flops 100000000 | bytes 1572864 | tf_op jit(solution)/shard_map/halving/pallas_call | solution.py:193
  96.4 4.3 %collective-permute-start.13 = (f32[1,128,384]{2,1,0:T(8,128)}, f32[1,128,384]{2,1,0:T(8,128)S(1)}, u32[]{:S(2)}, u32[]{:S(2)}) collective-permute-start(f32[1,128,384]{2,1,0:T(8,128)} %get-tuple-element.47), channel_id=1, source_target_pairs={{0,32},{16,48},{32,0},{48,16},{96,64},{112,80},{1,33},{17,49},{33,... | collective-permute-start | bytes 589832 | tf_op jit(solution)/shard_map/ppermute | solution.py:459
  100.7 3.8 %collective-permute-done.13.refs_5_ = f32[1,128,384]{2,1,0:T(8,128)S(1)} collective-permute-done((f32[1,128,384]{2,1,0:T(8,128)}, f32[1,128,384]{2,1,0:T(8,128)S(1)}, u32[]{:S(2)}, u32[]{:S(2)}) %collective-permute-start.13) | collective-permute-done | bytes 196640 | tf_op jit(solution)/shard_map/ppermute | solution.py:459
  105.2 2.2 %row.1.refs_0_ = f32[128,1152]{1,0:T(8,128)} custom-call(s32[34,6]{1,0:T(8,128)} %copy.35.masks, f32[1,128,384]{2,1,0:T(8,128)} %get-tuple-element.34.refs_0_, f32[1,128,384]{2,1,0:T(8,128)} %copy-done.14, f32[1,128,384]{2,1,0:T(8,128)} %get-tuple-element.40.refs_2_, f32[1,128,384]{2,1,0:T(8,128)} %copy-done.15, f32[1,128,384]{2,1,0:T(8,128)} %get-tuple-element.46.refs_4_, ...), custom_call_target="tpu_custom_call" | custom-call | flops 10000000 | bytes 2359296 | tf_op jit(solution)/shard_map/row/pallas_call | solution.py:221
  108.7 1.7 collective-permute-start.14
  110.4 16.8 %collective-permute-done.16 = f32[128,1152]{1,0:T(8,128)S(1)} collective-permute-done((f32[128,1152]{1,0:T(8,128)}, f32[128,1152]{1,0:T(8,128)S(1)}, u32[]{:S(2)}, u32[]{:S(2)}) %collective-permute-start.16) | collective-permute-done | bytes 589856 | tf_op jit(solution)/shard_map/ppermute | solution.py:475
  127.3 5.2 %collective-permute-start.18 = (f32[128,1152]{1,0:T(8,128)S(1)}, f32[128,1152]{1,0:T(8,128)S(1)}, u32[]{:S(2)}, u32[]{:S(2)}) collective-permute-start(f32[128,1152]{1,0:T(8,128)S(1)} %broadcast_select_fusion), channel_id=1, source_target_pairs={{0,4},{16,20},{32,36},{48,52},{1,5},{17,21},{33,37},{49,53},{68,64... | collective-permute-start | bytes 1769480 | tf_op jit(solution)/shard_map/ppermute | solution.py:480
  133.2 1.3 collective-permute-start.15
  134.5 5.3 %collective-permute-done.18 = f32[128,1152]{1,0:T(8,128)S(1)} collective-permute-done((f32[128,1152]{1,0:T(8,128)S(1)}, f32[128,1152]{1,0:T(8,128)S(1)}, u32[]{:S(2)}, u32[]{:S(2)}) %collective-permute-start.18) | collective-permute-done | bytes 589856 | tf_op jit(solution)/shard_map/ppermute | solution.py:480
  140.7 3.1 %column.2 = (f32[64,768]{1,0:T(8,128)}, f32[64,768]{1,0:T(8,128)}) custom-call(s32[34,6]{1,0:T(8,128)} %copy.35.masks, f32[128,1152]{1,0:T(8,128)} %select_select_fusion.value_ref.refs_1_, bf16[9,2,6,128,128]{4,3,2,1,0:T(8,128)(2,1)} %bitcast.13), custom_call_target="tpu_custom_call" | custom-call | flops 452984832 | bytes 4000000 | tf_op jit(solution)/shard_map/column/pallas_call | solution.py:256
  143.8 2.7 %collective-permute-done.15 = f32[128,1152]{1,0:T(8,128)S(1)} collective-permute-done((f32[128,1152]{1,0:T(8,128)S(1)}, f32[128,1152]{1,0:T(8,128)S(1)}, u32[]{:S(2)}, u32[]{:S(2)}) %collective-permute-start.15) | collective-permute-done | bytes 589856 | tf_op jit(solution)/shard_map/ppermute | solution.py:476
  147.4 3.2 %column.3 = (f32[64,768]{1,0:T(8,128)}, f32[64,768]{1,0:T(8,128)}) custom-call(s32[34,6]{1,0:T(8,128)} %copy.35.masks, f32[128,1152]{1,0:T(8,128)} %broadcast_select_fusion.1.value_ref.refs_2_, bf16[9,2,6,128,128]{4,3,2,1,0:T(8,128)(2,1)} %bitcast.14, f32[64,768]{1,0:T(8,128)} %get-tuple-element.48.refs_0_, f32[64,768]{1,0:T(8,128)} %get-tuple-element.49.refs_1_), custom_call_target="tpu_custom_call" | custom-call | flops 452984832 | bytes 4000000 | tf_op jit(solution)/shard_map/column/pallas_call | solution.py:256
  150.5 4.1 %collective-permute-start.19 = (f32[64,768]{1,0:T(8,128)}, f32[64,768]{1,0:T(8,128)S(1)}, u32[]{:S(2)}, u32[]{:S(2)}) collective-permute-start(f32[64,768]{1,0:T(8,128)} %get-tuple-element.50), channel_id=1, source_target_pairs={{0,16},{1,17},{2,18},{3,19},{4,20},{5,21},{16,0},{17,1},{18,2},{19... | collective-permute-start | bytes 589832 | tf_op jit(solution)/shard_map/ppermute | solution.py:492
  154.6 1.9 collective-permute-start.22
  156.6 3.0 %collective-permute-done.19 = f32[64,768]{1,0:T(8,128)S(1)} collective-permute-done((f32[64,768]{1,0:T(8,128)}, f32[64,768]{1,0:T(8,128)S(1)}, u32[]{:S(2)}, u32[]{:S(2)}) %collective-permute-start.19) | collective-permute-done | bytes 196640 | tf_op jit(solution)/shard_map/ppermute | solution.py:492
  160.5 3.0 %collective-permute-start.20 = (f32[64,768]{1,0:T(8,128)S(1)}, f32[64,768]{1,0:T(8,128)S(1)}, u32[]{:S(2)}, u32[]{:S(2)}) collective-permute-start(f32[64,768]{1,0:T(8,128)S(1)} %add.82), channel_id=1, source_target_pairs={{0,32},{1,33},{2,34},{3,35},{4,36},{5,37},{16,48},{17,49},{18,50},... | collective-permute-start | bytes 589832 | tf_op jit(solution)/shard_map/ppermute | solution.py:492
  164.5 4.2 %collective-permute-start.23 = (f32[64,768]{1,0:T(8,128)S(1)}, f32[64,768]{1,0:T(8,128)S(1)}, u32[]{:S(2)}, u32[]{:S(2)}) collective-permute-start(f32[64,768]{1,0:T(8,128)S(1)} %add.85), channel_id=1, source_target_pairs={{0,96},{1,97},{2,98},{3,99},{4,100},{5,101},{16,112},{17,113},{18,... | collective-permute-start | bytes 589832 | tf_op jit(solution)/shard_map/ppermute | solution.py:492
  169.2 4.2 %collective-permute-start.21 = (f32[64,768]{1,0:T(8,128)S(1)}, f32[64,768]{1,0:T(8,128)S(1)}, u32[]{:S(2)}, u32[]{:S(2)}) collective-permute-start(f32[64,768]{1,0:T(8,128)S(1)} %add.83), channel_id=1, source_target_pairs={{0,96},{1,97},{2,98},{3,99},{4,100},{5,101},{16,112},{17,113},{18,... | collective-permute-start | bytes 589832 | tf_op jit(solution)/shard_map/ppermute | solution.py:492
  173.4 1.9 collective-permute-done.23
  175.3 2.0 collective-permute-start.24
  177.3 1.6 collective-permute-done.21
  178.9 3.9 %collective-permute-done.24 = f32[64,768]{1,0:T(8,128)S(1)} collective-permute-done((f32[64,768]{1,0:T(8,128)S(1)}, f32[64,768]{1,0:T(8,128)S(1)}, u32[]{:S(2)}, u32[]{:S(2)}) %collective-permute-start.24) | collective-permute-done | bytes 196640 | tf_op jit(solution)/shard_map/ppermute | solution.py:492
  182.9 1.9 collective-permute-start.26
  184.9 5.1 %collective-permute-start.25 = (f32[128,768]{1,0:T(8,128)S(1)}, f32[128,768]{1,0:T(8,128)S(1)}, u32[]{:S(2)}, u32[]{:S(2)}) collective-permute-start(f32[128,768]{1,0:T(8,128)S(1)} %pad_maximum_fusion.1.refs_0_), channel_id=1, source_target_pairs={{0,18},{16,2},{32,50},{48,34},{64,82},{80,66},{96,114},{112,98},{1... | collective-permute-start | bytes 1179656 | tf_op jit(solution)/shard_map/ppermute | solution.py:504
  190.0 1.9 collective-permute-start.27
  191.9 2.8 %collective-permute-done.26.refs_2_ = f32[128,768]{1,0:T(8,128)S(1)} collective-permute-done((f32[128,768]{1,0:T(8,128)S(1)}, f32[128,768]{1,0:T(8,128)S(1)}, u32[]{:S(2)}, u32[]{:S(2)}) %collective-permute-start.26) | collective-permute-done | bytes 393248 | tf_op jit(solution)/shard_map/ppermute | solution.py:504
  194.8 1.9 collective-permute-start.29
  196.7 3.1 %collective-permute-done.25.refs_1_ = f32[128,768]{1,0:T(8,128)S(1)} collective-permute-done((f32[128,768]{1,0:T(8,128)S(1)}, f32[128,768]{1,0:T(8,128)S(1)}, u32[]{:S(2)}, u32[]{:S(2)}) %collective-permute-start.25) | collective-permute-done | bytes 393248 | tf_op jit(solution)/shard_map/ppermute | solution.py:504
  199.7 1.9 collective-permute-start.28
  201.7 3.0 %patch.1.refs_9_ = f32[18,9,128,128]{3,2,1,0:T(8,128)} custom-call(s32[34,6]{1,0:T(8,128)} %copy.35.masks, f32[128,1152]{1,0:T(8,128)} %row.1.refs_0_, f32[128,1152]{1,0:T(8,128)} %select_select_fusion.value_ref.refs_1_, f32[128,1152]{1,0:T(8,128)} %broadcast_select_fusion.1.value_ref.refs_2_, ...), custom_call_target="tpu_custom_call", output_to_operand_aliasing={{}: (4, {})} | custom-call | flops 100000000 | bytes 4000000 | tf_op jit(solution)/shard_map/patch/pallas_call | solution.py:384
  206.4 5.8 %corner.1 = f32[18,9,128,128]{3,2,1,0:T(8,128)} custom-call(s32[34,6]{1,0:T(8,128)} %copy.35.masks, f32[128,768]{1,0:T(8,128)} %copy-done.8, f32[128,768]{1,0:T(8,128)} %copy-done.10, f32[128,768]{1,0:T(8,128)} %copy-done.9, f32[128,768]{1,0:T(8,128)} %copy-done.11, f32[128,768]{1,0:T(8,128)} %copy-done.13, ...), custom_call_target="tpu_custom_call", output_to_operand_aliasing={{}: (10, {})} | custom-call | flops 1000000000 | bytes 1000000 | tf_op jit(solution)/shard_map/corner/pallas_call | solution.py:314
  (88 shorter events, 25.1 us)
Async XLA Ops:
  0.9 4.6 %collective-permute-start = (bf16[1,6,64,128]{3,2,1,0:T(8,128)(2,1)S(1)}, bf16[1,6,64,128]{3,2,1,0:T(8,128)(2,1)S(1)}, u32[]{:S(2)}, u32[]{:S(2)}) collective-permute-start(bf16[1,6,64,128]{3,2,1,0:T(8,128)(2,1)S(1)} %dynamic-slice_bitcast_fusion), channel_id=1, source_target_pairs={{0,16},{16,0},{32,48},{48,32},{64,80},{80,64},{96,112},{112,96},{1... | collective-permute-start | bytes 294920 | tf_op jit(solution)/shard_map/ppermute | solution.py:433
  5.5 11.9 %collective-permute-start.3 = (bf16[2,6,64,128]{3,2,1,0:T(8,128)(2,1)S(1)}, bf16[2,6,64,128]{3,2,1,0:T(8,128)(2,1)S(1)}, u32[]{:S(2)}, u32[]{:S(2)}) collective-permute-start(bf16[2,6,64,128]{3,2,1,0:T(8,128)(2,1)S(1)} %maximum_select_fusion), channel_id=1, source_target_pairs={{0,96},{16,112},{32,0},{48,16},{64,32},{80,48},{96,64},{112,80},{1... | collective-permute-start | bytes 589832 | tf_op jit(solution)/shard_map/ppermute | solution.py:434
  9.8 9.3 %collective-permute-start.2 = (bf16[2,6,64,128]{3,2,1,0:T(8,128)(2,1)S(1)}, bf16[2,6,64,128]{3,2,1,0:T(8,128)(2,1)S(1)}, u32[]{:S(2)}, u32[]{:S(2)}) collective-permute-start(bf16[2,6,64,128]{3,2,1,0:T(8,128)(2,1)S(1)} %maximum_select_fusion), channel_id=1, source_target_pairs={{0,64},{16,80},{32,96},{48,112},{64,0},{80,16},{96,32},{112,48},{1... | collective-permute-start | bytes 589832 | tf_op jit(solution)/shard_map/ppermute | solution.py:434
  9.8 11.1 %collective-permute-start.1 = (bf16[2,6,64,128]{3,2,1,0:T(8,128)(2,1)S(1)}, bf16[2,6,64,128]{3,2,1,0:T(8,128)(2,1)S(1)}, u32[]{:S(2)}, u32[]{:S(2)}) collective-permute-start(bf16[2,6,64,128]{3,2,1,0:T(8,128)(2,1)S(1)} %maximum_select_fusion), channel_id=1, source_target_pairs={{0,32},{16,48},{32,64},{48,80},{64,96},{80,112},{96,0},{112,16},{1... | collective-permute-start | bytes 589832 | tf_op jit(solution)/shard_map/ppermute | solution.py:434
  21.0 18.1 %copy-start = (bf16[6,6,64,128]{3,2,1,0:T(8,128)(2,1)}, bf16[6,6,64,128]{3,2,1,0:T(8,128)(2,1)S(1)}, u32[]{:S(2)}) copy-start(bf16[6,6,64,128]{3,2,1,0:T(8,128)(2,1)S(1)} %pad_maximum_fusion.refs_1_.refs_6_) | copy-start | bytes 1769476
  21.0 18.1 %collective-permute-start.4 = (bf16[6,6,64,128]{3,2,1,0:T(8,128)(2,1)S(1)}, bf16[6,6,64,128]{3,2,1,0:T(8,128)(2,1)S(1)}, u32[]{:S(2)}, u32[]{:S(2)}) collective-permute-start(bf16[6,6,64,128]{3,2,1,0:T(8,128)(2,1)S(1)} %pad_maximum_fusion.refs_1_.refs_6_), channel_id=1, source_target_pairs={{0,1},{1,0},{2,3},{3,2},{4,5},{5,4},{6,7},{7,6},{8,9},{9,8},{10,11... | collective-permute-start | bytes 1769480 | tf_op jit(solution)/shard_map/ppermute | solution.py:440
  39.1 0.9 copy-start.3
  46.8 21.7 %collective-permute-start.8 = (f32[4,128,384]{2,1,0:T(8,128)}, f32[4,128,384]{2,1,0:T(8,128)S(1)}, u32[]{:S(2)}, u32[]{:S(2)}) collective-permute-start(f32[4,128,384]{2,1,0:T(8,128)} %get-tuple-element.37), channel_id=1, source_target_pairs={{0,32},{16,48},{32,0},{48,16},{64,96},{80,112},{96,64},{112,80},{1... | collective-permute-start | bytes 2359304 | tf_op jit(solution)/shard_map/ppermute | solution.py:459
  46.8 27.2 %collective-permute-start.11 = (f32[4,128,384]{2,1,0:T(8,128)}, f32[4,128,384]{2,1,0:T(8,128)S(1)}, u32[]{:S(2)}, u32[]{:S(2)}) collective-permute-start(f32[4,128,384]{2,1,0:T(8,128)} %get-tuple-element.43), channel_id=1, source_target_pairs={{0,96},{16,112},{32,64},{48,80},{64,32},{80,48},{96,0},{112,16},{1... | collective-permute-start | bytes 2359304 | tf_op jit(solution)/shard_map/ppermute | solution.py:459
  47.9 15.4 %collective-permute-start.5 = (f32[3,128,384]{2,1,0:T(8,128)}, f32[3,128,384]{2,1,0:T(8,128)S(1)}, u32[]{:S(2)}, u32[]{:S(2)}) collective-permute-start(f32[3,128,384]{2,1,0:T(8,128)} %get-tuple-element.31), channel_id=1, source_target_pairs={{0,16},{16,0},{32,48},{48,32},{64,80},{80,64},{96,112},{112,96},{1... | collective-permute-start | bytes 1769480 | tf_op jit(solution)/shard_map/ppermute | solution.py:459
  63.4 0.8 copy-start.4
  67.4 12.0 %collective-permute-start.6 = (f32[2,128,384]{2,1,0:T(8,128)}, f32[2,128,384]{2,1,0:T(8,128)S(1)}, u32[]{:S(2)}, u32[]{:S(2)}) collective-permute-start(f32[2,128,384]{2,1,0:T(8,128)} %get-tuple-element.33), channel_id=1, source_target_pairs={{0,32},{16,48},{32,0},{48,16},{64,96},{80,112},{96,64},{112,80},{1... | collective-permute-start | bytes 1179656 | tf_op jit(solution)/shard_map/ppermute | solution.py:459
  68.5 0.9 copy-start.2
  72.7 13.1 %collective-permute-start.9 = (f32[2,128,384]{2,1,0:T(8,128)}, f32[2,128,384]{2,1,0:T(8,128)S(1)}, u32[]{:S(2)}, u32[]{:S(2)}) collective-permute-start(f32[2,128,384]{2,1,0:T(8,128)} %get-tuple-element.39), channel_id=1, source_target_pairs={{32,64},{48,80},{64,32},{80,48},{96,0},{112,16},{33,65},{49,81},{6... | collective-permute-start | bytes 1179656 | tf_op jit(solution)/shard_map/ppermute | solution.py:459
  74.0 0.9 copy-start.1
  78.2 14.4 %collective-permute-start.12 = (f32[2,128,384]{2,1,0:T(8,128)}, f32[2,128,384]{2,1,0:T(8,128)S(1)}, u32[]{:S(2)}, u32[]{:S(2)}) collective-permute-start(f32[2,128,384]{2,1,0:T(8,128)} %get-tuple-element.45), channel_id=1, source_target_pairs={{0,16},{16,0},{32,48},{48,32},{64,80},{80,64},{96,112},{112,96},{1... | collective-permute-start | bytes 1179656 | tf_op jit(solution)/shard_map/ppermute | solution.py:459
  79.4 0.8 copy-start.7
  83.1 17.5 %collective-permute-start.7 = (f32[1,128,384]{2,1,0:T(8,128)}, f32[1,128,384]{2,1,0:T(8,128)S(1)}, u32[]{:S(2)}, u32[]{:S(2)}) collective-permute-start(f32[1,128,384]{2,1,0:T(8,128)} %get-tuple-element.35), channel_id=1, source_target_pairs={{32,64},{48,80},{64,32},{80,48},{96,0},{112,16},{33,65},{49,81},{6... | collective-permute-start | bytes 589832 | tf_op jit(solution)/shard_map/ppermute | solution.py:459
  85.8 0.8 copy-start.5
  89.6 11.1 %collective-permute-start.10 = (f32[1,128,384]{2,1,0:T(8,128)}, f32[1,128,384]{2,1,0:T(8,128)S(1)}, u32[]{:S(2)}, u32[]{:S(2)}) collective-permute-start(f32[1,128,384]{2,1,0:T(8,128)} %get-tuple-element.41), channel_id=1, source_target_pairs={{0,16},{16,0},{32,48},{48,32},{64,80},{80,64},{1,17},{17,1},{33,49... | collective-permute-start | bytes 589832 | tf_op jit(solution)/shard_map/ppermute | solution.py:459
  92.6 0.8 copy-start.6
  96.4 8.1 %collective-permute-start.13 = (f32[1,128,384]{2,1,0:T(8,128)}, f32[1,128,384]{2,1,0:T(8,128)S(1)}, u32[]{:S(2)}, u32[]{:S(2)}) collective-permute-start(f32[1,128,384]{2,1,0:T(8,128)} %get-tuple-element.47), channel_id=1, source_target_pairs={{0,32},{16,48},{32,0},{48,16},{96,64},{112,80},{1,33},{17,49},{33,... | collective-permute-start | bytes 589832 | tf_op jit(solution)/shard_map/ppermute | solution.py:459
  100.7 3.8 %copy-start.14 = (f32[1,128,384]{2,1,0:T(8,128)}, f32[1,128,384]{2,1,0:T(8,128)S(1)}, u32[]{:S(2)}) copy-start(f32[1,128,384]{2,1,0:T(8,128)S(1)} %collective-permute-done.7.refs_1_) | copy-start | bytes 589828
  100.7 3.8 %copy-start.15 = (f32[1,128,384]{2,1,0:T(8,128)}, f32[1,128,384]{2,1,0:T(8,128)S(1)}, u32[]{:S(2)}) copy-start(f32[1,128,384]{2,1,0:T(8,128)S(1)} %collective-permute-done.10.refs_3_) | copy-start | bytes 589828
  104.5 0.7 copy-start.16
  107.4 19.8 %collective-permute-start.16 = (f32[128,1152]{1,0:T(8,128)}, f32[128,1152]{1,0:T(8,128)S(1)}, u32[]{:S(2)}, u32[]{:S(2)}) collective-permute-start(f32[128,1152]{1,0:T(8,128)} %row.1.refs_0_), channel_id=1, source_target_pairs={{64,0},{65,16},{66,32},{67,48},{68,68},{69,84},{70,100},{71,116},{... | collective-permute-start | bytes 1769480 | tf_op jit(solution)/shard_map/ppermute | solution.py:475
  108.7 18.5 %collective-permute-start.14 = (f32[128,1152]{1,0:T(8,128)}, f32[128,1152]{1,0:T(8,128)S(1)}, u32[]{:S(2)}, u32[]{:S(2)}) collective-permute-start(f32[128,1152]{1,0:T(8,128)} %row.1.refs_0_), channel_id=1, source_target_pairs={{0,0},{1,16},{2,32},{3,48},{4,68},{5,84},{6,100},{7,116},{8,8},{9,... | collective-permute-start | bytes 1769480 | tf_op jit(solution)/shard_map/ppermute | solution.py:474
  127.3 12.5 %collective-permute-start.18 = (f32[128,1152]{1,0:T(8,128)S(1)}, f32[128,1152]{1,0:T(8,128)S(1)}, u32[]{:S(2)}, u32[]{:S(2)}) collective-permute-start(f32[128,1152]{1,0:T(8,128)S(1)} %broadcast_select_fusion), channel_id=1, source_target_pairs={{0,4},{16,20},{32,36},{48,52},{1,5},{17,21},{33,37},{49,53},{68,64... | collective-permute-start | bytes 1769480 | tf_op jit(solution)/shard_map/ppermute | solution.py:480
  132.5 11.3 %collective-permute-start.17 = (f32[128,1152]{1,0:T(8,128)S(1)}, f32[128,1152]{1,0:T(8,128)S(1)}, u32[]{:S(2)}, u32[]{:S(2)}) collective-permute-start(f32[128,1152]{1,0:T(8,128)S(1)} %collective-permute-done.16), channel_id=1, source_target_pairs={{8,4},{24,20},{40,36},{56,52},{76,68},{92,84},{108,100},{124,116},... | collective-permute-start | bytes 1769480 | tf_op jit(solution)/shard_map/ppermute | solution.py:477
  133.2 13.3 %collective-permute-start.15 = (f32[128,1152]{1,0:T(8,128)S(1)}, f32[128,1152]{1,0:T(8,128)S(1)}, u32[]{:S(2)}, u32[]{:S(2)}) collective-permute-start(f32[128,1152]{1,0:T(8,128)S(1)} %collective-permute-done.14), channel_id=1, source_target_pairs={{8,0},{24,16},{40,32},{56,48},{76,64},{92,80},{108,96},{124,112},{... | collective-permute-start | bytes 1769480 | tf_op jit(solution)/shard_map/ppermute | solution.py:476
  150.5 9.0 %collective-permute-start.19 = (f32[64,768]{1,0:T(8,128)}, f32[64,768]{1,0:T(8,128)S(1)}, u32[]{:S(2)}, u32[]{:S(2)}) collective-permute-start(f32[64,768]{1,0:T(8,128)} %get-tuple-element.50), channel_id=1, source_target_pairs={{0,16},{1,17},{2,18},{3,19},{4,20},{5,21},{16,0},{17,1},{18,2},{19... | collective-permute-start | bytes 589832 | tf_op jit(solution)/shard_map/ppermute | solution.py:492
  154.6 8.9 %collective-permute-start.22 = (f32[64,768]{1,0:T(8,128)}, f32[64,768]{1,0:T(8,128)S(1)}, u32[]{:S(2)}, u32[]{:S(2)}) collective-permute-start(f32[64,768]{1,0:T(8,128)} %get-tuple-element.51), channel_id=1, source_target_pairs={{0,32},{1,33},{2,34},{3,35},{4,36},{5,37},{16,48},{17,49},{18,50},... | collective-permute-start | bytes 589832 | tf_op jit(solution)/shard_map/ppermute | solution.py:492
  160.5 8.6 %collective-permute-start.20 = (f32[64,768]{1,0:T(8,128)S(1)}, f32[64,768]{1,0:T(8,128)S(1)}, u32[]{:S(2)}, u32[]{:S(2)}) collective-permute-start(f32[64,768]{1,0:T(8,128)S(1)} %add.82), channel_id=1, source_target_pairs={{0,32},{1,33},{2,34},{3,35},{4,36},{5,37},{16,48},{17,49},{18,50},... | collective-permute-start | bytes 589832 | tf_op jit(solution)/shard_map/ppermute | solution.py:492
  164.5 10.8 %collective-permute-start.23 = (f32[64,768]{1,0:T(8,128)S(1)}, f32[64,768]{1,0:T(8,128)S(1)}, u32[]{:S(2)}, u32[]{:S(2)}) collective-permute-start(f32[64,768]{1,0:T(8,128)S(1)} %add.85), channel_id=1, source_target_pairs={{0,96},{1,97},{2,98},{3,99},{4,100},{5,101},{16,112},{17,113},{18,... | collective-permute-start | bytes 589832 | tf_op jit(solution)/shard_map/ppermute | solution.py:492
  169.2 9.7 %collective-permute-start.21 = (f32[64,768]{1,0:T(8,128)S(1)}, f32[64,768]{1,0:T(8,128)S(1)}, u32[]{:S(2)}, u32[]{:S(2)}) collective-permute-start(f32[64,768]{1,0:T(8,128)S(1)} %add.83), channel_id=1, source_target_pairs={{0,96},{1,97},{2,98},{3,99},{4,100},{5,101},{16,112},{17,113},{18,... | collective-permute-start | bytes 589832 | tf_op jit(solution)/shard_map/ppermute | solution.py:492
  175.3 7.6 %collective-permute-start.24 = (f32[64,768]{1,0:T(8,128)S(1)}, f32[64,768]{1,0:T(8,128)S(1)}, u32[]{:S(2)}, u32[]{:S(2)}) collective-permute-start(f32[64,768]{1,0:T(8,128)S(1)} %add.86), channel_id=1, source_target_pairs={{0,16},{1,17},{2,18},{3,19},{4,20},{5,21},{16,0},{17,1},{18,2},{19... | collective-permute-start | bytes 589832 | tf_op jit(solution)/shard_map/ppermute | solution.py:492
  182.9 21.8 %copy-start.8 = (f32[128,768]{1,0:T(8,128)}, f32[128,768]{1,0:T(8,128)S(1)}, u32[]{:S(2)}) copy-start(f32[128,768]{1,0:T(8,128)S(1)} %pad_maximum_fusion.1.refs_0_) | copy-start | bytes 1179652
  182.9 11.8 %collective-permute-start.26 = (f32[128,768]{1,0:T(8,128)S(1)}, f32[128,768]{1,0:T(8,128)S(1)}, u32[]{:S(2)}, u32[]{:S(2)}) collective-permute-start(f32[128,768]{1,0:T(8,128)S(1)} %pad_maximum_fusion.1.refs_0_), channel_id=1, source_target_pairs={{0,4},{16,20},{32,36},{48,52},{64,68},{80,84},{96,100},{112,116},{... | collective-permute-start | bytes 1179656 | tf_op jit(solution)/shard_map/ppermute | solution.py:504
  184.9 14.9 %collective-permute-start.25 = (f32[128,768]{1,0:T(8,128)S(1)}, f32[128,768]{1,0:T(8,128)S(1)}, u32[]{:S(2)}, u32[]{:S(2)}) collective-permute-start(f32[128,768]{1,0:T(8,128)S(1)} %pad_maximum_fusion.1.refs_0_), channel_id=1, source_target_pairs={{0,18},{16,2},{32,50},{48,34},{64,82},{80,66},{96,114},{112,98},{1... | collective-permute-start | bytes 1179656 | tf_op jit(solution)/shard_map/ppermute | solution.py:504
  190.0 14.7 %collective-permute-start.27 = (f32[128,768]{1,0:T(8,128)S(1)}, f32[128,768]{1,0:T(8,128)S(1)}, u32[]{:S(2)}, u32[]{:S(2)}) collective-permute-start(f32[128,768]{1,0:T(8,128)S(1)} %pad_maximum_fusion.1.refs_0_), channel_id=1, source_target_pairs={{0,1},{1,0},{2,3},{3,2},{4,5},{5,4},{16,17},{17,16},{18,19},{19,18... | collective-permute-start | bytes 1179656 | tf_op jit(solution)/shard_map/ppermute | solution.py:506
  194.8 10.0 %copy-start.9 = (f32[128,768]{1,0:T(8,128)}, f32[128,768]{1,0:T(8,128)S(1)}, u32[]{:S(2)}) copy-start(f32[128,768]{1,0:T(8,128)S(1)} %collective-permute-done.26.refs_2_) | copy-start | bytes 1179652
  194.8 10.0 %collective-permute-start.29 = (f32[128,768]{1,0:T(8,128)S(1)}, f32[128,768]{1,0:T(8,128)S(1)}, u32[]{:S(2)}, u32[]{:S(2)}) collective-permute-start(f32[128,768]{1,0:T(8,128)S(1)} %collective-permute-done.26.refs_2_), channel_id=1, source_target_pairs={{0,1},{1,0},{2,3},{3,2},{4,5},{5,4},{16,17},{17,16},{18,19},{19,18... | collective-permute-start | bytes 1179656 | tf_op jit(solution)/shard_map/ppermute | solution.py:506
  199.7 5.0 %copy-start.10 = (f32[128,768]{1,0:T(8,128)}, f32[128,768]{1,0:T(8,128)S(1)}, u32[]{:S(2)}) copy-start(f32[128,768]{1,0:T(8,128)S(1)} %collective-permute-done.25.refs_1_) | copy-start | bytes 1179652
  199.7 5.0 %collective-permute-start.28 = (f32[128,768]{1,0:T(8,128)S(1)}, f32[128,768]{1,0:T(8,128)S(1)}, u32[]{:S(2)}, u32[]{:S(2)}) collective-permute-start(f32[128,768]{1,0:T(8,128)S(1)} %collective-permute-done.25.refs_1_), channel_id=1, source_target_pairs={{0,1},{1,0},{2,3},{3,2},{4,5},{5,4},{16,17},{17,16},{18,19},{19,18... | collective-permute-start | bytes 1179656 | tf_op jit(solution)/shard_map/ppermute | solution.py:506
  204.7 0.8 copy-start.11
  204.8 0.9 copy-start.12
  205.6 0.8 copy-start.13

commit v6 on v5

--- a/solution.py
+++ b/solution.py
@@ -166,42 +166,29 @@
         out_shape=shapes,
         scratch_shapes=[pltpu.VMEM(parts[0].shape, F32)],
         cost_estimate=pl.CostEstimate(flops=1000 * parts[0].size, bytes_accessed=20 * parts[0].size, transcendentals=0),
+        compiler_params=pltpu.CompilerParams(vmem_limit_bytes=24 * 2**20),
         name="eliminate",
     )(masks, *parts, *corner)
 
 
-def halving_kernel(masks, stay_a, came_a, stay_b, came_b, send_ref, keep_ref):
-    send_ref[...] = stay_a[...] + came_a[...]
-    keep_ref[...] = stay_b[...] + came_b[...]
+def halving_kernel(group, stage, masks, stay_ref, came_ref, send_ref, keep_ref):
+    _, _, z, y = place_of(masks)
+    for ref, pieces in zip((send_ref, keep_ref), later_pieces(group, stage, z, y)):
+        for m, n in enumerate(pieces):
+            ref[m] = stay_ref[n] + came_ref[n]
 
 
 def halving(masks, group, stage, stay, came):
     _, width, wide = stay.shape
-    count = 4 - stage
-
-    def piece(side):
-        def index(m, masks):
-            _, _, z, y = place_of(masks)
-            slots = later_pieces(group, stage, z, y)[side]
-            slot = slots[0]
-            for n in range(1, count):
-                slot = jnp.where(m == n, slots[n], slot)
-            return slot, 0, 0
-
-        return pl.BlockSpec((1, width, wide), index)
-
-    return pl.pallas_call(
-        halving_kernel,
-        grid_spec=pltpu.PrefetchScalarGridSpec(
-            num_scalar_prefetch=1,
-            grid=(count,),
-            in_specs=[piece(0), piece(0), piece(1), piece(1)],
-            out_specs=[pl.BlockSpec((1, width, wide), lambda m, _: (m, 0, 0))] * 2,
-        ),
-        out_shape=[jax.ShapeDtypeStruct((count, width, wide), F32)] * 2,
+    return pl.pallas_call(
+        functools.partial(halving_kernel, group, stage),
+        in_specs=[SMEM, VMEM, VMEM],
+        out_specs=[VMEM] * 2,
+        out_shape=[jax.ShapeDtypeStruct((4 - stage, width, wide), F32)] * 2,
         cost_estimate=pl.CostEstimate(flops=10**8, bytes_accessed=32 * width * wide, transcendentals=0),
+        compiler_params=pltpu.CompilerParams(vmem_limit_bytes=8 * 2**20),
         name="halving",
-    )(masks, stay, came, stay, came)
+    )(masks, stay, came)
 
 
 def row_kernel(masks, *refs):
@@ -224,6 +211,7 @@
         out_specs=VMEM,
         out_shape=jax.ShapeDtypeStruct((width, wide * len(given) // 2), F32),
         cost_estimate=pl.CostEstimate(flops=10**7, bytes_accessed=8 * width * wide * len(given), transcendentals=0),
+        compiler_params=pltpu.CompilerParams(vmem_limit_bytes=12 * 2**20),
         name="row",
     )(masks, *given)
 
@@ -261,6 +249,7 @@
         out_specs=[VMEM] * 2,
         out_shape=[jax.ShapeDtypeStruct((width // 2, steps * width), F32)] * 2,
         cost_estimate=pl.CostEstimate(flops=4 * count * steps * width**3, bytes_accessed=4 * 10**6, transcendentals=0),
+        compiler_params=pltpu.CompilerParams(vmem_limit_bytes=16 * 2**20),
         name="column",
     )(masks, value, lower.reshape(count, 2, steps, width, width), *given)
 

time: 216 us -> 202 us (0.935)
  Pallas kernels: 60.9 us -> 41.3 us
  waiting for transfers between devices: 70.3 us -> 76.3 us
  starting transfers between devices: 64.1 us -> 66.9 us
  local copies, waits for them, and re-layouts: 11.6 us -> 8.81 us
    pallas_call x6, Pallas kernels: 18.8 us -> 5.65 us  [halving(): pl.pallas_call(functools.partial(halving_kernel, group, stage), in_specs=...]
    ppermute x9, waiting for transfers between devices: 19.4 us -> 29.9 us  [per_device(): lax.ppermute(send, 'prow', routes[n][stage])]
    ppermute x1, waiting for transfers between devices: 16.8 us -> 9.37 us  [per_device(): lax.ppermute(row, both, [turn(k, *place) for k in range(4, steps) for pla...]
    ppermute x1, starting transfers between devices: 1.72 us -> 5.95 us  [per_device(): lax.ppermute(row, both, [turn(k, *place) for k in range(4) for place in g...]
    ppermute x2, waiting for transfers between devices: 5.88 us -> 9.19 us  [per_device(): turns = [lax.ppermute(sums, both, around(t)) for t in (2, 4)]]
    pallas_call x2, Pallas kernels: 6.27 us -> 3.17 us  [column_products(): pl.pallas_call(functools.partial(column_kernel, parity), grid=(1,), in_sp...]
    pallas_call x1, Pallas kernels: 6.83 us -> 3.91 us  [eliminate(): pl.pallas_call(eliminate_kernel, in_specs=[SMEM] + [VMEM] * (len(parts) +...]
    unnamed x35 -> x25, local copies, waits for them, and re-layouts: 8.17 us -> 5.39 us
  transfers between devices with their start and end apart: 30 -> 30, of which waited for: 17 -> 19; matrix products, arithmetic and copies ran while one was open for 3% -> 2% of each run, Pallas kernels for 20% -> 14%
where the time goes in v6:
time: 202 us; the launch traced here: 199 us
  waiting for transfers between devices  76.3 us (38%)
  starting transfers between devices  66.9 us (33%)
  Pallas kernels  41.3 us (20%)
  local copies, waits for them, and re-layouts  8.81 us (4%)
  other arithmetic  4.96 us (2%)
    ppermute x9, waiting for transfers between devices, per_device(): lax.ppermute(send, 'prow', routes[n][stage])  29.9 us
    pallas_call x1, Pallas kernels, products(): pl.pallas_call(functools.partial(product_kernel, first), grid_spec=pltpu....  18 us
    ppermute x9, starting transfers between devices, per_device(): lax.ppermute(send, 'prow', routes[n][stage])  12.3 us
    ppermute x3, starting transfers between devices, per_device(): lax.ppermute(under, both, here(two))  9.73 us
    ppermute x3, starting transfers between devices, per_device(): lax.ppermute(upper, both, here(one))  9.49 us
    ppermute x1, waiting for transfers between devices, per_device(): lax.ppermute(row, both, [turn(k, *place) for k in range(4, steps) for pla...  9.37 us
    ppermute x2, waiting for transfers between devices, per_device(): turns = [lax.ppermute(sums, both, around(t)) for t in (2, 4)]  9.19 us
    ppermute x3, waiting for transfers between devices, per_device(): lax.ppermute(pair, 'prow', ring(shift))  9.02 us
  transfers between devices with their start and end apart: 30, of which 19 were waited for; matrix products, arithmetic and copies ran while one was open for 2% of the time, Pallas kernels for 14%

profile of v6, /device:TPU:0, one launch (start us, length us, event | category | flops | bytes accessed | tf_op | source)
XLA Modules:
  0.0 199.0 jit_solution(10785499226632122128)
XLA Ops:
  0.9 1.7 collective-permute-start
  5.5 4.2 %collective-permute-start.3 = (bf16[2,6,64,128]{3,2,1,0:T(8,128)(2,1)S(1)}, bf16[2,6,64,128]{3,2,1,0:T(8,128)(2,1)S(1)}, u32[]{:S(2)}, u32[]{:S(2)}) collective-permute-start(bf16[2,6,64,128]{3,2,1,0:T(8,128)(2,1)S(1)} %maximum_select_fusion), channel_id=1, source_target_pairs={{0,96},{16,112},{32,0},{48,16},{64,32},{80,48},{96,64},{112,80},{1... | collective-permute-start | bytes 589832 | tf_op jit(solution)/shard_map/ppermute | solution.py:423
  9.8 1.3 collective-permute-start.1
  11.8 5.6 %collective-permute-done.3 = bf16[2,6,64,128]{3,2,1,0:T(8,128)(2,1)S(1)} collective-permute-done((bf16[2,6,64,128]{3,2,1,0:T(8,128)(2,1)S(1)}, bf16[2,6,64,128]{3,2,1,0:T(8,128)(2,1)S(1)}, u32[]{:S(2)}, u32[]{:S(2)}) %collective-permute-start.3) | collective-permute-done | bytes 196640 | tf_op jit(solution)/shard_map/ppermute | solution.py:423
  17.4 1.6 collective-permute-done.2
  19.0 1.8 collective-permute-done.1
  21.8 18.0 %products.1 = (f32[18,9,128,128]{3,2,1,0:T(8,128)}, f32[6,128,1152]{2,1,0:T(8,128)}) custom-call(s32[34,6]{1,0:T(8,128)} %copy.35.masks, f32[18,9,128,128]{3,2,1,0:T(8,128)} %bitcast.15, bf16[18,6,128,128]{3,2,1,0:T(8,128)(2,1)} %bitcast.12), custom_call_target="tpu_custom_call" | custom-call | flops 8153726976 | bytes 21233664 | tf_op jit(solution)/shard_map/products/pallas_call | solution.py:70
  39.8 2.1 %copy-done.3 = f32[6,128,1152]{2,1,0:T(8,128)S(1)} copy-done((f32[6,128,1152]{2,1,0:T(8,128)S(1)}, f32[6,128,1152]{2,1,0:T(8,128)}, u32[]{:S(2)}) %copy-start.3) | copy-done | bytes 3538968
  42.7 3.9 %eliminate.1 = (f32[3,128,384]{2,1,0:T(8,128)S(1)}, f32[3,128,384]{2,1,0:T(8,128)S(1)}, f32[4,128,384]{2,1,0:T(8,128)S(1)}, f32[4,128,384]{2,1,0:T(8,128)S(1)}, ...) custom-call(s32[34,6]{1,0:T(8,128)S(1)} %copy-done.4, f32[6,128,1152]{2,1,0:T(8,128)S(1)} %copy-done.3, ...), custom_call_target="tpu_custom_call" | custom-call | flops 884736000 | bytes 17694720 | tf_op jit(solution)/shard_map/eliminate/pallas_call | solution.py:162
  49.0 14.2 %collective-permute-done.5.came_ref = f32[3,128,384]{2,1,0:T(8,128)S(1)} collective-permute-done((f32[3,128,384]{2,1,0:T(8,128)S(1)}, f32[3,128,384]{2,1,0:T(8,128)S(1)}, u32[]{:S(2)}, u32[]{:S(2)}) %collective-permute-start.5) | collective-permute-done | bytes 589856 | tf_op jit(solution)/shard_map/ppermute | solution.py:448
  65.2 1.9 collective-permute-done.8.came_ref
  68.0 1.3 collective-permute-start.9
  71.6 3.5 %collective-permute-done.6.came_ref = f32[2,128,384]{2,1,0:T(8,128)S(1)} collective-permute-done((f32[2,128,384]{2,1,0:T(8,128)S(1)}, f32[2,128,384]{2,1,0:T(8,128)S(1)}, u32[]{:S(2)}, u32[]{:S(2)}) %collective-permute-start.6) | collective-permute-done | bytes 393248 | tf_op jit(solution)/shard_map/ppermute | solution.py:448
  76.0 1.3 collective-permute-start.7
  77.3 4.8 %collective-permute-done.9.came_ref = f32[2,128,384]{2,1,0:T(8,128)S(1)} collective-permute-done((f32[2,128,384]{2,1,0:T(8,128)S(1)}, f32[2,128,384]{2,1,0:T(8,128)S(1)}, u32[]{:S(2)}, u32[]{:S(2)}) %collective-permute-start.9) | collective-permute-done | bytes 393248 | tf_op jit(solution)/shard_map/ppermute | solution.py:448
  83.0 3.1 %collective-permute-start.10 = (f32[1,128,384]{2,1,0:T(8,128)S(1)}, f32[1,128,384]{2,1,0:T(8,128)S(1)}, u32[]{:S(2)}, u32[]{:S(2)}) collective-permute-start(f32[1,128,384]{2,1,0:T(8,128)S(1)} %get-tuple-element.41), channel_id=1, source_target_pairs={{0,16},{16,0},{32,48},{48,32},{64,80},{80,64},{1,17},{17,1},{33,49... | collective-permute-start | bytes 589832 | tf_op jit(solution)/shard_map/ppermute | solution.py:448
  87.0 1.9 collective-permute-start.13
  88.9 1.6 collective-permute-done.10.refs_3_
  90.5 4.0 %collective-permute-done.13.refs_5_ = f32[1,128,384]{2,1,0:T(8,128)S(1)} collective-permute-done((f32[1,128,384]{2,1,0:T(8,128)S(1)}, f32[1,128,384]{2,1,0:T(8,128)S(1)}, u32[]{:S(2)}, u32[]{:S(2)}) %collective-permute-start.13) | collective-permute-done | bytes 196640 | tf_op jit(solution)/shard_map/ppermute | solution.py:448
  94.5 1.7 row.1.refs_0_
  96.3 1.3 collective-permute-start.16
  97.6 5.9 %collective-permute-start.14 = (f32[128,1152]{1,0:T(8,128)}, f32[128,1152]{1,0:T(8,128)}, u32[]{:S(2)}, u32[]{:S(2)}) collective-permute-start(f32[128,1152]{1,0:T(8,128)} %row.1.refs_0_), channel_id=1, source_target_pairs={{0,0},{1,16},{2,32},{3,48},{4,68},{5,84},{6,100},{7,116},{8,8},{9,... | collective-permute-start | bytes 1769480 | tf_op jit(solution)/shard_map/ppermute | solution.py:463
  103.5 9.4 %collective-permute-done.16 = f32[128,1152]{1,0:T(8,128)} collective-permute-done((f32[128,1152]{1,0:T(8,128)}, f32[128,1152]{1,0:T(8,128)}, u32[]{:S(2)}, u32[]{:S(2)}) %collective-permute-start.16) | collective-permute-done | bytes 589856 | tf_op jit(solution)/shard_map/ppermute | solution.py:464
  112.9 2.0 broadcast_select_fusion
  114.9 6.2 %collective-permute-start.18 = (f32[128,1152]{1,0:T(8,128)}, f32[128,1152]{1,0:T(8,128)}, u32[]{:S(2)}, u32[]{:S(2)}) collective-permute-start(f32[128,1152]{1,0:T(8,128)} %broadcast_select_fusion), channel_id=1, source_target_pairs={{0,4},{16,20},{32,36},{48,52},{1,5},{17,21},{33,37},{49,53},{68,64... | collective-permute-start | bytes 1769480 | tf_op jit(solution)/shard_map/ppermute | solution.py:469
  121.8 1.3 collective-permute-start.15
  123.1 4.9 %collective-permute-done.18 = f32[128,1152]{1,0:T(8,128)} collective-permute-done((f32[128,1152]{1,0:T(8,128)}, f32[128,1152]{1,0:T(8,128)}, u32[]{:S(2)}, u32[]{:S(2)}) %collective-permute-start.18) | collective-permute-done | bytes 589856 | tf_op jit(solution)/shard_map/ppermute | solution.py:469
  129.9 1.6 column.2
  131.5 3.8 %collective-permute-done.15 = f32[128,1152]{1,0:T(8,128)S(1)} collective-permute-done((f32[128,1152]{1,0:T(8,128)}, f32[128,1152]{1,0:T(8,128)S(1)}, u32[]{:S(2)}, u32[]{:S(2)}) %collective-permute-start.15) | collective-permute-done | bytes 589856 | tf_op jit(solution)/shard_map/ppermute | solution.py:465
  135.3 1.6 column.3
  137.0 1.9 collective-permute-start.19
  138.9 2.2 %collective-permute-start.22 = (f32[64,768]{1,0:T(8,128)S(1)}, f32[64,768]{1,0:T(8,128)S(1)}, u32[]{:S(2)}, u32[]{:S(2)}) collective-permute-start(f32[64,768]{1,0:T(8,128)S(1)} %get-tuple-element.51), channel_id=1, source_target_pairs={{0,32},{1,33},{2,34},{3,35},{4,36},{5,37},{16,48},{17,49},{18,50},... | collective-permute-start | bytes 589832 | tf_op jit(solution)/shard_map/ppermute | solution.py:481
  141.1 3.4 %collective-permute-done.19 = f32[64,768]{1,0:T(8,128)S(1)} collective-permute-done((f32[64,768]{1,0:T(8,128)S(1)}, f32[64,768]{1,0:T(8,128)S(1)}, u32[]{:S(2)}, u32[]{:S(2)}) %collective-permute-start.19) | collective-permute-done | bytes 196640 | tf_op jit(solution)/shard_map/ppermute | solution.py:481
  144.6 1.9 collective-permute-start.20
  147.8 4.4 %collective-permute-start.23 = (f32[64,768]{1,0:T(8,128)S(1)}, f32[64,768]{1,0:T(8,128)S(1)}, u32[]{:S(2)}, u32[]{:S(2)}) collective-permute-start(f32[64,768]{1,0:T(8,128)S(1)} %add.85), channel_id=1, source_target_pairs={{0,96},{1,97},{2,98},{3,99},{4,100},{5,101},{16,112},{17,113},{18,... | collective-permute-start | bytes 589832 | tf_op jit(solution)/shard_map/ppermute | solution.py:481
  152.2 5.7 %collective-permute-start.21 = (f32[64,768]{1,0:T(8,128)S(1)}, f32[64,768]{1,0:T(8,128)S(1)}, u32[]{:S(2)}, u32[]{:S(2)}) collective-permute-start(f32[64,768]{1,0:T(8,128)S(1)} %add.83), channel_id=1, source_target_pairs={{0,96},{1,97},{2,98},{3,99},{4,100},{5,101},{16,112},{17,113},{18,... | collective-permute-start | bytes 589832 | tf_op jit(solution)/shard_map/ppermute | solution.py:481
  157.9 3.1 %collective-permute-start.24 = (f32[64,768]{1,0:T(8,128)S(1)}, f32[64,768]{1,0:T(8,128)S(1)}, u32[]{:S(2)}, u32[]{:S(2)}) collective-permute-start(f32[64,768]{1,0:T(8,128)S(1)} %add.86), channel_id=1, source_target_pairs={{0,16},{1,17},{2,18},{3,19},{4,20},{5,21},{16,0},{17,1},{18,2},{19... | collective-permute-start | bytes 589832 | tf_op jit(solution)/shard_map/ppermute | solution.py:481
  161.0 1.6 collective-permute-done.21
  162.6 3.6 %collective-permute-done.24 = f32[64,768]{1,0:T(8,128)S(1)} collective-permute-done((f32[64,768]{1,0:T(8,128)S(1)}, f32[64,768]{1,0:T(8,128)S(1)}, u32[]{:S(2)}, u32[]{:S(2)}) %collective-permute-start.24) | collective-permute-done | bytes 196640 | tf_op jit(solution)/shard_map/ppermute | solution.py:481
  166.3 1.9 collective-permute-start.26
  168.2 5.1 %collective-permute-start.25 = (f32[128,768]{1,0:T(8,128)S(1)}, f32[128,768]{1,0:T(8,128)S(1)}, u32[]{:S(2)}, u32[]{:S(2)}) collective-permute-start(f32[128,768]{1,0:T(8,128)S(1)} %pad_maximum_fusion.1.refs_0_), channel_id=1, source_target_pairs={{0,18},{16,2},{32,50},{48,34},{64,82},{80,66},{96,114},{112,98},{1... | collective-permute-start | bytes 1179656 | tf_op jit(solution)/shard_map/ppermute | solution.py:493
  173.3 1.9 collective-permute-start.27
  175.3 3.9 %collective-permute-done.26.refs_2_ = f32[128,768]{1,0:T(8,128)S(1)} collective-permute-done((f32[128,768]{1,0:T(8,128)S(1)}, f32[128,768]{1,0:T(8,128)S(1)}, u32[]{:S(2)}, u32[]{:S(2)}) %collective-permute-start.26) | collective-permute-done | bytes 393248 | tf_op jit(solution)/shard_map/ppermute | solution.py:493
  179.2 1.9 collective-permute-start.29
  181.1 5.3 %collective-permute-done.25.refs_1_ = f32[128,768]{1,0:T(8,128)S(1)} collective-permute-done((f32[128,768]{1,0:T(8,128)S(1)}, f32[128,768]{1,0:T(8,128)S(1)}, u32[]{:S(2)}, u32[]{:S(2)}) %collective-permute-start.25) | collective-permute-done | bytes 393248 | tf_op jit(solution)/shard_map/ppermute | solution.py:493
  186.4 1.9 collective-permute-start.28
  188.3 3.0 %patch.1.refs_9_ = f32[18,9,128,128]{3,2,1,0:T(8,128)} custom-call(s32[34,6]{1,0:T(8,128)} %copy.35.masks, f32[128,1152]{1,0:T(8,128)} %row.1.refs_0_, f32[128,1152]{1,0:T(8,128)} %copy-done.1, f32[128,1152]{1,0:T(8,128)} %copy-done.2, f32[18,9,128,128]{3,2,1,0:T(8,128)} %get-tuple-element.52.refs_3_), custom_call_target="tpu_custom_call", output_to_operand_aliasing={{}: (4, {})} | custom-call | flops 100000000 | bytes 4000000 | tf_op jit(solution)/shard_map/patch/pallas_call | solution.py:373
  193.0 5.8 %corner.1 = f32[18,9,128,128]{3,2,1,0:T(8,128)} custom-call(s32[34,6]{1,0:T(8,128)} %copy.35.masks, f32[128,768]{1,0:T(8,128)} %copy-done.6, f32[128,768]{1,0:T(8,128)} %copy-done.8, f32[128,768]{1,0:T(8,128)} %copy-done.7, f32[128,768]{1,0:T(8,128)} %copy-done.9, f32[128,768]{1,0:T(8,128)} %copy-done.11, ...), custom_call_target="tpu_custom_call", output_to_operand_aliasing={{}: (10, {})} | custom-call | flops 1000000000 | bytes 1000000 | tf_op jit(solution)/shard_map/corner/pallas_call | solution.py:303
  (78 shorter events, 22.4 us)
Async XLA Ops:
  0.9 4.6 %collective-permute-start = (bf16[1,6,64,128]{3,2,1,0:T(8,128)(2,1)S(1)}, bf16[1,6,64,128]{3,2,1,0:T(8,128)(2,1)S(1)}, u32[]{:S(2)}, u32[]{:S(2)}) collective-permute-start(bf16[1,6,64,128]{3,2,1,0:T(8,128)(2,1)S(1)} %dynamic-slice_bitcast_fusion), channel_id=1, source_target_pairs={{0,16},{16,0},{32,48},{48,32},{64,80},{80,64},{96,112},{112,96},{1... | collective-permute-start | bytes 294920 | tf_op jit(solution)/shard_map/ppermute | solution.py:422
  5.5 11.9 %collective-permute-start.3 = (bf16[2,6,64,128]{3,2,1,0:T(8,128)(2,1)S(1)}, bf16[2,6,64,128]{3,2,1,0:T(8,128)(2,1)S(1)}, u32[]{:S(2)}, u32[]{:S(2)}) collective-permute-start(bf16[2,6,64,128]{3,2,1,0:T(8,128)(2,1)S(1)} %maximum_select_fusion), channel_id=1, source_target_pairs={{0,96},{16,112},{32,0},{48,16},{64,32},{80,48},{96,64},{112,80},{1... | collective-permute-start | bytes 589832 | tf_op jit(solution)/shard_map/ppermute | solution.py:423
  9.8 9.3 %collective-permute-start.2 = (bf16[2,6,64,128]{3,2,1,0:T(8,128)(2,1)S(1)}, bf16[2,6,64,128]{3,2,1,0:T(8,128)(2,1)S(1)}, u32[]{:S(2)}, u32[]{:S(2)}) collective-permute-start(bf16[2,6,64,128]{3,2,1,0:T(8,128)(2,1)S(1)} %maximum_select_fusion), channel_id=1, source_target_pairs={{0,64},{16,80},{32,96},{48,112},{64,0},{80,16},{96,32},{112,48},{1... | collective-permute-start | bytes 589832 | tf_op jit(solution)/shard_map/ppermute | solution.py:423
  9.8 11.1 %collective-permute-start.1 = (bf16[2,6,64,128]{3,2,1,0:T(8,128)(2,1)S(1)}, bf16[2,6,64,128]{3,2,1,0:T(8,128)(2,1)S(1)}, u32[]{:S(2)}, u32[]{:S(2)}) collective-permute-start(bf16[2,6,64,128]{3,2,1,0:T(8,128)(2,1)S(1)} %maximum_select_fusion), channel_id=1, source_target_pairs={{0,32},{16,48},{32,64},{48,80},{64,96},{80,112},{96,0},{112,16},{1... | collective-permute-start | bytes 589832 | tf_op jit(solution)/shard_map/ppermute | solution.py:423
  21.8 18.0 %collective-permute-start.4 = (bf16[6,6,64,128]{3,2,1,0:T(8,128)(2,1)}, bf16[6,6,64,128]{3,2,1,0:T(8,128)(2,1)}, u32[]{:S(2)}, u32[]{:S(2)}) collective-permute-start(bf16[6,6,64,128]{3,2,1,0:T(8,128)(2,1)} %pad_maximum_fusion.refs_1_.refs_6_), channel_id=1, source_target_pairs={{0,1},{1,0},{2,3},{3,2},{4,5},{5,4},{6,7},{7,6},{8,9},{9,8},{10,11... | collective-permute-start | bytes 1769480 | tf_op jit(solution)/shard_map/ppermute | solution.py:429
  39.8 89.4 %copy-start = (bf16[18,1,6,128,128]{4,3,2,1,0:T(8,128)(2,1)S(1)}, bf16[18,1,6,128,128]{4,3,2,1,0:T(8,128)(2,1)}, u32[]{:S(2)}) copy-start(bf16[18,1,6,128,128]{4,3,2,1,0:T(8,128)(2,1)} %param.5) | copy-start | bytes 10616836
  39.8 2.2 %copy-start.3 = (f32[6,128,1152]{2,1,0:T(8,128)S(1)}, f32[6,128,1152]{2,1,0:T(8,128)}, u32[]{:S(2)}) copy-start(f32[6,128,1152]{2,1,0:T(8,128)} %get-tuple-element.29.refs_0_) | copy-start | bytes 10616836
  41.9 0.7 copy-start.4
  46.6 20.5 %collective-permute-start.8 = (f32[4,128,384]{2,1,0:T(8,128)S(1)}, f32[4,128,384]{2,1,0:T(8,128)S(1)}, u32[]{:S(2)}, u32[]{:S(2)}) collective-permute-start(f32[4,128,384]{2,1,0:T(8,128)S(1)} %get-tuple-element.37), channel_id=1, source_target_pairs={{0,32},{16,48},{32,0},{48,16},{64,96},{80,112},{96,64},{112,80},{1... | collective-permute-start | bytes 2359304 | tf_op jit(solution)/shard_map/ppermute | solution.py:448
  46.7 22.7 %collective-permute-start.11 = (f32[4,128,384]{2,1,0:T(8,128)S(1)}, f32[4,128,384]{2,1,0:T(8,128)S(1)}, u32[]{:S(2)}, u32[]{:S(2)}) collective-permute-start(f32[4,128,384]{2,1,0:T(8,128)S(1)} %get-tuple-element.43), channel_id=1, source_target_pairs={{0,96},{16,112},{32,64},{48,80},{64,32},{80,48},{96,0},{112,16},{1... | collective-permute-start | bytes 2359304 | tf_op jit(solution)/shard_map/ppermute | solution.py:448
  47.8 15.3 %collective-permute-start.5 = (f32[3,128,384]{2,1,0:T(8,128)S(1)}, f32[3,128,384]{2,1,0:T(8,128)S(1)}, u32[]{:S(2)}, u32[]{:S(2)}) collective-permute-start(f32[3,128,384]{2,1,0:T(8,128)S(1)} %get-tuple-element.31), channel_id=1, source_target_pairs={{0,16},{16,0},{32,48},{48,32},{64,80},{80,64},{96,112},{112,96},{1... | collective-permute-start | bytes 1769480 | tf_op jit(solution)/shard_map/ppermute | solution.py:448
  64.1 11.0 %collective-permute-start.6 = (f32[2,128,384]{2,1,0:T(8,128)S(1)}, f32[2,128,384]{2,1,0:T(8,128)S(1)}, u32[]{:S(2)}, u32[]{:S(2)}) collective-permute-start(f32[2,128,384]{2,1,0:T(8,128)S(1)} %get-tuple-element.33), channel_id=1, source_target_pairs={{0,32},{16,48},{32,0},{48,16},{64,96},{80,112},{96,64},{112,80},{1... | collective-permute-start | bytes 1179656 | tf_op jit(solution)/shard_map/ppermute | solution.py:448
  68.0 14.0 %collective-permute-start.9 = (f32[2,128,384]{2,1,0:T(8,128)S(1)}, f32[2,128,384]{2,1,0:T(8,128)S(1)}, u32[]{:S(2)}, u32[]{:S(2)}) collective-permute-start(f32[2,128,384]{2,1,0:T(8,128)S(1)} %get-tuple-element.39), channel_id=1, source_target_pairs={{32,64},{48,80},{64,32},{80,48},{96,0},{112,16},{33,65},{49,81},{6... | collective-permute-start | bytes 1179656 | tf_op jit(solution)/shard_map/ppermute | solution.py:448
  70.3 15.7 %collective-permute-start.12 = (f32[2,128,384]{2,1,0:T(8,128)S(1)}, f32[2,128,384]{2,1,0:T(8,128)S(1)}, u32[]{:S(2)}, u32[]{:S(2)}) collective-permute-start(f32[2,128,384]{2,1,0:T(8,128)S(1)} %get-tuple-element.45), channel_id=1, source_target_pairs={{0,16},{16,0},{32,48},{48,32},{64,80},{80,64},{96,112},{112,96},{1... | collective-permute-start | bytes 1179656 | tf_op jit(solution)/shard_map/ppermute | solution.py:448
  76.0 12.9 %collective-permute-start.7 = (f32[1,128,384]{2,1,0:T(8,128)S(1)}, f32[1,128,384]{2,1,0:T(8,128)S(1)}, u32[]{:S(2)}, u32[]{:S(2)}) collective-permute-start(f32[1,128,384]{2,1,0:T(8,128)S(1)} %get-tuple-element.35), channel_id=1, source_target_pairs={{32,64},{48,80},{64,32},{80,48},{96,0},{112,16},{33,65},{49,81},{6... | collective-permute-start | bytes 589832 | tf_op jit(solution)/shard_map/ppermute | solution.py:448
  83.0 7.6 %collective-permute-start.10 = (f32[1,128,384]{2,1,0:T(8,128)S(1)}, f32[1,128,384]{2,1,0:T(8,128)S(1)}, u32[]{:S(2)}, u32[]{:S(2)}) collective-permute-start(f32[1,128,384]{2,1,0:T(8,128)S(1)} %get-tuple-element.41), channel_id=1, source_target_pairs={{0,16},{16,0},{32,48},{48,32},{64,80},{80,64},{1,17},{17,1},{33,49... | collective-permute-start | bytes 589832 | tf_op jit(solution)/shard_map/ppermute | solution.py:448
  87.0 7.6 %collective-permute-start.13 = (f32[1,128,384]{2,1,0:T(8,128)S(1)}, f32[1,128,384]{2,1,0:T(8,128)S(1)}, u32[]{:S(2)}, u32[]{:S(2)}) collective-permute-start(f32[1,128,384]{2,1,0:T(8,128)S(1)} %get-tuple-element.47), channel_id=1, source_target_pairs={{0,32},{16,48},{32,0},{48,16},{96,64},{112,80},{1,33},{17,49},{33,... | collective-permute-start | bytes 589832 | tf_op jit(solution)/shard_map/ppermute | solution.py:448
  96.3 16.6 %collective-permute-start.16 = (f32[128,1152]{1,0:T(8,128)}, f32[128,1152]{1,0:T(8,128)}, u32[]{:S(2)}, u32[]{:S(2)}) collective-permute-start(f32[128,1152]{1,0:T(8,128)} %row.1.refs_0_), channel_id=1, source_target_pairs={{64,0},{65,16},{66,32},{67,48},{68,68},{69,84},{70,100},{71,116},{... | collective-permute-start | bytes 1769480 | tf_op jit(solution)/shard_map/ppermute | solution.py:464
  97.6 15.3 %collective-permute-start.14 = (f32[128,1152]{1,0:T(8,128)}, f32[128,1152]{1,0:T(8,128)}, u32[]{:S(2)}, u32[]{:S(2)}) collective-permute-start(f32[128,1152]{1,0:T(8,128)} %row.1.refs_0_), channel_id=1, source_target_pairs={{0,0},{1,16},{2,32},{3,48},{4,68},{5,84},{6,100},{7,116},{8,8},{9,... | collective-permute-start | bytes 1769480 | tf_op jit(solution)/shard_map/ppermute | solution.py:463
  114.9 13.1 %collective-permute-start.18 = (f32[128,1152]{1,0:T(8,128)}, f32[128,1152]{1,0:T(8,128)}, u32[]{:S(2)}, u32[]{:S(2)}) collective-permute-start(f32[128,1152]{1,0:T(8,128)} %broadcast_select_fusion), channel_id=1, source_target_pairs={{0,4},{16,20},{32,36},{48,52},{1,5},{17,21},{33,37},{49,53},{68,64... | collective-permute-start | bytes 1769480 | tf_op jit(solution)/shard_map/ppermute | solution.py:469
  121.1 10.4 %collective-permute-start.17 = (f32[128,1152]{1,0:T(8,128)}, f32[128,1152]{1,0:T(8,128)S(1)}, u32[]{:S(2)}, u32[]{:S(2)}) collective-permute-start(f32[128,1152]{1,0:T(8,128)} %collective-permute-done.16), channel_id=1, source_target_pairs={{8,4},{24,20},{40,36},{56,52},{76,68},{92,84},{108,100},{124,116},... | collective-permute-start | bytes 1769480 | tf_op jit(solution)/shard_map/ppermute | solution.py:466
  121.8 13.5 %collective-permute-start.15 = (f32[128,1152]{1,0:T(8,128)}, f32[128,1152]{1,0:T(8,128)S(1)}, u32[]{:S(2)}, u32[]{:S(2)}) collective-permute-start(f32[128,1152]{1,0:T(8,128)} %collective-permute-done.14), channel_id=1, source_target_pairs={{8,0},{24,16},{40,32},{56,48},{76,64},{92,80},{108,96},{124,112},{... | collective-permute-start | bytes 1769480 | tf_op jit(solution)/shard_map/ppermute | solution.py:465
  129.1 7.8 %copy-start.1 = (f32[128,1152]{1,0:T(8,128)}, f32[128,1152]{1,0:T(8,128)S(1)}, u32[]{:S(2)}) copy-start(f32[128,1152]{1,0:T(8,128)S(1)} %select_select_fusion.value_ref.refs_1_) | copy-start | bytes 1769476
  129.1 0.8 copy-start.5
  135.3 1.6 copy-start.2
  137.0 7.6 %collective-permute-start.19 = (f32[64,768]{1,0:T(8,128)S(1)}, f32[64,768]{1,0:T(8,128)S(1)}, u32[]{:S(2)}, u32[]{:S(2)}) collective-permute-start(f32[64,768]{1,0:T(8,128)S(1)} %get-tuple-element.50), channel_id=1, source_target_pairs={{0,16},{1,17},{2,18},{3,19},{4,20},{5,21},{16,0},{17,1},{18,2},{19... | collective-permute-start | bytes 589832 | tf_op jit(solution)/shard_map/ppermute | solution.py:481
  138.9 8.8 %collective-permute-start.22 = (f32[64,768]{1,0:T(8,128)S(1)}, f32[64,768]{1,0:T(8,128)S(1)}, u32[]{:S(2)}, u32[]{:S(2)}) collective-permute-start(f32[64,768]{1,0:T(8,128)S(1)} %get-tuple-element.51), channel_id=1, source_target_pairs={{0,32},{1,33},{2,34},{3,35},{4,36},{5,37},{16,48},{17,49},{18,50},... | collective-permute-start | bytes 589832 | tf_op jit(solution)/shard_map/ppermute | solution.py:481
  144.6 7.6 %collective-permute-start.20 = (f32[64,768]{1,0:T(8,128)S(1)}, f32[64,768]{1,0:T(8,128)S(1)}, u32[]{:S(2)}, u32[]{:S(2)}) collective-permute-start(f32[64,768]{1,0:T(8,128)S(1)} %add.82), channel_id=1, source_target_pairs={{0,32},{1,33},{2,34},{3,35},{4,36},{5,37},{16,48},{17,49},{18,50},... | collective-permute-start | bytes 589832 | tf_op jit(solution)/shard_map/ppermute | solution.py:481
  147.8 10.1 %collective-permute-start.23 = (f32[64,768]{1,0:T(8,128)S(1)}, f32[64,768]{1,0:T(8,128)S(1)}, u32[]{:S(2)}, u32[]{:S(2)}) collective-permute-start(f32[64,768]{1,0:T(8,128)S(1)} %add.85), channel_id=1, source_target_pairs={{0,96},{1,97},{2,98},{3,99},{4,100},{5,101},{16,112},{17,113},{18,... | collective-permute-start | bytes 589832 | tf_op jit(solution)/shard_map/ppermute | solution.py:481
  152.2 10.4 %collective-permute-start.21 = (f32[64,768]{1,0:T(8,128)S(1)}, f32[64,768]{1,0:T(8,128)S(1)}, u32[]{:S(2)}, u32[]{:S(2)}) collective-permute-start(f32[64,768]{1,0:T(8,128)S(1)} %add.83), channel_id=1, source_target_pairs={{0,96},{1,97},{2,98},{3,99},{4,100},{5,101},{16,112},{17,113},{18,... | collective-permute-start | bytes 589832 | tf_op jit(solution)/shard_map/ppermute | solution.py:481
  157.9 8.3 %collective-permute-start.24 = (f32[64,768]{1,0:T(8,128)S(1)}, f32[64,768]{1,0:T(8,128)S(1)}, u32[]{:S(2)}, u32[]{:S(2)}) collective-permute-start(f32[64,768]{1,0:T(8,128)S(1)} %add.86), channel_id=1, source_target_pairs={{0,16},{1,17},{2,18},{3,19},{4,20},{5,21},{16,0},{17,1},{18,2},{19... | collective-permute-start | bytes 589832 | tf_op jit(solution)/shard_map/ppermute | solution.py:481
  166.3 25.1 %copy-start.6 = (f32[128,768]{1,0:T(8,128)}, f32[128,768]{1,0:T(8,128)S(1)}, u32[]{:S(2)}) copy-start(f32[128,768]{1,0:T(8,128)S(1)} %pad_maximum_fusion.1.refs_0_) | copy-start | bytes 1179652
  166.3 12.9 %collective-permute-start.26 = (f32[128,768]{1,0:T(8,128)S(1)}, f32[128,768]{1,0:T(8,128)S(1)}, u32[]{:S(2)}, u32[]{:S(2)}) collective-permute-start(f32[128,768]{1,0:T(8,128)S(1)} %pad_maximum_fusion.1.refs_0_), channel_id=1, source_target_pairs={{0,4},{16,20},{32,36},{48,52},{64,68},{80,84},{96,100},{112,116},{... | collective-permute-start | bytes 1179656 | tf_op jit(solution)/shard_map/ppermute | solution.py:493
  168.2 18.2 %collective-permute-start.25 = (f32[128,768]{1,0:T(8,128)S(1)}, f32[128,768]{1,0:T(8,128)S(1)}, u32[]{:S(2)}, u32[]{:S(2)}) collective-permute-start(f32[128,768]{1,0:T(8,128)S(1)} %pad_maximum_fusion.1.refs_0_), channel_id=1, source_target_pairs={{0,18},{16,2},{32,50},{48,34},{64,82},{80,66},{96,114},{112,98},{1... | collective-permute-start | bytes 1179656 | tf_op jit(solution)/shard_map/ppermute | solution.py:493
  173.3 18.0 %collective-permute-start.27 = (f32[128,768]{1,0:T(8,128)S(1)}, f32[128,768]{1,0:T(8,128)S(1)}, u32[]{:S(2)}, u32[]{:S(2)}) collective-permute-start(f32[128,768]{1,0:T(8,128)S(1)} %pad_maximum_fusion.1.refs_0_), channel_id=1, source_target_pairs={{0,1},{1,0},{2,3},{3,2},{4,5},{5,4},{16,17},{17,16},{18,19},{19,18... | collective-permute-start | bytes 1179656 | tf_op jit(solution)/shard_map/ppermute | solution.py:495
  179.2 12.2 %copy-start.7 = (f32[128,768]{1,0:T(8,128)}, f32[128,768]{1,0:T(8,128)S(1)}, u32[]{:S(2)}) copy-start(f32[128,768]{1,0:T(8,128)S(1)} %collective-permute-done.26.refs_2_) | copy-start | bytes 1179652
  179.2 12.2 %collective-permute-start.29 = (f32[128,768]{1,0:T(8,128)S(1)}, f32[128,768]{1,0:T(8,128)S(1)}, u32[]{:S(2)}, u32[]{:S(2)}) collective-permute-start(f32[128,768]{1,0:T(8,128)S(1)} %collective-permute-done.26.refs_2_), channel_id=1, source_target_pairs={{0,1},{1,0},{2,3},{3,2},{4,5},{5,4},{16,17},{17,16},{18,19},{19,18... | collective-permute-start | bytes 1179656 | tf_op jit(solution)/shard_map/ppermute | solution.py:495
  186.4 5.0 %copy-start.8 = (f32[128,768]{1,0:T(8,128)}, f32[128,768]{1,0:T(8,128)S(1)}, u32[]{:S(2)}) copy-start(f32[128,768]{1,0:T(8,128)S(1)} %collective-permute-done.25.refs_1_) | copy-start | bytes 1179652
  186.4 5.0 %collective-permute-start.28 = (f32[128,768]{1,0:T(8,128)S(1)}, f32[128,768]{1,0:T(8,128)S(1)}, u32[]{:S(2)}, u32[]{:S(2)}) collective-permute-start(f32[128,768]{1,0:T(8,128)S(1)} %collective-permute-done.25.refs_1_), channel_id=1, source_target_pairs={{0,1},{1,0},{2,3},{3,2},{4,5},{5,4},{16,17},{17,16},{18,19},{19,18... | collective-permute-start | bytes 1179656 | tf_op jit(solution)/shard_map/ppermute | solution.py:495
  191.4 0.8 copy-start.9
  191.4 0.9 copy-start.10
  192.3 0.7 copy-start.11
